TPU v7x, 256 devices: a whole 4x4x8 slice. The times are simulated.
256 devices in a mesh: dp: 8 (over x, z_hi), ts: 32 (over z_lo, y, core).
Axes of the slice: x: 4, y: 4, z: 8 (z_hi: 2, z_lo: 4; z = z_hi * 4 + z_lo), core: 2. Of those that a mesh axis runs over, the one named last changes fastest.
Arguments:
- clip_video: bfloat16 [512, 4, 40, 128], P(('dp', 'ts')), may hold values from -6 to 6
- conv_weight: bfloat16 [3, 3, 3, 128, 128], replicated, may hold values from -0.109375 to 0.109375
- embed_weight: bfloat16 [128, 5120], replicated, may hold values from -0.5 to 0.5
- gain_spatial: float32 [5120], replicated, may hold values from 0.5 to 1.5
- gain_temporal: float32 [5120], replicated, may hold values from 0.5 to 1.5
- input_spatial: bfloat16 [5120, 384], P(('dp', 'ts')), may hold values from -0.078125 to 0.078125
- input_temporal: bfloat16 [5120, 384], P(('dp', 'ts')), may hold values from -0.078125 to 0.078125
- output_spatial: bfloat16 [128, 5120], replicated, may hold values from -2 to 2
- output_temporal: bfloat16 [128, 5120], replicated, may hold values from -2 to 2
- cotangent: bfloat16 [512, 4, 40, 5120], P(('dp', 'ts')), may hold values from -6 to 6
Outputs:
- layer_output: bfloat16 [512, 4, 40, 5120], P(('dp', 'ts'))
- grad_spatial: float32 [5120, 384], P(('dp', 'ts'))
All inputs are finite; a program needn't handle non-finite values.
Results may differ from a plain program's by a relative error of at most 0.015.
Values may be sent and summed in bfloat16 or wider, within the bound.
No kernel may reach another device: no remote copies, remote signals or barrier semaphores. Data moves between devices by JAX's collectives and lax.ppermute only.
A program may use at most 128 MiB of HBM per device.

v0:
```python
import jax
import jax.numpy as jnp
from jax import lax
from jax.sharding import PartitionSpec as P

FR = 16


epsilon = 1e-06
masked = -1e30


def passed_along(block, axis, distance):
    devices = range(lax.axis_size(axis))
    route = [(i - distance, i) for i in devices if i - distance in devices]
    return lax.ppermute(block, axis, route)


def side_by_side(arrays, axis, dim, along):
    widths = [a.shape[along] for a in arrays]
    both = jnp.concatenate(arrays, axis=along)
    whole = lax.all_gather(both, axis, axis=dim, tiled=True)
    return tuple(jnp.split(whole, [sum(widths[:k]) for k in range(1, len(widths))], axis=along))


def in_blocks(value, dim, size):
    dims = value.shape
    parts = value.reshape(*dims[:dim], size, dims[dim] // size, *dims[dim + 1 :])
    return jnp.moveaxis(parts, dim, 0)


def sum_at_owner(value, axis, dim):
    parts = in_blocks(value, dim, lax.axis_size(axis))
    arrived = lax.all_to_all(parts, axis, split_axis=0, concat_axis=0, tiled=True)
    return arrived.astype(jnp.float32).sum(axis=0)


def conv_local(volume, weight, count):
    frames, height, columns, channels = volume.shape
    out_channels = weight.shape[-1]
    padded = jnp.pad(volume, ((0, 0), (1, 1), (1, 1), (0, 0)))
    summed = jnp.zeros((count * height * columns, out_channels), jnp.float32)
    for time_tap in range(3):
        for row_tap in range(3):
            for col_tap in range(3):
                window = padded[
                    2 - time_tap : 2 - time_tap + count,
                    row_tap : row_tap + height,
                    col_tap : col_tap + columns,
                    :,
                ]
                summed = summed + jnp.dot(
                    window.reshape(-1, channels),
                    weight[time_tap, row_tap, col_tap],
                    preferred_element_type=jnp.float32,
                )
    return summed.reshape(count, height, columns, out_channels)


def rms_norm(hidden, norm_gain):
    widened = hidden.astype(jnp.float32)
    factor = lax.rsqrt(jnp.mean(widened * widened, axis=-1, keepdims=True) + epsilon)
    return ((widened * factor * norm_gain).astype(jnp.bfloat16), factor)


def rms_norm_grad(hidden, norm_gain, factor, upstream):
    widened = hidden.astype(jnp.float32)
    scaled = upstream * norm_gain
    inner_mean = jnp.mean(widened * scaled, axis=-1, keepdims=True)
    return factor * scaled - widened * factor**3 * inner_mean


def frame_forward(packed):
    frames, places, triple = packed.shape
    head_size = triple // 3
    queries = packed[..., :head_size]
    key_rows = packed[..., head_size : 2 * head_size]
    values = packed[..., 2 * head_size :]
    scores = jnp.einsum(
        "fqd,fkd->fqk", queries, key_rows, preferred_element_type=jnp.float32
    ) * head_size ** (-0.5)
    attend = jax.nn.softmax(scores, axis=-1)
    rounded = attend.astype(jnp.bfloat16)
    mixture = jnp.einsum("fqk,fkd->fqd", rounded, values, preferred_element_type=jnp.float32)
    return (mixture.astype(jnp.bfloat16), attend)


def frame_backward(packed, attend, upstream):
    frames, places, triple = packed.shape
    head_size = triple // 3
    scale_factor = head_size ** (-0.5)
    queries = packed[..., :head_size]
    key_rows = packed[..., head_size : 2 * head_size]
    values = packed[..., 2 * head_size :]
    rounded = attend.astype(jnp.bfloat16)
    grad_attend = jnp.einsum("fqd,fkd->fqk", upstream, values, preferred_element_type=jnp.float32)
    grad_values = jnp.einsum("fqk,fqd->fkd", rounded, upstream, preferred_element_type=jnp.float32)
    grad_scores = attend * (grad_attend - jnp.sum(grad_attend * attend, axis=-1, keepdims=True))
    grad_rounded = grad_scores.astype(jnp.bfloat16)
    grad_queries = (
        jnp.einsum("fqk,fkd->fqd", grad_rounded, key_rows, preferred_element_type=jnp.float32)
        * scale_factor
    )
    grad_keys = (
        jnp.einsum("fqk,fqd->fkd", grad_rounded, queries, preferred_element_type=jnp.float32)
        * scale_factor
    )
    joined = jnp.concatenate([grad_queries, grad_keys, grad_values], axis=-1)
    return joined.astype(jnp.bfloat16)


def clip_forward(packed):
    frames, places, triple = packed.shape
    head_size = triple // 3
    volume = packed.reshape(frames // FR, FR, places, triple)
    queries = volume[..., :head_size]
    key_rows = volume[..., head_size : 2 * head_size]
    values = volume[..., 2 * head_size :]
    scores = jnp.einsum(
        "cqpd,ckpd->cpqk", queries, key_rows, preferred_element_type=jnp.float32
    ) * head_size ** (-0.5)
    allowed = jnp.arange(FR)[:, None] >= jnp.arange(FR)[None, :]
    scores = jnp.where(allowed, scores, masked)
    attend = jax.nn.softmax(scores, axis=-1)
    rounded = attend.astype(jnp.bfloat16)
    mixture = jnp.einsum("cpqk,ckpd->cqpd", rounded, values, preferred_element_type=jnp.float32)
    return (mixture.astype(jnp.bfloat16).reshape(frames, places, head_size), attend)


def clip_backward(packed, attend, upstream):
    frames, places, triple = packed.shape
    head_size = triple // 3
    scale_factor = head_size ** (-0.5)
    volume = packed.reshape(frames // FR, FR, places, triple)
    queries = volume[..., :head_size]
    key_rows = volume[..., head_size : 2 * head_size]
    values = volume[..., 2 * head_size :]
    grad_out = upstream.reshape(frames // FR, FR, places, head_size)
    rounded = attend.astype(jnp.bfloat16)
    grad_attend = jnp.einsum(
        "cqpd,ckpd->cpqk", grad_out, values, preferred_element_type=jnp.float32
    )
    grad_values = jnp.einsum(
        "cpqk,cqpd->ckpd", rounded, grad_out, preferred_element_type=jnp.float32
    )
    grad_scores = attend * (grad_attend - jnp.sum(grad_attend * attend, axis=-1, keepdims=True))
    grad_rounded = grad_scores.astype(jnp.bfloat16)
    grad_queries = (
        jnp.einsum("cpqk,ckpd->cqpd", grad_rounded, key_rows, preferred_element_type=jnp.float32)
        * scale_factor
    )
    grad_keys = (
        jnp.einsum("cpqk,cqpd->ckpd", grad_rounded, queries, preferred_element_type=jnp.float32)
        * scale_factor
    )
    joined = jnp.concatenate([grad_queries, grad_keys, grad_values], axis=-1)
    return joined.astype(jnp.bfloat16).reshape(frames, places, triple)


def shards(
    clip_video,
    conv_weight,
    embed_weight,
    gain_spatial,
    gain_temporal,
    input_spatial,
    input_temporal,
    output_spatial,
    output_temporal,
    cotangent,
):
    frames_here = clip_video.shape[0]
    prior = passed_along(clip_video, "ts", 1)
    opening = lax.axis_index("ts") == 0
    prior = jnp.where(opening, jnp.zeros_like(prior), prior)
    volume = jnp.concatenate([prior, clip_video], axis=0)
    whole_spatial, whole_temporal = side_by_side(
        (input_spatial, input_temporal), ("dp", "ts"), 0, 1
    )
    features = jax.nn.gelu(conv_local(volume, conv_weight, frames_here), approximate=True).astype(
        jnp.bfloat16
    )
    frames, height, columns, channels = features.shape
    places = height * columns
    tokens = frames * places
    embedded = jnp.dot(
        features.reshape(tokens, channels), embed_weight, preferred_element_type=jnp.float32
    ).astype(jnp.bfloat16)
    normed_one, factor_one = rms_norm(embedded, gain_spatial)
    packed_one = jnp.dot(normed_one, whole_spatial, preferred_element_type=jnp.float32).astype(
        jnp.bfloat16
    )
    packed_one = packed_one.reshape(frames, places, -1)
    mixture_one, attend_one = frame_forward(packed_one)
    after_space = (
        embedded.astype(jnp.float32)
        + jnp.dot(
            mixture_one.reshape(tokens, -1), output_spatial, preferred_element_type=jnp.float32
        )
    ).astype(jnp.bfloat16)
    normed_two, factor_two = rms_norm(after_space, gain_temporal)
    packed_two = jnp.dot(normed_two, whole_temporal, preferred_element_type=jnp.float32).astype(
        jnp.bfloat16
    )
    packed_two = packed_two.reshape(frames, places, -1)
    cotangent_rows = cotangent.reshape(tokens, -1)
    grad_mix_two = jnp.dot(
        cotangent_rows, output_temporal.T, preferred_element_type=jnp.float32
    ).astype(jnp.bfloat16)
    grad_mix_two = grad_mix_two.reshape(frames, places, -1)
    patched = lax.all_to_all(packed_two, "ts", split_axis=1, concat_axis=0, tiled=True)
    mixture_patched, attend_two = clip_forward(patched)
    mixture_two = lax.all_to_all(mixture_patched, "ts", split_axis=0, concat_axis=1, tiled=True)
    grad_patched = lax.all_to_all(grad_mix_two, "ts", split_axis=1, concat_axis=0, tiled=True)
    grad_packed_patched = clip_backward(patched, attend_two, grad_patched)
    grad_packed_two = lax.all_to_all(
        grad_packed_patched, "ts", split_axis=0, concat_axis=1, tiled=True
    )
    after_time = (
        after_space.astype(jnp.float32)
        + jnp.dot(
            mixture_two.reshape(tokens, -1), output_temporal, preferred_element_type=jnp.float32
        )
    ).astype(jnp.bfloat16)
    grad_packed_two = grad_packed_two.reshape(tokens, -1)
    grad_normed_two = jnp.dot(grad_packed_two, whole_temporal.T, preferred_element_type=jnp.float32)
    grad_after = (
        cotangent_rows.astype(jnp.float32)
        + rms_norm_grad(after_space, gain_temporal, factor_two, grad_normed_two)
    ).astype(jnp.bfloat16)
    grad_mix_one = jnp.dot(grad_after, output_spatial.T, preferred_element_type=jnp.float32).astype(
        jnp.bfloat16
    )
    grad_packed_one = frame_backward(
        packed_one, attend_one, grad_mix_one.reshape(frames, places, -1)
    ).reshape(tokens, -1)
    part_spatial = lax.dot_general(
        normed_one, grad_packed_one, (((0,), (0,)), ((), ())), preferred_element_type=jnp.float32
    )
    group_spatial = lax.psum_scatter(
        part_spatial.astype(jnp.bfloat16), "dp", scatter_dimension=0, tiled=True
    )
    grad_spatial = sum_at_owner(group_spatial, "ts", 0)
    return (after_time.reshape(frames, height, columns, -1), grad_spatial)


def solution(mesh):
    placed = (
        P(("dp", "ts"), None, None, None),
        P(),
        P(),
        P(),
        P(),
        P(("dp", "ts"), None),
        P(("dp", "ts"), None),
        P(),
        P(),
        P(("dp", "ts"), None, None, None),
    )
    return jax.shard_map(
        shards,
        mesh=mesh,
        in_specs=placed,
        out_specs=(P(("dp", "ts"), None, None, None), P(("dp", "ts"), None)),
        check_vma=False,
    )
```

profile of v0, /device:TPU:1, one launch (start us, length us, event | category | flops | bytes accessed | tf_op | source)
XLA Modules:
  0.0 364.3 jit_solution(13691863951065526166)
XLA Ops:
  7.2 1.5 maximum_bitcast_fusion
  8.7 4.6 %collective-permute-start = (bf16[2,4,40,128]{3,2,1,0:T(8,128)(2,1)}, bf16[2,4,40,128]{3,2,1,0:T(8,128)(2,1)S(1)}, u32[]{:S(2)}, u32[]{:S(2)}) collective-permute-start(bf16[2,4,40,128]{3,2,1,0:T(8,128)(2,1)} %param.10), channel_id=1, source_target_pairs={{0,1},{1,2},{2,3},{3,4},{4,5},{5,6},{6,7},{7,8},{8,9},{9,10},{10,1... | collective-permute-start | bytes 245768 | tf_op jit(solution)/shard_map/ppermute | solution.py:16
  13.3 3.4 convolution_convert_fusion.2
  16.7 0.7 copy.45
  17.4 8.5 %all-to-all-start.2 = ((bf16[2,160,128]{2,0,1:T(2,128)(2,1)}), bf16[2,160,128]{2,0,1:T(2,128)(2,1)S(1)}, u32[]{:S(2)}, u32[]{:S(2)}) async-start(bf16[2,160,128]{2,0,1:T(2,128)(2,1)} %copy.45), calls=%async_computation.2 | async-start | bytes 163840 | tf_op jit(solution)/shard_map/all_to_all | solution.py:214
  30.5 4.2 %fusion.4 = (f32[320]{0:T(512)S(1)}, bf16[320,5120]{1,0:T(8,128)(2,1)}) fusion(bf16[128,5120]{1,0:T(8,128)(2,1)} %param.12, f32[320,128]{1,0:T(8,128)S(1)} %convolution_add_fusion.1, bf16[320,128]{1,0:T(8,128)(2,1)S(1)} %bitcast.244, bf16[3,3,3,128,128]{4,3,2,1,0:T(8,128)(2,1)S(1)} %copy-done.5), kind=kOutput, calls=%fused_computation.15 | convolution fusion | flops 436879040 | bytes 4867328 | tf_op jit(solution)/shard_map/dot_general | solution.py:186
  34.7 100.0 %all-gather.3.cloned.1.call-done = bf16[256,20,768]{2,1,0:T(8,128)(2,1)} async-done(((bf16[1,20,768]{2,1,0:T(8,128)(2,1)}), bf16[256,20,768]{2,1,0:T(8,128)(2,1)}) %all-gather.3.cloned.1.call-update) | async-done | bytes 7864336 | tf_op jit(solution)/shard_map/all_gather | solution.py:22
  134.7 12.5 %reshape.220 = bf16[5120,768]{1,0:T(8,128)(2,1)} reshape(bf16[256,20,768]{2,1,0:T(8,128)(2,1)} %all-gather.3.cloned.1.call-done) | data formatting | bytes 15728640
  147.2 5.0 %fusion.26 = bf16[320,384]{1,0:T(8,128)(2,1)S(1)} fusion(bf16[5120,768]{1,0:T(8,128)(2,1)} %reshape.220, bf16[320,5120]{1,0:T(8,128)(2,1)} %get-tuple-element.32, f32[5120]{0:T(1024)S(1)} %copy-done.8, f32[320]{0:T(512)S(1)} %add_rsqrt_fusion.1), kind=kOutput, calls=%fused_computation.35 | convolution fusion | flops 1264967680 | bytes 7476480 | tf_op jit(solution)/shard_map/dot_general | solution.py:190
  152.2 0.3 fusion.182
  152.5 0.5 convolution_convert_fusion.6
  153.0 3.3 fusion.7
  156.3 5.2 %fusion.29 = bf16[320,384]{1,0:T(8,128)(2,1)S(1)} fusion(bf16[5120,768]{1,0:T(8,128)(2,1)} %reshape.220, bf16[320,5120]{1,0:T(8,128)(2,1)S(1)} %get-tuple-element.36, f32[5120]{0:T(1024)S(1)} %copy-done.7, f32[320]{0:T(512)S(1)} %get-tuple-element.30), kind=kOutput, calls=%fused_computation.36 | convolution fusion | flops 1264967680 | bytes 7476480 | tf_op jit(solution)/shard_map/dot_general | solution.py:202
  161.5 0.9 copy.36
  162.4 7.1 %all-to-all-start = ((bf16[2,160,384]{2,0,1:T(2,128)(2,1)}), bf16[2,160,384]{2,0,1:T(2,128)(2,1)S(1)}, u32[]{:S(2)}, u32[]{:S(2)}) async-start(bf16[2,160,384]{2,0,1:T(2,128)(2,1)} %copy.36), calls=%async_computation | async-start | bytes 491520 | tf_op jit(solution)/shard_map/all_to_all | solution.py:211
  169.7 10.6 %all-to-all-done = bf16[2,160,384]{2,0,1:T(2,128)(2,1)S(1)} async-done(((bf16[2,160,384]{2,0,1:T(2,128)(2,1)}), bf16[2,160,384]{2,0,1:T(2,128)(2,1)S(1)}, u32[]{:S(2)}, u32[]{:S(2)}) %all-to-all-start) | async-done | bytes 245792 | tf_op jit(solution)/shard_map/all_to_all | solution.py:211
  180.8 0.8 fusion.187
  182.6 17.4 %all_to_all.65 = bf16[64,5,384]{2,1,0:T(8,128)(2,1)S(1)} all-to-all(bf16[64,5,384]{2,1,0:T(8,128)(2,1)S(1)} %copy.53), channel_id=1, replica_groups=mesh['dp'=8,'ts'=32] {'ts'}, dimensions={0} | all-to-all | bytes 491520 | tf_op jit(solution)/shard_map/all_to_all | solution.py:216
  200.2 5.3 %fusion.14 = (f32[320]{0:T(512)S(1)}, f32[320,5120]{1,0:T(8,128)S(1)}) fusion(bf16[320,5120]{1,0:T(8,128)(2,1)} %copy-done.1, f32[5120]{0:T(1024)S(1)} %copy-done.7, bf16[320,384]{1,0:T(8,128)(2,1)S(1)} %reshape.216, bf16[5120,768]{1,0:T(8,128)(2,1)} %reshape.220), kind=kOutput, calls=%fused_computation.25 | convolution fusion | flops 1264844544 | bytes 14030080 | tf_op jit(solution)/shard_map/dot_general | solution.py:226
  205.5 2.0 fusion.41
  207.5 0.4 convolution_convert_fusion.4
  208.4 0.3 fusion.39
  208.6 6.6 %convolution_convert_fusion = bf16[5120,384]{1,0:T(8,128)(2,1)} fusion(bf16[320,5120]{1,0:T(8,128)(2,1)} %get-tuple-element.32, f32[5120]{0:T(1024)S(1)} %copy-done.8, f32[320]{0:T(512)S(1)} %add_rsqrt_fusion.1, bf16[320,128]{1,0:T(8,128)(2,1)S(1)} %bitcast.251, bf16[320,128]{1,0:T(8,128)(2,1)S(1)} %bitcast.252, bf16[320,128]{1,0:T(8,128)(2,1)S(1)} %bitcast.241), kind=kOutput, calls=%fused_computation.11 | convolution fusion | flops 1267548160 | bytes 7476480 | tf_op jit(solution)/shard_map/dot_general | solution.py:237
  215.3 0.2 fusion.46
  215.5 0.7 copy.43
  216.2 3.9 %all-to-all-start.1 = ((bf16[64,5,128]{2,1,0:T(8,128)(2,1)}), bf16[64,5,128]{2,1,0:T(8,128)(2,1)S(1)}, u32[]{:S(2)}, u32[]{:S(2)}) async-start(bf16[64,5,128]{2,1,0:T(8,128)(2,1)} %copy.43), calls=%async_computation.1 | async-start | bytes 262144 | tf_op jit(solution)/shard_map/all_to_all | solution.py:213
  220.2 109.8 %reduce-scatter.2.cloned.1.call-done = bf16[640,384]{1,0:T(8,128)(2,1)} async-done(((bf16[5120,384]{1,0:T(8,128)(2,1)}), bf16[640,384]{1,0:T(8,128)(2,1)}) %reduce-scatter.2.cloned.1.call-update) | async-done | bytes 491536 | tf_op jit(solution)/shard_map/reduce_scatter | solution.py:240
  330.0 1.9 reshape.218
  331.9 7.1 %all-to-all-start.4 = ((bf16[32,20,384]{2,1,0:T(8,128)(2,1)}), bf16[32,20,384]{2,1,0:T(8,128)(2,1)S(1)}, u32[]{:S(2)}, u32[]{:S(2)}) async-start(bf16[32,20,384]{2,1,0:T(8,128)(2,1)} %reshape.218), calls=%async_computation.5 | async-start | bytes 1179648 | tf_op jit(solution)/shard_map/all_to_all | solution.py:34
  339.1 4.6 %fusion.3 = bf16[320,5120]{1,0:T(8,128)(2,1)} fusion(bf16[320,128]{1,0:T(8,128)(2,1)S(1)} %reshape.211, bf16[128,5120]{1,0:T(8,128)(2,1)S(1)} %copy-done.4, bf16[320,5120]{1,0:T(8,128)(2,1)} %copy-done.1), kind=kOutput, calls=%fused_computation.13 | convolution fusion | flops 424345600 | bytes 7946240 | tf_op jit(solution)/shard_map/dot_general | solution.py:221
  343.7 13.0 %all-to-all-done.4 = bf16[32,20,384]{2,1,0:T(8,128)(2,1)S(1)} async-done(((bf16[32,20,384]{2,1,0:T(8,128)(2,1)}), bf16[32,20,384]{2,1,0:T(8,128)(2,1)S(1)}, u32[]{:S(2)}, u32[]{:S(2)}) %all-to-all-start.4) | async-done | bytes 491552 | tf_op jit(solution)/shard_map/all_to_all | solution.py:34
  356.7 0.7 convert_reduce_fusion
  (83 shorter events, 6.9 us)
Async XLA Ops:
  7.2 145.8 %copy-start = (bf16[128,5120]{1,0:T(8,128)(2,1)S(1)}, bf16[128,5120]{1,0:T(8,128)(2,1)}, u32[]{:S(2)}) copy-start(bf16[128,5120]{1,0:T(8,128)(2,1)} %param.17) | copy-start | bytes 3932164
  7.2 18.8 %copy-start.6 = (bf16[2,4,40,128]{3,2,1,0:T(8,128)(2,1)S(1)}, bf16[2,4,40,128]{3,2,1,0:T(8,128)(2,1)}, u32[]{:S(2)}) copy-start(bf16[2,4,40,128]{3,2,1,0:T(8,128)(2,1)} %param.10) | copy-start | bytes 245764
  7.2 127.5 %all-gather.3.cloned.1.call-start = ((), (), s32[]{:S(2)}) async-start(), calls=%async_computation.7 | async-start | bytes 9474048 | tf_op jit(solution)/shard_map/all_gather | solution.py:22
  8.7 17.2 %collective-permute-start = (bf16[2,4,40,128]{3,2,1,0:T(8,128)(2,1)}, bf16[2,4,40,128]{3,2,1,0:T(8,128)(2,1)S(1)}, u32[]{:S(2)}, u32[]{:S(2)}) collective-permute-start(bf16[2,4,40,128]{3,2,1,0:T(8,128)(2,1)} %param.10), channel_id=1, source_target_pairs={{0,1},{1,2},{2,3},{3,4},{4,5},{5,6},{6,7},{7,8},{8,9},{9,10},{10,1... | collective-permute-start | bytes 245768 | tf_op jit(solution)/shard_map/ppermute | solution.py:16
  13.3 13.0 %copy-start.5 = (bf16[3,3,3,128,128]{4,3,2,1,0:T(8,128)(2,1)S(1)}, bf16[3,3,3,128,128]{4,3,2,1,0:T(8,128)(2,1)}, u32[]{:S(2)}) copy-start(bf16[3,3,3,128,128]{4,3,2,1,0:T(8,128)(2,1)} %param.11) | copy-start | bytes 2654212
  17.4 145.0 %all-to-all-start.2 = ((bf16[2,160,128]{2,0,1:T(2,128)(2,1)}), bf16[2,160,128]{2,0,1:T(2,128)(2,1)S(1)}, u32[]{:S(2)}, u32[]{:S(2)}) async-start(bf16[2,160,128]{2,0,1:T(2,128)(2,1)} %copy.45), calls=%async_computation.2 | async-start | bytes 163840 | tf_op jit(solution)/shard_map/all_to_all | solution.py:214
  34.7 112.5 %copy-start.8 = (f32[5120]{0:T(1024)S(1)}, f32[5120]{0:T(1024)}, u32[]{:S(2)}) copy-start(f32[5120]{0:T(1024)} %param.13) | copy-start | bytes 61444
  153.0 3.3 copy-start.7
  156.2 5.3 %copy-start.1 = (bf16[320,5120]{1,0:T(8,128)(2,1)}, bf16[320,5120]{1,0:T(8,128)(2,1)S(1)}, u32[]{:S(2)}) copy-start(bf16[320,5120]{1,0:T(8,128)(2,1)S(1)} %get-tuple-element.36) | copy-start | bytes 9830404
  162.4 17.8 %all-to-all-start = ((bf16[2,160,384]{2,0,1:T(2,128)(2,1)}), bf16[2,160,384]{2,0,1:T(2,128)(2,1)S(1)}, u32[]{:S(2)}, u32[]{:S(2)}) async-start(bf16[2,160,384]{2,0,1:T(2,128)(2,1)} %copy.36), calls=%async_computation | async-start | bytes 491520 | tf_op jit(solution)/shard_map/all_to_all | solution.py:211
  169.5 160.4 %reduce-scatter.2.cloned.1.call-start = ((), (), s32[]{:S(2)}) async-start(), calls=%async_computation.6 | async-start | bytes 4423680 | tf_op jit(solution)/shard_map/reduce_scatter | solution.py:240
  200.2 5.3 %copy-start.2 = (bf16[320,5120]{1,0:T(8,128)(2,1)S(1)}, bf16[320,5120]{1,0:T(8,128)(2,1)}, u32[]{:S(2)}) copy-start(bf16[320,5120]{1,0:T(8,128)(2,1)} %copy-done.1) | copy-start | bytes 9830404
  200.2 5.3 %copy-start.3 = (bf16[2,4,40,5120]{3,2,1,0:T(8,128)(2,1)S(1)}, bf16[2,4,40,5120]{3,2,1,0:T(8,128)(2,1)}, u32[]{:S(2)}) copy-start(bf16[2,4,40,5120]{3,2,1,0:T(8,128)(2,1)} %param.19) | copy-start | bytes 9830404
  215.2 123.9 %copy-start.4 = (bf16[128,5120]{1,0:T(8,128)(2,1)S(1)}, bf16[128,5120]{1,0:T(8,128)(2,1)}, u32[]{:S(2)}) copy-start(bf16[128,5120]{1,0:T(8,128)(2,1)} %param.18) | copy-start | bytes 3932164
  216.2 115.7 %all-to-all-start.1 = ((bf16[64,5,128]{2,1,0:T(8,128)(2,1)}), bf16[64,5,128]{2,1,0:T(8,128)(2,1)S(1)}, u32[]{:S(2)}, u32[]{:S(2)}) async-start(bf16[64,5,128]{2,1,0:T(8,128)(2,1)} %copy.43), calls=%async_computation.1 | async-start | bytes 262144 | tf_op jit(solution)/shard_map/all_to_all | solution.py:213
  331.9 24.8 %all-to-all-start.4 = ((bf16[32,20,384]{2,1,0:T(8,128)(2,1)}), bf16[32,20,384]{2,1,0:T(8,128)(2,1)S(1)}, u32[]{:S(2)}, u32[]{:S(2)}) async-start(bf16[32,20,384]{2,1,0:T(8,128)(2,1)} %reshape.218), calls=%async_computation.5 | async-start | bytes 1179648 | tf_op jit(solution)/shard_map/all_to_all | solution.py:34
Sparse Core Ops, SparseCore 0:
  12.3 122.3 all-gather.2
  215.4 114.5 reduce-scatter.1
where the time goes:
time: 365 us; the launch traced here: 364 us
  waiting for transfers between devices  233 us (64%)
  matrix products  46.7 us (13%)
  starting transfers between devices  31.3 us (9%)
  local copies, waits for them, and re-layouts  17.8 us (5%)
  blocking collectives  17.4 us (5%)
  between operations  14.5 us (4%)
    reduce_scatter x1, waiting for transfers between devices, shards(): lax.psum_scatter(part_spatial.astype(jnp.bfloat16), 'dp', scatter_dimensi...  110 us
    all_gather x1, waiting for transfers between devices, side_by_side(): whole = lax.all_gather(both, axis, axis=dim, tiled=True)  100 us
    all_to_all x1, blocking collectives, shards(): lax.all_to_all(grad_packed_patched, 'ts', split_axis=0, concat_axis=1, ti...  17.4 us
    all_to_all x1, waiting for transfers between devices, sum_at_owner(): lax.all_to_all(parts, axis, split_axis=0, concat_axis=0, tiled=True)  13 us
    unnamed x19, local copies, waits for them, and re-layouts  12.5 us
    all_to_all x1, waiting for transfers between devices, shards(): lax.all_to_all(packed_two, 'ts', split_axis=1, concat_axis=0, tiled=True)  10.6 us
    all_to_all x1, starting transfers between devices, shards(): lax.all_to_all(grad_mix_two, 'ts', split_axis=1, concat_axis=0, tiled=True)  8.51 us
  transfers between devices with their start and end apart: 7, of which 4 were waited for; matrix products, arithmetic and copies ran while one was open for 13% of the time, Pallas kernels for 0%

commit v1 on v0

v1 whole, which is shorter than its diff:
```python
import jax
import jax.numpy as jnp
from jax import lax
from jax.experimental import pallas as pl
from jax.experimental.pallas import tpu as pltpu
from jax.sharding import Mesh
from jax.sharding import PartitionSpec as P

FR = 16
epsilon = 1e-06
masked = -1e30
f32 = jnp.float32
bf16 = jnp.bfloat16

TS = ("z1", "z0", "y", "c")
ROWS = ("z0", "y", "c")
REST = ("x", "zh", "z1")
CLIP = ("y", "c")
ALL = ("x", "zh", "z1", "z0", "y", "c")


def nt(a, b, **kw):
    return lax.dot_general(a, b, (((1,), (1,)), ((), ())), preferred_element_type=f32, **kw)


def tn(a, b, **kw):
    return lax.dot_general(a, b, (((0,), (0,)), ((), ())), preferred_element_type=f32, **kw)


def nn(a, b, **kw):
    return lax.dot_general(a, b, (((1,), (0,)), ((), ())), preferred_element_type=f32, **kw)


def exchange(parts, axes):
    return lax.all_to_all(parts, axes, 0, 0, tiled=True)


def to_all(value, axes):
    size = 1
    for a in axes:
        size *= lax.axis_size(a)
    return exchange(jnp.broadcast_to(value, (size,) + value.shape), axes)


def conv_local(volume, weight, count):
    frames, height, columns, channels = volume.shape
    out_channels = weight.shape[-1]
    padded = jnp.pad(volume, ((0, 0), (1, 1), (1, 1), (0, 0)))
    summed = jnp.zeros((count * height * columns, out_channels), f32)
    for time_tap in range(3):
        for row_tap in range(3):
            for col_tap in range(3):
                window = padded[
                    2 - time_tap : 2 - time_tap + count,
                    row_tap : row_tap + height,
                    col_tap : col_tap + columns,
                    :,
                ]
                summed = summed + nn(
                    window.reshape(-1, channels), weight[time_tap, row_tap, col_tap]
                )
    return summed


def products_kernel(e_ref, os_ref, ot_ref, cot_ref, gram_ref, cots_ref, cott_ref):
    @pl.when(pl.program_id(0) == 0)
    def _():
        gram_ref[...] = jnp.zeros_like(gram_ref)
        cots_ref[...] = jnp.zeros_like(cots_ref)
        cott_ref[...] = jnp.zeros_like(cott_ref)

    e, o, t, c = e_ref[...], os_ref[...], ot_ref[...], cot_ref[...]
    both = jnp.concatenate([e, o], axis=0)
    gram_ref[...] += nt(both, both)
    cots_ref[...] += nt(c, o)
    cott_ref[...] += nt(c, t)


def products(embed, out_s, out_t, cot):
    width = embed.shape[1]
    head = embed.shape[0]
    tokens = cot.shape[0]
    block = 1024
    row = lambda rows: pl.BlockSpec((rows, block), lambda i: (0, i))
    full = lambda r, c: pl.BlockSpec((r, c), lambda i: (0, 0))
    return pl.pallas_call(
        products_kernel,
        grid=(width // block,),
        in_specs=[row(head), row(head), row(head), row(tokens)],
        out_specs=[full(2 * head, 2 * head), full(tokens, head), full(tokens, head)],
        out_shape=[
            jax.ShapeDtypeStruct((2 * head, 2 * head), f32),
            jax.ShapeDtypeStruct((tokens, head), f32),
            jax.ShapeDtypeStruct((tokens, head), f32),
        ],
        name="products",
    )(embed, out_s, out_t, cot)


def output_kernel(f_ref, m_ref, t_ref, e_ref, os_ref, ot_ref, out_ref):
    total = nn(f_ref[...], e_ref[...]) + nn(m_ref[...], os_ref[...]) + nn(t_ref[...], ot_ref[...])
    out_ref[...] = total.astype(bf16)


def output_rows(feats, mix_s, mix_t, embed, out_s, out_t):
    tokens, head = feats.shape
    width = embed.shape[1]
    block = 1024
    row = lambda rows: pl.BlockSpec((rows, block), lambda i: (0, i))
    full = pl.BlockSpec((tokens, head), lambda i: (0, 0))
    return pl.pallas_call(
        output_kernel,
        grid=(width // block,),
        in_specs=[full, full, full, row(head), row(head), row(head)],
        out_specs=row(tokens),
        out_shape=jax.ShapeDtypeStruct((tokens, width), bf16),
        name="output_rows",
    )(feats, mix_s, mix_t, embed, out_s, out_t)


def softmax_rows(scores):
    top = jnp.max(scores, axis=-1, keepdims=True)
    raised = jnp.exp(scores - top)
    return raised / jnp.sum(raised, axis=-1, keepdims=True)


def shards(
    clip_video,
    conv_weight,
    embed_weight,
    gain_spatial,
    gain_temporal,
    input_spatial,
    input_temporal,
    output_spatial,
    output_temporal,
    cotangent,
):
    frames, height, columns, channels = clip_video.shape
    places = height * columns
    tokens = frames * places
    head = embed_weight.shape[0]
    width = embed_weight.shape[1]
    triple = 3 * head
    rows_here = input_spatial.shape[0]
    n_rows = 1
    for a in ROWS:
        n_rows *= lax.axis_size(a)
    cols = triple // n_rows
    scale = head**-0.5
    exact = dict(precision=lax.Precision.HIGHEST)

    n_ts = 1
    for a in TS:
        n_ts *= lax.axis_size(a)
    prior = lax.ppermute(clip_video, TS, [(i, i + 1) for i in range(n_ts - 1)])

    both = jnp.concatenate(
        [input_spatial.reshape(rows_here, n_rows, cols), input_temporal.reshape(rows_here, n_rows, cols)],
        axis=-1,
    )
    mine = exchange(jnp.moveaxis(both, 1, 0), ROWS).reshape(n_rows * rows_here, 2 * cols)
    start = lax.axis_index(REST) * (n_rows * rows_here)
    e_cut = lax.dynamic_slice_in_dim(embed_weight, start, n_rows * rows_here, 1).astype(f32)
    o_cut = lax.dynamic_slice_in_dim(output_spatial, start, n_rows * rows_here, 1).astype(f32)
    gs_cut = lax.dynamic_slice_in_dim(gain_spatial, start, n_rows * rows_here, 0)
    gt_cut = lax.dynamic_slice_in_dim(gain_temporal, start, n_rows * rows_here, 0)
    w_s = mine[:, :cols].astype(f32) * gs_cut[:, None]
    w_t = mine[:, cols:].astype(f32) * gt_cut[:, None]
    dims = (((0,), (1,)), ((), ()))
    part = jnp.concatenate(
        [
            lax.dot_general(w_s, e_cut, dims, preferred_element_type=f32, **exact),
            lax.dot_general(w_t, e_cut, dims, preferred_element_type=f32, **exact),
            lax.dot_general(w_t, o_cut, dims, preferred_element_type=f32, **exact),
        ],
        axis=0,
    ).astype(bf16)
    piece = to_all(part, REST).astype(f32).sum(axis=0).astype(bf16)
    pieces = to_all(piece, ROWS)
    map_s = pieces[:, :cols].reshape(triple, head)
    map_te = pieces[:, cols : 2 * cols].reshape(triple, head)
    map_to = pieces[:, 2 * cols :].reshape(triple, head)

    volume = jnp.concatenate([prior, clip_video], axis=0)
    feats = jax.nn.gelu(conv_local(volume, conv_weight, frames), approximate=True).astype(bf16)
    gram, cot_s, cot_t = products(
        embed_weight, output_spatial, output_temporal, cotangent.reshape(tokens, width)
    )
    gram = gram * (1.0 / width)
    wide = feats.astype(f32)
    square = jnp.sum(nn(wide, gram[:head, :head], **exact) * wide, axis=-1, keepdims=True)
    factor_one = lax.rsqrt(square + epsilon)

    packed = (nt(feats, map_s) * factor_one).astype(bf16).reshape(frames, places, triple)
    q, k, v = packed[..., :head], packed[..., head : 2 * head], packed[..., 2 * head :]
    scores = jnp.einsum("fqd,fkd->fqk", q, k, preferred_element_type=f32) * scale
    attend = softmax_rows(scores)
    rounded = attend.astype(bf16)
    mix = jnp.einsum("fqk,fkd->fqd", rounded, v, preferred_element_type=f32).astype(bf16)

    sent = jnp.concatenate(
        [feats.reshape(frames, places, head), mix, cot_t.astype(bf16).reshape(frames, places, head)],
        axis=-1,
    )
    got = lax.all_to_all(sent, CLIP, split_axis=1, concat_axis=0, tiled=True)
    spots = got.shape[1]
    got = got.reshape(FR * spots, triple)
    x = got[:, : 2 * head]
    g = got[:, 2 * head :]
    xw = x.astype(f32)
    xg = nn(xw, gram, **exact)
    factor_two = lax.rsqrt(jnp.sum(xg * xw, axis=-1, keepdims=True) + epsilon)
    raw = nt(x[:, :head], map_te) + nt(x[:, head:], map_to)
    packed_t = (raw * factor_two).astype(bf16)
    qt, kt, vt = packed_t[:, :head], packed_t[:, head : 2 * head], packed_t[:, 2 * head :]
    n = FR * spots
    row = lax.broadcasted_iota(jnp.int32, (n, n), 0)
    col = lax.broadcasted_iota(jnp.int32, (n, n), 1)
    allowed = (row >= col) & (row % spots == col % spots)
    att_t = softmax_rows(jnp.where(allowed, nt(qt, kt) * scale, masked))
    rnd_t = att_t.astype(bf16)
    mix_t = nn(rnd_t, vt).astype(bf16)
    d_att = nt(g, vt)
    d_v = tn(rnd_t, g)
    d_sc = (att_t * (d_att - jnp.sum(d_att * att_t, axis=-1, keepdims=True))).astype(bf16)
    d_q = nn(d_sc, kt) * scale
    d_k = tn(d_sc, qt) * scale
    gpt = jnp.concatenate([d_q, d_k, d_v], axis=-1).astype(bf16)
    inner = jnp.sum(gpt.astype(f32) * raw, axis=-1, keepdims=True) * (1.0 / width)
    corr = factor_two * nn(gpt, map_to) - (factor_two**3 * inner * width) * xg[:, head:]
    back = jnp.concatenate([mix_t, corr.astype(bf16)], axis=-1).reshape(FR, spots, 2 * head)
    home = lax.all_to_all(back, CLIP, split_axis=0, concat_axis=1, tiled=True)
    home = home.reshape(tokens, 2 * head)
    mix_home = home[:, :head]

    up = (cot_s + home[:, head:].astype(f32)).astype(bf16).reshape(frames, places, head)
    d_att = jnp.einsum("fqd,fkd->fqk", up, v, preferred_element_type=f32)
    d_v = jnp.einsum("fqk,fqd->fkd", rounded, up, preferred_element_type=f32)
    d_sc = (attend * (d_att - jnp.sum(d_att * attend, axis=-1, keepdims=True))).astype(bf16)
    d_q = jnp.einsum("fqk,fkd->fqd", d_sc, k, preferred_element_type=f32) * scale
    d_k = jnp.einsum("fqk,fqd->fkd", d_sc, q, preferred_element_type=f32) * scale
    gps = jnp.concatenate([d_q, d_k, d_v], axis=-1).astype(bf16).reshape(tokens, triple)
    total = tn(gps, (wide * factor_one).astype(bf16)).astype(bf16)
    total = exchange(total.reshape(n_rows, cols, head), ROWS).astype(f32).sum(axis=0).astype(bf16)
    total = to_all(total, REST).astype(f32).sum(axis=0).astype(bf16)
    total = to_all(total, ROWS).reshape(triple, head)
    first = lax.axis_index(ALL) * rows_here
    e_mine = lax.dynamic_slice_in_dim(embed_weight, first, rows_here, 1)
    g_mine = lax.dynamic_slice_in_dim(gain_spatial, first, rows_here, 0)
    grad = lax.dot_general(e_mine, total, (((0,), (1,)), ((), ())), preferred_element_type=f32)
    grad = grad * g_mine[:, None]

    layer = output_rows(
        feats, mix.reshape(tokens, head), mix_home, embed_weight, output_spatial, output_temporal
    )
    return (layer.reshape(frames, height, columns, width), grad)


def solution(mesh):
    split = Mesh(mesh.devices.reshape(4, 2, 2, 2, 4, 2), ALL)
    rows = P(ALL, None)
    blocks = P(ALL, None, None, None)
    placed = (blocks, P(), P(), P(), P(), rows, rows, P(), P(), blocks)
    return jax.shard_map(
        shards,
        mesh=split,
        in_specs=placed,
        out_specs=(blocks, rows),
        check_vma=False,
    )
```

time: 365 us -> 133 us (0.36)
  waiting for transfers between devices: 233 us -> 21.9 us
  matrix products: 46.7 us -> 15.6 us
  blocking collectives: 17.4 us -> 31 us
  Pallas kernels: 0 us -> 13.5 us
  between operations: 14.5 us -> 1.08 us
  local copies, waits for them, and re-layouts: 17.8 us -> 10.2 us
  starting transfers between devices: 31.3 us -> 35.5 us
    reduce_scatter x1 -> x0, waiting for transfers between devices: 110 us -> none  [shards(): lax.psum_scatter(part_spatial.astype(jnp.bfloat16), 'dp', scatter_dimensi...]
    all_gather x1 -> x0, waiting for transfers between devices: 100 us -> none  [side_by_side(): whole = lax.all_gather(both, axis, axis=dim, tiled=True)]
    dot_general x46 -> x49, matrix products: 46.4 us -> 15.3 us  [the longest x32 5.99 us: nn(): lax.dot_general(a, b, (((1,), (0,)), ((), ())), preferred_element_type=f3...]
    all_to_all x1 -> x3, blocking collectives: 17.4 us -> 31 us  [the longest x2 21.8 us: exchange(): return lax.all_to_all(parts, axes, 0, 0, tiled=True)]
    pallas_call x0 -> x2, Pallas kernels: none -> 13.5 us  [the longest x1 6.8 us: output_rows(): pl.pallas_call(output_kernel, grid=(width // block,), in_specs=[full, ful...]
    unnamed x19 -> x15, local copies, waits for them, and re-layouts: 12.5 us -> 1.75 us
    all_to_all x4 -> x5, starting transfers between devices: 26.6 us -> 31.9 us  [the longest x4 27.6 us: exchange(): return lax.all_to_all(parts, axes, 0, 0, tiled=True)]
    all_to_all x4 -> x5, waiting for transfers between devices: 23.6 us -> 21.9 us  [the longest x4 15.6 us: exchange(): return lax.all_to_all(parts, axes, 0, 0, tiled=True)]
  transfers between devices with their start and end apart: 7 -> 6, of which waited for: 4 -> 3; matrix products, arithmetic and copies ran while one was open for 13% -> 11% of each run, Pallas kernels for 0% -> 10%
where the time goes in v1:
time: 133 us; the launch traced here: 132 us
  starting transfers between devices  35.5 us (27%)
  blocking collectives  31 us (23%)
  waiting for transfers between devices  21.9 us (16%)
  matrix products  15.6 us (12%)
  Pallas kernels  13.5 us (10%)
  local copies, waits for them, and re-layouts  10.2 us (8%)
  other arithmetic  2.69 us (2%)
    all_to_all x4, starting transfers between devices, exchange(): return lax.all_to_all(parts, axes, 0, 0, tiled=True)  27.6 us
    all_to_all x2, blocking collectives, exchange(): return lax.all_to_all(parts, axes, 0, 0, tiled=True)  21.8 us
    all_to_all x4, waiting for transfers between devices, exchange(): return lax.all_to_all(parts, axes, 0, 0, tiled=True)  15.6 us
    all_to_all x1, blocking collectives, shards(): home = lax.all_to_all(back, CLIP, split_axis=0, concat_axis=1, tiled=True)  9.27 us
    pallas_call x1, Pallas kernels, output_rows(): pl.pallas_call(output_kernel, grid=(width // block,), in_specs=[full, ful...  6.8 us
    pallas_call x1, Pallas kernels, products(): pl.pallas_call(products_kernel, grid=(width // block,), in_specs=[row(hea...  6.73 us
    all_to_all x1, waiting for transfers between devices, shards(): got = lax.all_to_all(sent, CLIP, split_axis=1, concat_axis=0, tiled=True)  6.32 us
    dot_general x32, matrix products, nn(): lax.dot_general(a, b, (((1,), (0,)), ((), ())), preferred_element_type=f3...  5.99 us
  transfers between devices with their start and end apart: 6, of which 3 were waited for; matrix products, arithmetic and copies ran while one was open for 11% of the time, Pallas kernels for 10%

profile of v1, /device:TPU:1, one launch (start us, length us, event | category | flops | bytes accessed | tf_op | source)
XLA Modules:
  0.0 131.5 jit_solution(408887727086307722)
XLA Ops:
  0.6 0.9 reshape.210
  1.5 0.9 reshape.211
  2.5 0.8 reshape.228
  3.3 7.3 %all-to-all-start = ((bf16[16,2,480]{2,1,0:T(2,128)(2,1)}), bf16[16,2,480]{2,1,0:T(2,128)(2,1)S(1)}, u32[]{:S(2)}, u32[]{:S(2)}) async-start(bf16[16,2,480]{2,1,0:T(2,128)(2,1)} %reshape.228), calls=%async_computation | async-start | bytes 65536 | tf_op jit(solution)/shard_map/all_to_all | solution.py:35
  10.6 3.5 %collective-permute-start = (bf16[2,4,40,128]{3,2,1,0:T(8,128)(2,1)}, bf16[2,4,40,128]{3,2,1,0:T(8,128)(2,1)S(1)}, u32[]{:S(2)}, u32[]{:S(2)}) collective-permute-start(bf16[2,4,40,128]{3,2,1,0:T(8,128)(2,1)} %param.10), channel_id=1, source_target_pairs={{0,1},{1,2},{2,3},{3,4},{4,5},{5,6},{6,7},{7,8},{8,9},{9,10},{10,1... | collective-permute-start | bytes 245768 | tf_op jit(solution)/shard_map/ppermute | solution.py:156
  14.2 6.7 %products.1 = (f32[256,256]{1,0:T(8,128)}, f32[320,128]{1,0:T(8,128)}, f32[320,128]{1,0:T(8,128)}) custom-call(bf16[128,5120]{1,0:T(8,128)(2,1)} %e_ref.3, bf16[128,5120]{1,0:T(8,128)(2,1)} %os_ref.3, bf16[128,5120]{1,0:T(8,128)(2,1)} %ot_ref.3, bf16[320,5120]{1,0:T(8,128)(2,1)} %bitcast.172), custom_call_target="tpu_custom_call" | custom-call | tf_op jit(solution)/shard_map/products/pallas_call | solution.py:86
  20.9 1.0 broadcast_multiply_fusion
  21.9 0.8 dynamic_slice.20
  22.7 0.8 dynamic_slice.18
  23.5 0.9 convert_element_type.81
  24.6 1.3 %convolution_convert_fusion.5 = bf16[24,128]{1,0:T(8,128)(2,1)S(1)} fusion(bf16[128,5120]{1,0:T(8,128)(2,1)} %os_ref.3, s32[]{:T(128)S(6)} %select_n.25, f32[320]{0:T(512)S(1)} %dynamic_slice.20, bf16[320,48]{1,0:T(8,128)(2,1)S(1)} %reshape.212), kind=kOutput, calls=%fused_computation.54 | convolution fusion | flops 11814912 | bytes 136452 | tf_op jit(solution)/shard_map/dot_general | solution.py:175
  25.9 1.3 %convolution_convert_fusion.6 = bf16[24,128]{1,0:T(8,128)(2,1)S(1)} fusion(bf16[128,5120]{1,0:T(8,128)(2,1)} %e_ref.3, s32[]{:T(128)S(6)} %select_n.25, f32[320]{0:T(512)S(1)} %dynamic_slice.20, bf16[320,48]{1,0:T(8,128)(2,1)S(1)} %reshape.212), kind=kOutput, calls=%fused_computation.55 | convolution fusion | flops 11814912 | bytes 136452 | tf_op jit(solution)/shard_map/dot_general | solution.py:174
  27.2 1.3 convolution_convert_fusion.7
  28.6 0.8 broadcast_in_dim.12
  29.3 9.9 %all-to-all-start.1 = ((bf16[16,72,128]{2,1,0:T(8,128)(2,1)}), bf16[16,72,128]{2,1,0:T(8,128)(2,1)S(1)}, u32[]{:S(2)}, u32[]{:S(2)}) async-start(bf16[16,72,128]{2,1,0:T(8,128)(2,1)} %broadcast_in_dim.12), calls=%async_computation.1 | async-start | bytes 589824 | tf_op jit(solution)/shard_map/all_to_all | solution.py:35
  39.6 0.8 copy-done.2
  44.6 8.7 %all-to-all-done.1 = bf16[16,72,128]{2,1,0:T(8,128)(2,1)S(1)} async-done(((bf16[16,72,128]{2,1,0:T(8,128)(2,1)}), bf16[16,72,128]{2,1,0:T(8,128)(2,1)S(1)}, u32[]{:S(2)}, u32[]{:S(2)}) %all-to-all-start.1) | async-done | bytes 294944 | tf_op jit(solution)/shard_map/all_to_all | solution.py:35
  53.3 0.8 broadcast_in_dim.13
  54.1 5.4 %all-to-all-start.2 = ((bf16[16,72,128]{2,1,0:T(8,128)(2,1)}), bf16[16,72,128]{2,1,0:T(8,128)(2,1)S(1)}, u32[]{:S(2)}, u32[]{:S(2)}) async-start(bf16[16,72,128]{2,1,0:T(8,128)(2,1)} %broadcast_in_dim.13), calls=%async_computation.2 | async-start | bytes 589824 | tf_op jit(solution)/shard_map/all_to_all | solution.py:35
  60.1 6.9 %all-to-all-done.2 = bf16[16,72,128]{2,1,0:T(8,128)(2,1)S(1)} async-done(((bf16[16,72,128]{2,1,0:T(8,128)(2,1)}), bf16[16,72,128]{2,1,0:T(8,128)(2,1)S(1)}, u32[]{:S(2)}, u32[]{:S(2)}) %all-to-all-start.2) | async-done | bytes 294944 | tf_op jit(solution)/shard_map/all_to_all | solution.py:35
  68.1 0.9 copy.34
  69.0 4.3 %all-to-all-start.3 = ((bf16[2,160,384]{2,0,1:T(2,128)(2,1)}), bf16[2,160,384]{2,0,1:T(2,128)(2,1)S(1)}, u32[]{:S(2)}, u32[]{:S(2)}) async-start(bf16[2,160,384]{2,0,1:T(2,128)(2,1)} %copy.34), calls=%async_computation.3 | async-start | bytes 491520 | tf_op jit(solution)/shard_map/all_to_all | solution.py:206
  73.3 6.3 %all-to-all-done.3 = bf16[2,160,384]{2,0,1:T(2,128)(2,1)S(1)} async-done(((bf16[2,160,384]{2,0,1:T(2,128)(2,1)}), bf16[2,160,384]{2,0,1:T(2,128)(2,1)S(1)}, u32[]{:S(2)}, u32[]{:S(2)}) %all-to-all-start.3) | async-done | bytes 245792 | tf_op jit(solution)/shard_map/all_to_all | solution.py:206
  83.0 9.3 %all_to_all.60 = bf16[16,20,256]{2,1,0:T(8,128)(2,1)S(1)} all-to-all(bf16[16,20,256]{2,1,0:T(8,128)(2,1)S(1)} %reshape.222), channel_id=1, replica_groups=mesh['x'=4,'zh'=2,'z1'=2,'z0'=2,'y'=4,'c'=2] {'y','c'}, dimensions={0} | all-to-all | bytes 327680 | tf_op jit(solution)/shard_map/all_to_all | solution.py:233
  94.1 9.3 %all_to_all.61 = bf16[16,24,128]{2,1,0:T(8,128)(2,1)S(1)} all-to-all(bf16[16,24,128]{2,1,0:T(8,128)(2,1)S(1)} %bitcast.217), channel_id=1, replica_groups=mesh['x'=4,'zh'=2,'z1'=2,'z0'=2,'y'=4,'c'=2] {'z0','y','c'}, dimensions={0} | all-to-all | bytes 196608 | tf_op jit(solution)/shard_map/all_to_all | solution.py:35
  103.4 12.5 %all_to_all.62 = bf16[16,24,128]{2,1,0:T(8,128)(2,1)S(1)} all-to-all(bf16[16,24,128]{2,1,0:T(8,128)(2,1)S(1)} %broadcast_in_dim.15), channel_id=1, replica_groups=mesh['x'=4,'zh'=2,'z1'=2,'z0'=2,'y'=4,'c'=2] {'x','zh','z1'}, dimensions={0} | all-to-all | bytes 196608 | tf_op jit(solution)/shard_map/all_to_all | solution.py:35
  115.9 0.6 broadcast_in_dim.16
  116.6 5.0 %all-to-all-start.7 = ((bf16[16,24,128]{2,1,0:T(8,128)(2,1)}), bf16[16,24,128]{2,1,0:T(8,128)(2,1)S(1)}, u32[]{:S(2)}, u32[]{:S(2)}) async-start(bf16[16,24,128]{2,1,0:T(8,128)(2,1)} %broadcast_in_dim.16), calls=%async_computation.7 | async-start | bytes 196608 | tf_op jit(solution)/shard_map/all_to_all | solution.py:35
  121.6 0.8 dynamic_slice.23
  122.4 0.6 slice.309.t_ref
  123.0 6.8 %output_rows.1 = bf16[320,5120]{1,0:T(8,128)(2,1)} custom-call(bf16[320,128]{1,0:T(8,128)(2,1)} %copy-done, bf16[320,128]{1,0:T(8,128)(2,1)} %bitcast.189, bf16[320,128]{1,0:T(8,128)(2,1)} %slice.309.t_ref, bf16[128,5120]{1,0:T(8,128)(2,1)} %e_ref.3, bf16[128,5120]{1,0:T(8,128)(2,1)} %os_ref.3, bf16[128,5120]{1,0:T(8,128)(2,1)} %ot_ref.3), custom_call_target="tpu_custom_call" | custom-call | tf_op jit(solution)/shard_map/output_rows/pallas_call | solution.py:111
  129.8 1.7 %convolution_multiply_fusion.9 = f32[20,384]{1,0:T(8,128)} fusion(bf16[384,128]{1,0:T(8,128)(2,1)S(1)} %bitcast.184, bf16[128,5120]{1,0:T(8,128)(2,1)} %e_ref.3, s32[]{:T(128)S(6)} %select_n.29, f32[20]{0:T(128)S(1)} %dynamic_slice.23), kind=kOutput, calls=%fused_computation.53 | convolution fusion | flops 1973760 | bytes 161876 | tf_op jit(solution)/shard_map/dot_general | solution.py:251
  (93 shorter events, 11.7 us)
Async XLA Ops:
  3.3 21.1 %all-to-all-start = ((bf16[16,2,480]{2,1,0:T(2,128)(2,1)}), bf16[16,2,480]{2,1,0:T(2,128)(2,1)S(1)}, u32[]{:S(2)}, u32[]{:S(2)}) async-start(bf16[16,2,480]{2,1,0:T(2,128)(2,1)} %reshape.228), calls=%async_computation | async-start | bytes 65536 | tf_op jit(solution)/shard_map/all_to_all | solution.py:35
  10.6 28.6 %collective-permute-start = (bf16[2,4,40,128]{3,2,1,0:T(8,128)(2,1)}, bf16[2,4,40,128]{3,2,1,0:T(8,128)(2,1)S(1)}, u32[]{:S(2)}, u32[]{:S(2)}) collective-permute-start(bf16[2,4,40,128]{3,2,1,0:T(8,128)(2,1)} %param.10), channel_id=1, source_target_pairs={{0,1},{1,2},{2,3},{3,4},{4,5},{5,6},{6,7},{7,8},{8,9},{9,10},{10,1... | collective-permute-start | bytes 245768 | tf_op jit(solution)/shard_map/ppermute | solution.py:156
  20.9 18.3 %copy-start.4 = (bf16[2,4,40,128]{3,2,1,0:T(8,128)(2,1)S(1)}, bf16[2,4,40,128]{3,2,1,0:T(8,128)(2,1)}, u32[]{:S(2)}) copy-start(bf16[2,4,40,128]{3,2,1,0:T(8,128)(2,1)} %param.10) | copy-start | bytes 245764
  29.3 24.0 %all-to-all-start.1 = ((bf16[16,72,128]{2,1,0:T(8,128)(2,1)}), bf16[16,72,128]{2,1,0:T(8,128)(2,1)S(1)}, u32[]{:S(2)}, u32[]{:S(2)}) async-start(bf16[16,72,128]{2,1,0:T(8,128)(2,1)} %broadcast_in_dim.12), calls=%async_computation.1 | async-start | bytes 589824 | tf_op jit(solution)/shard_map/all_to_all | solution.py:35
  39.2 1.2 copy-start.2
  54.1 12.9 %all-to-all-start.2 = ((bf16[16,72,128]{2,1,0:T(8,128)(2,1)}), bf16[16,72,128]{2,1,0:T(8,128)(2,1)S(1)}, u32[]{:S(2)}, u32[]{:S(2)}) async-start(bf16[16,72,128]{2,1,0:T(8,128)(2,1)} %broadcast_in_dim.13), calls=%async_computation.2 | async-start | bytes 589824 | tf_op jit(solution)/shard_map/all_to_all | solution.py:35
  59.7 34.0 %copy-start = (bf16[320,128]{1,0:T(8,128)(2,1)}, bf16[320,128]{1,0:T(8,128)(2,1)S(1)}, u32[]{:S(2)}) copy-start(bf16[320,128]{1,0:T(8,128)(2,1)S(1)} %fusion.29.f_ref) | copy-start | bytes 245764
  68.0 12.2 %copy-start.3 = (bf16[2,160,128]{2,1,0:T(8,128)(2,1)}, bf16[2,160,128]{2,1,0:T(8,128)(2,1)S(1)}, u32[]{:S(2)}) copy-start(bf16[2,160,128]{2,1,0:T(8,128)(2,1)S(1)} %convolution_convert_fusion.4) | copy-start | bytes 245764
  68.0 11.7 %copy-start.1 = (f32[256,256]{1,0:T(8,128)S(1)}, f32[256,256]{1,0:T(8,128)}, u32[]{:S(2)}) copy-start(f32[256,256]{1,0:T(8,128)} %get-tuple-element.5) | copy-start | bytes 786436
  69.0 10.7 %all-to-all-start.3 = ((bf16[2,160,384]{2,0,1:T(2,128)(2,1)}), bf16[2,160,384]{2,0,1:T(2,128)(2,1)S(1)}, u32[]{:S(2)}, u32[]{:S(2)}) async-start(bf16[2,160,384]{2,0,1:T(2,128)(2,1)} %copy.34), calls=%async_computation.3 | async-start | bytes 491520 | tf_op jit(solution)/shard_map/all_to_all | solution.py:206
  82.9 9.6 %copy-start.5 = (f32[320,128]{1,0:T(8,128)S(1)}, f32[320,128]{1,0:T(8,128)}, u32[]{:S(2)}) copy-start(f32[320,128]{1,0:T(8,128)} %get-tuple-element.7) | copy-start | bytes 491524
  116.6 13.3 %all-to-all-start.7 = ((bf16[16,24,128]{2,1,0:T(8,128)(2,1)}), bf16[16,24,128]{2,1,0:T(8,128)(2,1)S(1)}, u32[]{:S(2)}, u32[]{:S(2)}) async-start(bf16[16,24,128]{2,1,0:T(8,128)(2,1)} %broadcast_in_dim.16), calls=%async_computation.7 | async-start | bytes 196608 | tf_op jit(solution)/shard_map/all_to_all | solution.py:35

commit v2 on v1

v2 whole, which is shorter than its diff:
```python
import jax
import jax.numpy as jnp
from jax import lax
from jax.experimental import pallas as pl
from jax.experimental.pallas import tpu as pltpu
from jax.sharding import Mesh
from jax.sharding import PartitionSpec as P

FR = 16
epsilon = 1e-06
masked = -1e30
f32 = jnp.float32
bf16 = jnp.bfloat16

ALL = ("x", "zh", "zl", "y", "c")
TS = ("zl", "y", "c")
DP = ("x", "zh")
PLANE = ("x", "y", "c")
LINE = ("zh", "zl")
CLIP = ("y", "c")


def nt(a, b, **kw):
    return lax.dot_general(a, b, (((1,), (1,)), ((), ())), preferred_element_type=f32, **kw)


def tn(a, b, **kw):
    return lax.dot_general(a, b, (((0,), (0,)), ((), ())), preferred_element_type=f32, **kw)


def nn(a, b, **kw):
    return lax.dot_general(a, b, (((1,), (0,)), ((), ())), preferred_element_type=f32, **kw)


def exchange(parts, axes):
    return lax.all_to_all(parts, axes, 0, 0, tiled=True)


def to_all(value, axes):
    size = 1
    for a in axes:
        size *= lax.axis_size(a)
    return exchange(jnp.broadcast_to(value, (size,) + value.shape), axes)


def conv_local(volume, weight, count):
    frames, height, columns, channels = volume.shape
    out_channels = weight.shape[-1]
    padded = jnp.pad(volume, ((0, 0), (1, 1), (1, 1), (0, 0)))
    summed = jnp.zeros((count * height * columns, out_channels), f32)
    for time_tap in range(3):
        for row_tap in range(3):
            for col_tap in range(3):
                window = padded[
                    2 - time_tap : 2 - time_tap + count,
                    row_tap : row_tap + height,
                    col_tap : col_tap + columns,
                    :,
                ]
                summed = summed + nn(
                    window.reshape(-1, channels), weight[time_tap, row_tap, col_tap]
                )
    return summed


def products_kernel(e_ref, os_ref, ot_ref, cot_ref, gram_ref, cots_ref, cott_ref):
    @pl.when(pl.program_id(0) == 0)
    def _():
        gram_ref[...] = jnp.zeros_like(gram_ref)
        cots_ref[...] = jnp.zeros_like(cots_ref)
        cott_ref[...] = jnp.zeros_like(cott_ref)

    e, o, t, c = e_ref[...], os_ref[...], ot_ref[...], cot_ref[...]
    both = jnp.concatenate([e, o], axis=0)
    gram_ref[...] += nt(both, both)
    cots_ref[...] += nt(c, o)
    cott_ref[...] += nt(c, t)


def products(embed, out_s, out_t, cot):
    width = embed.shape[1]
    head = embed.shape[0]
    tokens = cot.shape[0]
    block = 1024
    row = lambda rows: pl.BlockSpec((rows, block), lambda i: (0, i))
    full = lambda r, c: pl.BlockSpec((r, c), lambda i: (0, 0))
    return pl.pallas_call(
        products_kernel,
        grid=(width // block,),
        in_specs=[row(head), row(head), row(head), row(tokens)],
        out_specs=[full(2 * head, 2 * head), full(tokens, head), full(tokens, head)],
        out_shape=[
            jax.ShapeDtypeStruct((2 * head, 2 * head), f32),
            jax.ShapeDtypeStruct((tokens, head), f32),
            jax.ShapeDtypeStruct((tokens, head), f32),
        ],
        name="products",
    )(embed, out_s, out_t, cot)


def output_kernel(f_ref, m_ref, t_ref, e_ref, os_ref, ot_ref, out_ref):
    total = nn(f_ref[...], e_ref[...]) + nn(m_ref[...], os_ref[...]) + nn(t_ref[...], ot_ref[...])
    out_ref[...] = total.astype(bf16)


def output_rows(feats, mix_s, mix_t, embed, out_s, out_t):
    tokens, head = feats.shape
    width = embed.shape[1]
    block = 1024
    row = lambda rows: pl.BlockSpec((rows, block), lambda i: (0, i))
    full = pl.BlockSpec((tokens, head), lambda i: (0, 0))
    return pl.pallas_call(
        output_kernel,
        grid=(width // block,),
        in_specs=[full, full, full, row(head), row(head), row(head)],
        out_specs=row(tokens),
        out_shape=jax.ShapeDtypeStruct((tokens, width), bf16),
        name="output_rows",
    )(feats, mix_s, mix_t, embed, out_s, out_t)


def maps_kernel(at_ref, ws_ref, wt_ref, e_ref, os_ref, gs_ref, gt_ref, maps_ref, e_mine_ref, g_mine_ref):
    rows, triple = ws_ref.shape
    head, wide = e_ref.shape
    first = at_ref[1] * rows
    r = lax.broadcasted_iota(jnp.int32, (rows, wide), 0)
    c = lax.broadcasted_iota(jnp.int32, (rows, wide), 1)
    chosen = jnp.where(c == r + first, 1.0, 0.0)
    pick = chosen.astype(bf16)
    e = e_ref[...]
    e32 = e.astype(f32)
    o32 = os_ref[...].astype(f32)

    def product(weight, scaled):
        placed = tn(weight, pick).astype(bf16)
        high = scaled.astype(bf16)
        low = (scaled - high.astype(f32)).astype(bf16)
        return nt(placed, high) + nt(placed, low)

    gs = gs_ref[...]
    gt = gt_ref[...]
    maps_ref[:triple] = product(ws_ref[...], e32 * gs).astype(bf16)
    later = product(wt_ref[...], jnp.concatenate([e32, o32], axis=0) * gt)
    maps_ref[triple : 2 * triple] = later[:, :head].astype(bf16)
    maps_ref[2 * triple : 3 * triple] = later[:, head:].astype(bf16)
    maps_ref[3 * triple :] = jnp.zeros((maps_ref.shape[0] - 3 * triple, head), bf16)
    e_mine_ref[...] = nt(pick, e).astype(bf16)
    g_mine_ref[...] = jnp.broadcast_to(jnp.sum(chosen * gs, axis=1, keepdims=True), g_mine_ref.shape)


def local_maps(at, w_s, w_t, embed, out_s, gain_s, gain_t, padded):
    rows, triple = w_s.shape
    head, width = embed.shape
    wide = width // lax.axis_size(DP[0]) // lax.axis_size(DP[1])
    full = lambda r, c: pl.BlockSpec((r, c), lambda i, at: (0, 0))
    cut = lambda r: pl.BlockSpec((r, wide), lambda i, at: (0, at[0]))
    return pl.pallas_call(
        maps_kernel,
        grid_spec=pltpu.PrefetchScalarGridSpec(
            num_scalar_prefetch=1,
            grid=(1,),
            in_specs=[full(rows, triple), full(rows, triple), cut(head), cut(head), cut(1), cut(1)],
            out_specs=[full(padded, head), full(rows, head), full(rows, triple)],
        ),
        out_shape=[
            jax.ShapeDtypeStruct((padded, head), bf16),
            jax.ShapeDtypeStruct((rows, head), bf16),
            jax.ShapeDtypeStruct((rows, triple), f32),
        ],
        name="local_maps",
    )(at, w_s, w_t, embed, out_s, gain_s.reshape(1, width), gain_t.reshape(1, width))


def group_size(axes):
    size = 1
    for a in axes:
        size *= lax.axis_size(a)
    return size


def summed_everywhere(value):
    n = group_size(PLANE)
    parts = exchange(value.reshape(n, value.shape[0] // n, value.shape[1]), PLANE)
    mine = parts.astype(f32).sum(axis=0).astype(bf16)
    mine = to_all(mine, LINE).astype(f32).sum(axis=0).astype(bf16)
    return to_all(mine, PLANE).reshape(value.shape)


def softmax_rows(scores):
    top = jnp.max(scores, axis=-1, keepdims=True)
    raised = jnp.exp(scores - top)
    return raised / jnp.sum(raised, axis=-1, keepdims=True)


def shards(
    clip_video,
    conv_weight,
    embed_weight,
    gain_spatial,
    gain_temporal,
    input_spatial,
    input_temporal,
    output_spatial,
    output_temporal,
    cotangent,
):
    frames, height, columns, channels = clip_video.shape
    places = height * columns
    tokens = frames * places
    head, width = embed_weight.shape
    triple = 3 * head
    scale = head**-0.5
    exact = dict(precision=lax.Precision.HIGHEST)
    n_ts = group_size(TS)
    n_clip = group_size(CLIP)
    spots = places // n_clip
    clip_tokens = FR * places
    own = FR * spots

    prior = lax.ppermute(clip_video, TS, [(i, i + 1) for i in range(n_ts - 1)])

    at = jnp.stack([lax.axis_index(DP), lax.axis_index(TS)]).astype(jnp.int32)
    maps, e_mine, g_mine = local_maps(
        at, input_spatial, input_temporal, embed_weight, output_spatial, gain_spatial, gain_temporal, 10 * head
    )
    maps = summed_everywhere(maps)
    map_s = maps[:triple]
    map_te = maps[triple : 2 * triple]
    map_to = maps[2 * triple : 3 * triple]

    volume = jnp.concatenate([prior, clip_video], axis=0)
    feats_home = jax.nn.gelu(conv_local(volume, conv_weight, frames), approximate=True).astype(bf16)
    feats = to_all(feats_home, CLIP).reshape(FR, places, head)
    gram, cot_s, cot_t = products(
        embed_weight, output_spatial, output_temporal, cotangent.reshape(tokens, width)
    )
    sent = jnp.concatenate([cot_s, cot_t], axis=-1).astype(bf16).reshape(frames, places, 2 * head)
    cots = lax.all_to_all(sent, CLIP, split_axis=1, concat_axis=0, tiled=True)
    gram = gram * (1.0 / width)
    slot = lax.axis_index(CLIP) * spots
    flat = feats.reshape(clip_tokens, head)
    wide = flat.astype(f32)
    square = jnp.sum(nn(wide, gram[:head, :head], **exact) * wide, axis=-1, keepdims=True)
    factor_one = lax.rsqrt(square + epsilon)
    scaled = (wide * factor_one).astype(bf16)
    feats_own = lax.dynamic_slice_in_dim(feats, slot, spots, 1).reshape(own, head)
    scaled_own = lax.dynamic_slice_in_dim(scaled.reshape(FR, places, head), slot, spots, 1).reshape(own, head)
    factor_own = lax.dynamic_slice_in_dim(factor_one.reshape(FR, places, 1), slot, spots, 1).reshape(own, 1)

    q = (nt(feats_own, map_s[:head]) * factor_own).astype(bf16).reshape(FR, spots, head)
    kv = (nt(flat, map_s[head:]) * factor_one).astype(bf16).reshape(FR, places, 2 * head)
    k, v = kv[..., :head], kv[..., head:]
    scores = jnp.einsum("fqd,fkd->fqk", q, k, preferred_element_type=f32) * scale
    attend = softmax_rows(scores)
    rounded = attend.astype(bf16)
    mix = jnp.einsum("fqk,fkd->fqd", rounded, v, preferred_element_type=f32).astype(bf16)

    mix_own = mix.reshape(own, head)
    g = cots[..., head:].reshape(own, head)
    x = jnp.concatenate([feats_own, mix_own], axis=-1)
    xw = x.astype(f32)
    xg = nn(xw, gram, **exact)
    factor_two = lax.rsqrt(jnp.sum(xg * xw, axis=-1, keepdims=True) + epsilon)
    raw = nt(feats_own, map_te) + nt(mix_own, map_to)
    packed_t = (raw * factor_two).astype(bf16)
    qt, kt, vt = packed_t[:, :head], packed_t[:, head : 2 * head], packed_t[:, 2 * head :]
    row = lax.broadcasted_iota(jnp.int32, (own, own), 0)
    col = lax.broadcasted_iota(jnp.int32, (own, own), 1)
    allowed = (row >= col) & (row % spots == col % spots)
    att_t = softmax_rows(jnp.where(allowed, nt(qt, kt) * scale, masked))
    rnd_t = att_t.astype(bf16)
    mix_t = nn(rnd_t, vt).astype(bf16)
    d_att = nt(g, vt)
    d_v = tn(rnd_t, g)
    d_sc = (att_t * (d_att - jnp.sum(d_att * att_t, axis=-1, keepdims=True))).astype(bf16)
    d_q = nn(d_sc, kt) * scale
    d_k = tn(d_sc, qt) * scale
    gpt = jnp.concatenate([d_q, d_k, d_v], axis=-1).astype(bf16)
    inner = jnp.sum(gpt.astype(f32) * raw, axis=-1, keepdims=True)
    corr = factor_two * nn(gpt, map_to) - (factor_two**3 * inner) * xg[:, head:]

    up = (cots[..., :head].astype(f32) + corr.reshape(FR, spots, head)).astype(bf16)
    d_att = jnp.einsum("fqd,fkd->fqk", up, v, preferred_element_type=f32)
    d_v = jnp.einsum("fqk,fqd->fkd", rounded, up, preferred_element_type=f32).astype(bf16)
    d_sc = (attend * (d_att - jnp.sum(d_att * attend, axis=-1, keepdims=True))).astype(bf16)
    d_q = (jnp.einsum("fqk,fkd->fqd", d_sc, k, preferred_element_type=f32) * scale).astype(bf16)
    d_k = (jnp.einsum("fqk,fqd->fkd", d_sc, q, preferred_element_type=f32) * scale).astype(bf16)
    total = jnp.concatenate(
        [
            tn(d_q.reshape(own, head), scaled_own),
            tn(d_k.reshape(clip_tokens, head), scaled),
            tn(d_v.reshape(clip_tokens, head), scaled),
            jnp.zeros((head, head), f32),
        ],
        axis=0,
    ).astype(bf16)
    total = summed_everywhere(total)[:triple]
    grad = nt(e_mine, total) * g_mine

    back = jnp.concatenate([mix, mix_t.reshape(FR, spots, head)], axis=-1)
    home = lax.all_to_all(back, CLIP, split_axis=0, concat_axis=1, tiled=True).reshape(tokens, 2 * head)
    layer = output_rows(
        feats_home, home[:, :head], home[:, head:], embed_weight, output_spatial, output_temporal
    )
    return (layer.reshape(frames, height, columns, width), grad)


def solution(mesh):
    split = Mesh(mesh.devices.reshape(4, 2, 4, 4, 2), ALL)
    rows = P(ALL, None)
    blocks = P(ALL, None, None, None)
    placed = (blocks, P(), P(), P(), P(), rows, rows, P(), P(), blocks)
    return jax.shard_map(
        shards,
        mesh=split,
        in_specs=placed,
        out_specs=(blocks, rows),
        check_vma=False,
    )
```

time: 133 us -> 159 us (1.20)
  blocking collectives: 31 us -> 0 us
  waiting for transfers between devices: 21.9 us -> 46.8 us
  starting transfers between devices: 35.5 us -> 52.6 us
  other arithmetic: 2.69 us -> 8.4 us
  Pallas kernels: 13.5 us -> 17.5 us
  matrix products: 15.6 us -> 19 us
  local copies, waits for them, and re-layouts: 10.2 us -> 12.4 us
    all_to_all x3 -> x0, blocking collectives: 31 us -> none  [the longest x2 21.8 us: exchange(): return lax.all_to_all(parts, axes, 0, 0, tiled=True)]
    all_to_all x4 -> x7, waiting for transfers between devices: 15.6 us -> 35.6 us  [exchange(): return lax.all_to_all(parts, axes, 0, 0, tiled=True)]
    all_to_all x4 -> x7, starting transfers between devices: 27.6 us -> 39.5 us  [exchange(): return lax.all_to_all(parts, axes, 0, 0, tiled=True)]
    all_to_all x1 -> x2, waiting for transfers between devices: 6.32 us -> 11.2 us  [the longest x1 5.84 us: shards(): lax.all_to_all(back, CLIP, split_axis=0, concat_axis=1, tiled=True)]
    all_to_all x1 -> x2, starting transfers between devices: 4.32 us -> 8.51 us  [the longest x1 4.83 us: shards(): cots = lax.all_to_all(sent, CLIP, split_axis=1, concat_axis=0, tiled=True)]
    pallas_call x0 -> x1, Pallas kernels: none -> 3.97 us  [local_maps(): pl.pallas_call(maps_kernel, grid_spec=pltpu.PrefetchScalarGridSpec(num_sc...]
    dot_general x32, matrix products: 5.99 us -> 9.86 us  [nn(): lax.dot_general(a, b, (((1,), (0,)), ((), ())), preferred_element_type=f3...]
    dot_general x6 -> x2, matrix products: 6.32 us -> 3.29 us  [the longest x1 2.84 us: shards(): jnp.einsum('fqk,fqd->fkd', rounded, up, preferred_element_type=f32)]
  transfers between devices with their start and end apart: 6 -> 10, of which waited for: 3 -> 8; matrix products, arithmetic and copies ran while one was open for 11% -> 10% of each run, Pallas kernels for 10% -> 11%
where the time goes in v2:
time: 159 us; the launch traced here: 158 us
  starting transfers between devices  52.6 us (33%)
  waiting for transfers between devices  46.8 us (29%)
  matrix products  19 us (12%)
  Pallas kernels  17.5 us (11%)
  local copies, waits for them, and re-layouts  12.4 us (8%)
  other arithmetic  8.4 us (5%)
    all_to_all x7, starting transfers between devices, exchange(): return lax.all_to_all(parts, axes, 0, 0, tiled=True)  39.5 us
    all_to_all x7, waiting for transfers between devices, exchange(): return lax.all_to_all(parts, axes, 0, 0, tiled=True)  35.6 us
    dot_general x32, matrix products, nn(): lax.dot_general(a, b, (((1,), (0,)), ((), ())), preferred_element_type=f3...  9.86 us
    pallas_call x1, Pallas kernels, output_rows(): pl.pallas_call(output_kernel, grid=(width // block,), in_specs=[full, ful...  6.84 us
    pallas_call x1, Pallas kernels, products(): pl.pallas_call(products_kernel, grid=(width // block,), in_specs=[row(hea...  6.73 us
    all_to_all x1, waiting for transfers between devices, shards(): lax.all_to_all(back, CLIP, split_axis=0, concat_axis=1, tiled=True)  5.84 us
    all_to_all x1, waiting for transfers between devices, shards(): cots = lax.all_to_all(sent, CLIP, split_axis=1, concat_axis=0, tiled=True)  5.32 us
    all_to_all x1, starting transfers between devices, shards(): cots = lax.all_to_all(sent, CLIP, split_axis=1, concat_axis=0, tiled=True)  4.83 us
  transfers between devices with their start and end apart: 10, of which 8 were waited for; matrix products, arithmetic and copies ran while one was open for 10% of the time, Pallas kernels for 11%

profile of v2, /device:TPU:1, one launch (start us, length us, event | category | flops | bytes accessed | tf_op | source)
XLA Modules:
  0.0 158.0 jit_solution(7533113711522328731)
XLA Ops:
  0.6 4.6 %collective-permute-start = (bf16[2,4,40,128]{3,2,1,0:T(8,128)(2,1)}, bf16[2,4,40,128]{3,2,1,0:T(8,128)(2,1)S(1)}, u32[]{:S(2)}, u32[]{:S(2)}) collective-permute-start(bf16[2,4,40,128]{3,2,1,0:T(8,128)(2,1)} %param.10), channel_id=1, source_target_pairs={{0,1},{1,2},{2,3},{3,4},{4,5},{5,6},{6,7},{7,8},{8,9},{9,10},{10,1... | collective-permute-start | bytes 245768 | tf_op jit(solution)/shard_map/ppermute | solution.py:220
  5.8 4.0 %local_maps.1 = (bf16[1280,128]{1,0:T(8,128)(2,1)}, bf16[20,128]{1,0:T(8,128)(2,1)}, f32[20,384]{1,0:T(8,128)}) custom-call(s32[2]{0:T(128)} %pad_add_fusion.at_ref, bf16[20,384]{1,0:T(8,128)(2,1)} %ws_ref.1, bf16[20,384]{1,0:T(8,128)(2,1)} %wt_ref.1, bf16[128,5120]{1,0:T(8,128)(2,1)} %e_ref.5, bf16[128,5120]{1,0:T(8,128)(2,1)} %os_ref.5, ...), custom_call_target="tpu_custom_call" | custom-call | tf_op jit(solution)/shard_map/local_maps/pallas_call | solution.py:157
  9.8 7.0 %all-to-all-start.1 = ((bf16[32,40,128]{2,1,0:T(8,128)(2,1)}), bf16[32,40,128]{2,1,0:T(8,128)(2,1)S(1)}, u32[]{:S(2)}, u32[]{:S(2)}) async-start(bf16[32,40,128]{2,1,0:T(8,128)(2,1)} %bitcast.216), calls=%async_computation.1 | async-start | bytes 655360 | tf_op jit(solution)/shard_map/all_to_all | solution.py:36
  16.8 6.7 %products.1 = (f32[256,256]{1,0:T(8,128)}, f32[320,128]{1,0:T(8,128)}, f32[320,128]{1,0:T(8,128)}) custom-call(bf16[128,5120]{1,0:T(8,128)(2,1)} %e_ref.5, bf16[128,5120]{1,0:T(8,128)(2,1)} %os_ref.5, bf16[128,5120]{1,0:T(8,128)(2,1)} %ot_ref.3, bf16[320,5120]{1,0:T(8,128)(2,1)} %bitcast.197), custom_call_target="tpu_custom_call" | custom-call | tf_op jit(solution)/shard_map/products/pallas_call | solution.py:87
  23.5 1.0 convert.32
  24.6 0.9 convert.33
  25.6 0.8 pad_maximum_fusion.2
  26.8 0.8 copy-done.3
  31.6 4.8 %all-to-all-start.5 = ((bf16[2,160,256]{2,0,1:T(2,128)(2,1)}), bf16[2,160,256]{2,0,1:T(2,128)(2,1)S(1)}, u32[]{:S(2)}, u32[]{:S(2)}) async-start(bf16[2,160,256]{2,0,1:T(2,128)(2,1)} %pad_maximum_fusion.2), calls=%async_computation.5 | async-start | bytes 327680 | tf_op jit(solution)/shard_map/all_to_all | solution.py:238
  36.7 5.3 %all-to-all-done.5 = bf16[2,160,256]{2,0,1:T(2,128)(2,1)S(1)} async-done(((bf16[2,160,256]{2,0,1:T(2,128)(2,1)}), bf16[2,160,256]{2,0,1:T(2,128)(2,1)S(1)}, u32[]{:S(2)}, u32[]{:S(2)}) %all-to-all-start.5) | async-done | bytes 163872 | tf_op jit(solution)/shard_map/all_to_all | solution.py:238
  42.6 8.1 %all-to-all-start.2 = ((bf16[8,40,128]{2,1,0:T(8,128)(2,1)}), bf16[8,40,128]{2,1,0:T(8,128)(2,1)S(1)}, u32[]{:S(2)}, u32[]{:S(2)}) async-start(bf16[8,40,128]{2,1,0:T(8,128)(2,1)} %broadcast_in_dim.32), calls=%async_computation.2 | async-start | bytes 163840 | tf_op jit(solution)/shard_map/all_to_all | solution.py:36
  50.9 7.2 %all-to-all-done.2 = bf16[8,40,128]{2,1,0:T(8,128)(2,1)S(1)} async-done(((bf16[8,40,128]{2,1,0:T(8,128)(2,1)}), bf16[8,40,128]{2,1,0:T(8,128)(2,1)S(1)}, u32[]{:S(2)}, u32[]{:S(2)}) %all-to-all-start.2) | async-done | bytes 81952 | tf_op jit(solution)/shard_map/all_to_all | solution.py:36
  58.1 0.9 broadcast_in_dim.16
  59.0 5.8 %all-to-all-start = ((bf16[8,320,128]{2,1,0:T(8,128)(2,1)}), bf16[8,320,128]{2,1,0:T(8,128)(2,1)S(1)}, u32[]{:S(2)}, u32[]{:S(2)}) async-start(bf16[8,320,128]{2,1,0:T(8,128)(2,1)} %broadcast_in_dim.16), calls=%async_computation | async-start | bytes 1310720 | tf_op jit(solution)/shard_map/all_to_all | solution.py:36
  66.4 9.2 %all-to-all-done = bf16[8,320,128]{2,1,0:T(8,128)(2,1)S(1)} async-done(((bf16[8,320,128]{2,1,0:T(8,128)(2,1)}), bf16[8,320,128]{2,1,0:T(8,128)(2,1)S(1)}, u32[]{:S(2)}, u32[]{:S(2)}) %all-to-all-start) | async-done | bytes 655392 | tf_op jit(solution)/shard_map/all_to_all | solution.py:36
  76.4 6.0 %all-to-all-start.3 = ((bf16[32,40,128]{2,1,0:T(8,128)(2,1)}), bf16[32,40,128]{2,1,0:T(8,128)(2,1)S(1)}, u32[]{:S(2)}, u32[]{:S(2)}) async-start(bf16[32,40,128]{2,1,0:T(8,128)(2,1)} %broadcast_in_dim.33), calls=%async_computation.3 | async-start | bytes 655360 | tf_op jit(solution)/shard_map/all_to_all | solution.py:36
  85.6 6.4 %all-to-all-done.3 = bf16[32,40,128]{2,1,0:T(8,128)(2,1)S(1)} async-done(((bf16[32,40,128]{2,1,0:T(8,128)(2,1)}), bf16[32,40,128]{2,1,0:T(8,128)(2,1)S(1)}, u32[]{:S(2)}, u32[]{:S(2)}) %all-to-all-start.3) | async-done | bytes 327712 | tf_op jit(solution)/shard_map/all_to_all | solution.py:36
  93.4 0.9 fusion.123
  95.7 1.5 multiply_reduce_fusion.3
  99.8 1.8 %fusion.7 = f32[320,128]{1,0:T(8,128)} fusion(f32[320,256]{1,0:T(8,128)S(1)} %get-tuple-element.44, bf16[320,128]{1,0:T(8,128)(2,1)S(1)} %convolution_convert_fusion.2, bf16[320,128]{1,0:T(8,128)(2,1)S(1)} %fusion.11, bf16[320,128]{1,0:T(8,128)(2,1)S(1)} %fusion.10, bf16[1280,128]{1,0:T(8,128)(2,1)} %bitcast.208, f32[320]{0:T(512)S(1)} %fusion.112, ...), kind=kOutput, calls=%fused_computation.17 | convolution fusion | flops 32317440 | bytes 674304 | tf_op jit(solution)/shard_map/dot_general | solution.py:32
  101.6 1.0 reshape.264
  102.6 1.6 fusion.33
  104.1 2.8 %convolution_convert_fusion = bf16[16,160,128]{2,1,0:T(8,128)(2,1)} fusion(bf16[16,20,128]{2,0,1:T(8,128)(2,1)} %fusion.33, f32[16,20]{1,0:T(8,128)S(1)} %get-tuple-element.41, f32[16,20,160]{2,1,0:T(8,128)S(1)} %convolution_multiply_fusion.4), kind=kOutput, calls=%fused_computation.5 | convolution fusion | flops 13588959 | bytes 943360 | tf_op jit(solution)/shard_map/fqk,fqd->fkd/dot_general | solution.py:284
  111.2 3.8 %all-to-all-start.6 = ((bf16[32,16,128]{2,1,0:T(8,128)(2,1)}), bf16[32,16,128]{2,1,0:T(8,128)(2,1)S(1)}, u32[]{:S(2)}, u32[]{:S(2)}) async-start(bf16[32,16,128]{2,1,0:T(8,128)(2,1)} %bitcast.75), calls=%async_computation.6 | async-start | bytes 262144 | tf_op jit(solution)/shard_map/all_to_all | solution.py:36
  114.9 1.2 convolution_convert_fusion.3
  116.9 5.9 %all-to-all-done.6 = bf16[32,16,128]{2,1,0:T(8,128)(2,1)S(1)} async-done(((bf16[32,16,128]{2,1,0:T(8,128)(2,1)}), bf16[32,16,128]{2,1,0:T(8,128)(2,1)S(1)}, u32[]{:S(2)}, u32[]{:S(2)}) %all-to-all-start.6) | async-done | bytes 131104 | tf_op jit(solution)/shard_map/all_to_all | solution.py:36
  122.7 3.7 %all-to-all-start.4 = ((bf16[16,20,256]{2,1,0:T(8,128)(2,1)}), bf16[16,20,256]{2,1,0:T(8,128)(2,1)S(1)}, u32[]{:S(2)}, u32[]{:S(2)}) async-start(bf16[16,20,256]{2,1,0:T(8,128)(2,1)} %pad_maximum_fusion.1), calls=%async_computation.4 | async-start | bytes 393216 | tf_op jit(solution)/shard_map/all_to_all | solution.py:301
  126.4 5.8 %all-to-all-done.4 = bf16[16,20,256]{2,1,0:T(8,128)(2,1)S(1)} async-done(((bf16[16,20,256]{2,1,0:T(8,128)(2,1)}), bf16[16,20,256]{2,1,0:T(8,128)(2,1)S(1)}, u32[]{:S(2)}, u32[]{:S(2)}) %all-to-all-start.4) | async-done | bytes 163872 | tf_op jit(solution)/shard_map/all_to_all | solution.py:301
  132.9 3.3 %all-to-all-start.7 = ((bf16[8,16,128]{2,1,0:T(8,128)(2,1)}), bf16[8,16,128]{2,1,0:T(8,128)(2,1)S(1)}, u32[]{:S(2)}, u32[]{:S(2)}) async-start(bf16[8,16,128]{2,1,0:T(8,128)(2,1)} %broadcast_in_dim.36), calls=%async_computation.7 | async-start | bytes 65536 | tf_op jit(solution)/shard_map/all_to_all | solution.py:36
  136.3 6.7 %all-to-all-done.7 = bf16[8,16,128]{2,1,0:T(8,128)(2,1)S(1)} async-done(((bf16[8,16,128]{2,1,0:T(8,128)(2,1)}), bf16[8,16,128]{2,1,0:T(8,128)(2,1)S(1)}, u32[]{:S(2)}, u32[]{:S(2)}) %all-to-all-start.7) | async-done | bytes 32800 | tf_op jit(solution)/shard_map/all_to_all | solution.py:36
  143.7 5.6 %all-to-all-start.8 = ((bf16[32,16,128]{2,1,0:T(8,128)(2,1)}), bf16[32,16,128]{2,1,0:T(8,128)(2,1)S(1)}, u32[]{:S(2)}, u32[]{:S(2)}) async-start(bf16[32,16,128]{2,1,0:T(8,128)(2,1)} %broadcast_in_dim.37), calls=%async_computation.8 | async-start | bytes 262144 | tf_op jit(solution)/shard_map/all_to_all | solution.py:36
  150.0 6.8 %output_rows.1 = bf16[320,5120]{1,0:T(8,128)(2,1)} custom-call(bf16[320,128]{1,0:T(8,128)(2,1)} %copy-done.11, bf16[320,128]{1,0:T(8,128)(2,1)} %get-tuple-element.15.m_ref, bf16[320,128]{1,0:T(8,128)(2,1)} %get-tuple-element.14.t_ref, bf16[128,5120]{1,0:T(8,128)(2,1)} %e_ref.5, bf16[128,5120]{1,0:T(8,128)(2,1)} %os_ref.5, bf16[128,5120]{1,0:T(8,128)(2,1)} %ot_ref.3), custom_call_target="tpu_custom_call" | custom-call | tf_op jit(solution)/shard_map/output_rows/pallas_call | solution.py:112
  (138 shorter events, 24.9 us)
Async XLA Ops:
  0.6 25.8 %collective-permute-start = (bf16[2,4,40,128]{3,2,1,0:T(8,128)(2,1)}, bf16[2,4,40,128]{3,2,1,0:T(8,128)(2,1)S(1)}, u32[]{:S(2)}, u32[]{:S(2)}) collective-permute-start(bf16[2,4,40,128]{3,2,1,0:T(8,128)(2,1)} %param.10), channel_id=1, source_target_pairs={{0,1},{1,2},{2,3},{3,4},{4,5},{5,6},{6,7},{7,8},{8,9},{9,10},{10,1... | collective-permute-start | bytes 245768 | tf_op jit(solution)/shard_map/ppermute | solution.py:220
  9.8 21.8 %all-to-all-start.1 = ((bf16[32,40,128]{2,1,0:T(8,128)(2,1)}), bf16[32,40,128]{2,1,0:T(8,128)(2,1)S(1)}, u32[]{:S(2)}, u32[]{:S(2)}) async-start(bf16[32,40,128]{2,1,0:T(8,128)(2,1)} %bitcast.216), calls=%async_computation.1 | async-start | bytes 655360 | tf_op jit(solution)/shard_map/all_to_all | solution.py:36
  23.5 2.9 %copy-start.12 = (bf16[2,4,40,128]{3,2,1,0:T(8,128)(2,1)S(1)}, bf16[2,4,40,128]{3,2,1,0:T(8,128)(2,1)}, u32[]{:S(2)}) copy-start(bf16[2,4,40,128]{3,2,1,0:T(8,128)(2,1)} %param.10) | copy-start | bytes 245764
  26.4 1.2 copy-start.3
  31.6 10.4 %all-to-all-start.5 = ((bf16[2,160,256]{2,0,1:T(2,128)(2,1)}), bf16[2,160,256]{2,0,1:T(2,128)(2,1)S(1)}, u32[]{:S(2)}, u32[]{:S(2)}) async-start(bf16[2,160,256]{2,0,1:T(2,128)(2,1)} %pad_maximum_fusion.2), calls=%async_computation.5 | async-start | bytes 327680 | tf_op jit(solution)/shard_map/all_to_all | solution.py:238
  42.6 15.5 %all-to-all-start.2 = ((bf16[8,40,128]{2,1,0:T(8,128)(2,1)}), bf16[8,40,128]{2,1,0:T(8,128)(2,1)S(1)}, u32[]{:S(2)}, u32[]{:S(2)}) async-start(bf16[8,40,128]{2,1,0:T(8,128)(2,1)} %broadcast_in_dim.32), calls=%async_computation.2 | async-start | bytes 163840 | tf_op jit(solution)/shard_map/all_to_all | solution.py:36
  50.7 14.7 %copy-start.2 = (f32[256,256]{1,0:T(8,128)S(1)}, f32[256,256]{1,0:T(8,128)}, u32[]{:S(2)}) copy-start(f32[256,256]{1,0:T(8,128)} %get-tuple-element.9) | copy-start | bytes 786436
  50.9 14.5 %copy-start.11 = (bf16[320,128]{1,0:T(8,128)(2,1)}, bf16[320,128]{1,0:T(8,128)(2,1)S(1)}, u32[]{:S(2)}) copy-start(bf16[320,128]{1,0:T(8,128)(2,1)S(1)} %fusion.32.f_ref) | copy-start | bytes 245764
  59.0 16.6 %all-to-all-start = ((bf16[8,320,128]{2,1,0:T(8,128)(2,1)}), bf16[8,320,128]{2,1,0:T(8,128)(2,1)S(1)}, u32[]{:S(2)}, u32[]{:S(2)}) async-start(bf16[8,320,128]{2,1,0:T(8,128)(2,1)} %broadcast_in_dim.16), calls=%async_computation | async-start | bytes 1310720 | tf_op jit(solution)/shard_map/all_to_all | solution.py:36
  65.7 16.7 %copy-start.6 = (bf16[16,20,256]{2,0,1:T(8,128)(2,1)}, bf16[16,20,256]{2,0,1:T(8,128)(2,1)S(1)}, u32[]{:S(2)}) copy-start(bf16[16,20,256]{2,0,1:T(8,128)(2,1)S(1)} %all_to_all.55) | copy-start | bytes 491524
  76.4 15.6 %all-to-all-start.3 = ((bf16[32,40,128]{2,1,0:T(8,128)(2,1)}), bf16[32,40,128]{2,1,0:T(8,128)(2,1)S(1)}, u32[]{:S(2)}, u32[]{:S(2)}) async-start(bf16[32,40,128]{2,1,0:T(8,128)(2,1)} %broadcast_in_dim.33), calls=%async_computation.3 | async-start | bytes 655360 | tf_op jit(solution)/shard_map/all_to_all | solution.py:36
  83.8 0.7 copy-start.7
  92.0 5.3 %copy-start.1 = (bf16[32,40,128]{2,1,0:T(8,128)(2,1)}, bf16[32,40,128]{2,1,0:T(8,128)(2,1)S(1)}, u32[]{:S(2)}) copy-start(bf16[32,40,128]{2,1,0:T(8,128)(2,1)S(1)} %all-to-all-done.3) | copy-start | bytes 983044
  95.0 2.8 %copy-start.9 = (bf16[16,20,128]{2,1,0:T(8,128)(2,1)}, bf16[16,20,128]{2,1,0:T(8,128)(2,1)S(1)}, u32[]{:S(2)}) copy-start(bf16[16,20,128]{2,1,0:T(8,128)(2,1)S(1)} %convolution_convert_fusion.1) | copy-start | bytes 245764
  97.5 1.6 %copy-start.4 = (bf16[320,384]{1,0:T(8,128)(2,1)}, bf16[320,384]{1,0:T(8,128)(2,1)S(1)}, u32[]{:S(2)}) copy-start(bf16[320,384]{1,0:T(8,128)(2,1)S(1)} %get-tuple-element.45) | copy-start | bytes 737284
  97.5 1.0 copy-start.13
  101.6 5.4 %copy-start = (f32[16,20,160]{2,1,0:T(8,128)S(1)}, f32[16,20,160]{2,1,0:T(8,128)}, u32[]{:S(2)}) copy-start(f32[16,20,160]{2,1,0:T(8,128)} %get-tuple-element.42) | copy-start | bytes 614404
  104.1 2.8 %copy-start.14 = (bf16[16,20,128]{2,0,1:T(8,128)(2,1)S(1)}, bf16[16,20,128]{2,0,1:T(8,128)(2,1)}, u32[]{:S(2)}) copy-start(bf16[16,20,128]{2,0,1:T(8,128)(2,1)} %fusion.33) | copy-start | bytes 245764
  107.5 0.9 copy-start.8
  107.5 0.9 copy-start.16
  108.9 1.1 copy-start.5
  108.9 1.5 copy-start.18
  111.2 5.0 %copy-start.10 = (bf16[16,20,128]{2,1,0:T(8,128)(2,1)S(1)}, bf16[16,20,128]{2,1,0:T(8,128)(2,1)}, u32[]{:S(2)}) copy-start(bf16[16,20,128]{2,1,0:T(8,128)(2,1)} %copy-done.9) | copy-start | bytes 245764
  111.2 11.6 %all-to-all-start.6 = ((bf16[32,16,128]{2,1,0:T(8,128)(2,1)}), bf16[32,16,128]{2,1,0:T(8,128)(2,1)S(1)}, u32[]{:S(2)}, u32[]{:S(2)}) async-start(bf16[32,16,128]{2,1,0:T(8,128)(2,1)} %bitcast.75), calls=%async_computation.6 | async-start | bytes 262144 | tf_op jit(solution)/shard_map/all_to_all | solution.py:36
  122.7 9.6 %all-to-all-start.4 = ((bf16[16,20,256]{2,1,0:T(8,128)(2,1)}), bf16[16,20,256]{2,1,0:T(8,128)(2,1)S(1)}, u32[]{:S(2)}, u32[]{:S(2)}) async-start(bf16[16,20,256]{2,1,0:T(8,128)(2,1)} %pad_maximum_fusion.1), calls=%async_computation.4 | async-start | bytes 393216 | tf_op jit(solution)/shard_map/all_to_all | solution.py:301
  132.9 10.1 %all-to-all-start.7 = ((bf16[8,16,128]{2,1,0:T(8,128)(2,1)}), bf16[8,16,128]{2,1,0:T(8,128)(2,1)S(1)}, u32[]{:S(2)}, u32[]{:S(2)}) async-start(bf16[8,16,128]{2,1,0:T(8,128)(2,1)} %broadcast_in_dim.36), calls=%async_computation.7 | async-start | bytes 65536 | tf_op jit(solution)/shard_map/all_to_all | solution.py:36
  143.7 13.4 %all-to-all-start.8 = ((bf16[32,16,128]{2,1,0:T(8,128)(2,1)}), bf16[32,16,128]{2,1,0:T(8,128)(2,1)S(1)}, u32[]{:S(2)}, u32[]{:S(2)}) async-start(bf16[32,16,128]{2,1,0:T(8,128)(2,1)} %broadcast_in_dim.37), calls=%async_computation.8 | async-start | bytes 262144 | tf_op jit(solution)/shard_map/all_to_all | solution.py:36
  150.0 7.1 %copy-start.15 = (f32[20,384]{1,0:T(8,128)S(1)}, f32[20,384]{1,0:T(8,128)}, u32[]{:S(2)}) copy-start(f32[20,384]{1,0:T(8,128)} %get-tuple-element.13) | copy-start | bytes 92164
  150.0 7.1 %copy-start.17 = (bf16[20,128]{1,0:T(8,128)(2,1)S(1)}, bf16[20,128]{1,0:T(8,128)(2,1)}, u32[]{:S(2)}) copy-start(bf16[20,128]{1,0:T(8,128)(2,1)} %get-tuple-element.10) | copy-start | bytes 15364

commit v3 on v2

--- a/solution.py
+++ b/solution.py
@@ -44,7 +44,7 @@
 
 
 def conv_local(volume, weight, count):
-    frames, height, columns, channels = volume.shape
+    _, height, columns, channels = volume.shape
     out_channels = weight.shape[-1]
     padded = jnp.pad(volume, ((0, 0), (1, 1), (1, 1), (0, 0)))
     summed = jnp.zeros((count * height * columns, out_channels), f32)
@@ -63,7 +63,7 @@
     return summed
 
 
-def products_kernel(e_ref, os_ref, ot_ref, cot_ref, gram_ref, cots_ref, cott_ref):
+def products_kernel(after_ref, e_ref, os_ref, ot_ref, cot_ref, gram_ref, cots_ref, cott_ref):
     @pl.when(pl.program_id(0) == 0)
     def _():
         gram_ref[...] = jnp.zeros_like(gram_ref)
@@ -77,7 +77,7 @@
     cott_ref[...] += nt(c, t)
 
 
-def products(embed, out_s, out_t, cot):
+def products(after, embed, out_s, out_t, cot):
     width = embed.shape[1]
     head = embed.shape[0]
     tokens = cot.shape[0]
@@ -87,7 +87,7 @@
     return pl.pallas_call(
         products_kernel,
         grid=(width // block,),
-        in_specs=[row(head), row(head), row(head), row(tokens)],
+        in_specs=[full(*after.shape), row(head), row(head), row(head), row(tokens)],
         out_specs=[full(2 * head, 2 * head), full(tokens, head), full(tokens, head)],
         out_shape=[
             jax.ShapeDtypeStruct((2 * head, 2 * head), f32),
@@ -95,7 +95,7 @@
             jax.ShapeDtypeStruct((tokens, head), f32),
         ],
         name="products",
-    )(embed, out_s, out_t, cot)
+    )(after, embed, out_s, out_t, cot)
 
 
 def output_kernel(f_ref, m_ref, t_ref, e_ref, os_ref, ot_ref, out_ref):
@@ -178,18 +178,154 @@
     return size
 
 
-def summed_everywhere(value):
+def scattered(value):
     n = group_size(PLANE)
     parts = exchange(value.reshape(n, value.shape[0] // n, value.shape[1]), PLANE)
+    return parts.astype(f32).sum(axis=0).astype(bf16)
+
+
+def gathered(mine, shape):
+    parts = to_all(mine, LINE)
     mine = parts.astype(f32).sum(axis=0).astype(bf16)
-    mine = to_all(mine, LINE).astype(f32).sum(axis=0).astype(bf16)
-    return to_all(mine, PLANE).reshape(value.shape)
+    return to_all(mine, PLANE).reshape(shape)
 
 
 def softmax_rows(scores):
     top = jnp.max(scores, axis=-1, keepdims=True)
     raised = jnp.exp(scores - top)
     return raised / jnp.sum(raised, axis=-1, keepdims=True)
+
+
+def attend_kernel(
+    at_ref, flat_ref, scaled_ref, gram_ref, cots_ref, maps_ref,
+    total_ref, mix_ref, mix_t_ref, qkv_ref, att_ref, dkv_ref, up_ref, score_ref, rounded_ref, slope_ref,
+):
+    frames = FR
+    head = flat_ref.shape[1]
+    places = flat_ref.shape[0] // frames
+    pad = mix_ref.shape[0] // frames
+    triple = 3 * head
+    own = frames * pad
+    scale = head**-0.5
+    line, core, slot, spots = at_ref[0], at_ref[1], at_ref[2], at_ref[3]
+
+    qkv_ref[...] = nt(scaled_ref[...], maps_ref[:triple]).astype(bf16)
+    r = lax.broadcasted_iota(jnp.int32, (pad, places), 0)
+    c = lax.broadcasted_iota(jnp.int32, (pad, places), 1)
+    pick = jnp.where((c == r + slot) & (r < spots), 1.0, 0.0).astype(bf16)
+
+    feats_own, scaled_own, queries = [], [], []
+    for f in range(frames):
+        here = slice(f * places, (f + 1) * places)
+        both = jnp.concatenate([flat_ref[here], scaled_ref[here], qkv_ref[here, :head]], axis=1)
+        got = nn(pick, both).astype(bf16)
+        feats_own.append(got[:, :head])
+        scaled_own.append(got[:, head : 2 * head])
+        queries.append(got[:, 2 * head :])
+    for f in range(frames):
+        here = slice(f * places, (f + 1) * places)
+        score_ref[f * pad : (f + 1) * pad] = nt(queries[f], qkv_ref[here, head : 2 * head])
+    att = softmax_rows(score_ref[...] * scale)
+    att_ref[...] = att
+    rounded_ref[...] = att.astype(bf16)
+    for f in range(frames):
+        here = slice(f * places, (f + 1) * places)
+        mine = slice(f * pad, (f + 1) * pad)
+        mix_ref[mine] = nn(rounded_ref[mine], qkv_ref[here, 2 * head :]).astype(bf16)
+
+    feats = jnp.concatenate(feats_own, axis=0)
+    mix = mix_ref[...]
+    x = jnp.concatenate([feats, mix], axis=1)
+    gram = gram_ref[...]
+    first = gram.astype(bf16)
+    rest = gram - first.astype(f32)
+    second = rest.astype(bf16)
+    third = (rest - second.astype(f32)).astype(bf16)
+    xg = nn(x, first) + (nn(x, second) + nn(x, third))
+    factor = lax.rsqrt(jnp.sum(xg * x.astype(f32), axis=-1, keepdims=True) + epsilon)
+    map_to = maps_ref[2 * triple : 3 * triple]
+    raw = nt(feats, maps_ref[triple : 2 * triple]) + nt(mix, map_to)
+    packed = (raw * factor).astype(bf16)
+    q, k, v = packed[:, :head], packed[:, head : 2 * head], packed[:, 2 * head :]
+    g = jnp.concatenate([cots_ref[i, j, 1] for i in range(2) for j in range(4)], axis=0)
+
+    def spot_frame(shape, dim):
+        i = lax.broadcasted_iota(jnp.int32, shape, dim)
+        f = i // pad
+        other = f // 8
+        step = (f // 2) % 4
+        number = ((line + 4 - step) % 4) * 4 + (core + other - 2 * core * other) * 2 + f % 2
+        return i % pad, number
+
+    row_spot, row_frame = spot_frame((own, 1), 0)
+    col_spot, col_frame = spot_frame((1, own), 1)
+    allowed = (row_spot == col_spot) & (row_frame >= col_frame)
+    att = softmax_rows(jnp.where(allowed, nt(q, k) * scale, masked))
+    rounded = att.astype(bf16)
+    mix_t_ref[...] = nn(rounded, v).astype(bf16)
+    d_att = nt(g, v)
+    d_sc = (att * (d_att - jnp.sum(d_att * att, axis=-1, keepdims=True))).astype(bf16)
+    d_packed = jnp.concatenate(
+        [nn(d_sc, k) * scale, tn(d_sc, q) * scale, tn(rounded, g)], axis=1
+    ).astype(bf16)
+    inner = jnp.sum(d_packed.astype(f32) * raw, axis=-1, keepdims=True)
+    corr = factor * nn(d_packed, map_to) - (factor * factor * factor * inner) * xg[:, head:]
+    cot = jnp.concatenate([cots_ref[i, j, 0] for i in range(2) for j in range(4)], axis=0)
+    up_ref[...] = (cot.astype(f32) + corr).astype(bf16)
+
+    for f in range(frames):
+        here = slice(f * places, (f + 1) * places)
+        mine = slice(f * pad, (f + 1) * pad)
+        score_ref[mine] = nt(up_ref[mine], qkv_ref[here, 2 * head :])
+        dkv_ref[here, head:] = tn(rounded_ref[mine], up_ref[mine]).astype(bf16)
+    att = att_ref[...]
+    d_att = score_ref[...]
+    slope_ref[...] = (att * (d_att - jnp.sum(d_att * att, axis=-1, keepdims=True)) * scale).astype(bf16)
+    d_queries = []
+    for f in range(frames):
+        here = slice(f * places, (f + 1) * places)
+        mine = slice(f * pad, (f + 1) * pad)
+        slope = slope_ref[mine]
+        d_queries.append(nn(slope, qkv_ref[here, head : 2 * head]).astype(bf16))
+        dkv_ref[here, :head] = tn(slope, queries[f]).astype(bf16)
+    by_query = tn(jnp.concatenate(scaled_own, axis=0), jnp.concatenate(d_queries, axis=0))
+    by_key = tn(scaled_ref[...], dkv_ref[...])
+    total_ref[:head] = by_query.astype(bf16)
+    total_ref[head : 2 * head] = by_key[:, :head].astype(bf16)
+    total_ref[2 * head : 3 * head] = by_key[:, head:].astype(bf16)
+    total_ref[3 * head :] = jnp.zeros((total_ref.shape[0] - 3 * head, head), bf16)
+
+
+def attend_all(at, flat, scaled, gram, cots, maps, pad):
+    rows, head = flat.shape
+    places = rows // FR
+    own = FR * pad
+    vmem = pl.BlockSpec(memory_space=pltpu.VMEM)
+    return pl.pallas_call(
+        attend_kernel,
+        in_specs=[pl.BlockSpec(memory_space=pltpu.SMEM)] + [vmem] * 5,
+        out_specs=[vmem] * 3,
+        out_shape=[
+            jax.ShapeDtypeStruct((4 * head, head), bf16),
+            jax.ShapeDtypeStruct((own, head), bf16),
+            jax.ShapeDtypeStruct((own, head), bf16),
+        ],
+        scratch_shapes=[
+            pltpu.VMEM((rows, 3 * head), bf16),
+            pltpu.VMEM((own, places), f32),
+            pltpu.VMEM((rows, 2 * head), bf16),
+            pltpu.VMEM((own, head), bf16),
+            pltpu.VMEM((own, places), f32),
+            pltpu.VMEM((own, places), bf16),
+            pltpu.VMEM((own, places), bf16),
+        ],
+        name="attend_all",
+    )(at, flat, scaled, gram, cots, maps)
+
+
+def turned(value, axis, step):
+    n = lax.axis_size(axis)
+    return lax.ppermute(value, axis, [(i, (i + step) % n) for i in range(n)])
 
 
 def shards(
@@ -204,18 +340,15 @@
     output_temporal,
     cotangent,
 ):
-    frames, height, columns, channels = clip_video.shape
+    frames, height, columns, _ = clip_video.shape
     places = height * columns
     tokens = frames * places
     head, width = embed_weight.shape
-    triple = 3 * head
-    scale = head**-0.5
     exact = dict(precision=lax.Precision.HIGHEST)
     n_ts = group_size(TS)
     n_clip = group_size(CLIP)
     spots = places // n_clip
     clip_tokens = FR * places
-    own = FR * spots
 
     prior = lax.ppermute(clip_video, TS, [(i, i + 1) for i in range(n_ts - 1)])
 
@@ -223,82 +356,61 @@
     maps, e_mine, g_mine = local_maps(
         at, input_spatial, input_temporal, embed_weight, output_spatial, gain_spatial, gain_temporal, 10 * head
     )
-    maps = summed_everywhere(maps)
-    map_s = maps[:triple]
-    map_te = maps[triple : 2 * triple]
-    map_to = maps[2 * triple : 3 * triple]
+    prior, g_mine = lax.optimization_barrier((prior, g_mine))
+    maps = gathered(scattered(maps), maps.shape)
 
     volume = jnp.concatenate([prior, clip_video], axis=0)
     feats_home = jax.nn.gelu(conv_local(volume, conv_weight, frames), approximate=True).astype(bf16)
-    feats = to_all(feats_home, CLIP).reshape(FR, places, head)
     gram, cot_s, cot_t = products(
-        embed_weight, output_spatial, output_temporal, cotangent.reshape(tokens, width)
+        g_mine, embed_weight, output_spatial, output_temporal, cotangent.reshape(tokens, width)
     )
-    sent = jnp.concatenate([cot_s, cot_t], axis=-1).astype(bf16).reshape(frames, places, 2 * head)
-    cots = lax.all_to_all(sent, CLIP, split_axis=1, concat_axis=0, tiled=True)
     gram = gram * (1.0 / width)
-    slot = lax.axis_index(CLIP) * spots
-    flat = feats.reshape(clip_tokens, head)
+    n_line = lax.axis_size("y")
+    line = lax.axis_index("y")
+    core = lax.axis_index("c")
+    pad = 32
+    cots = jnp.stack([cot_s, cot_t]).astype(bf16).reshape(2, frames, n_line, 2, spots, head)
+    cots = jnp.pad(cots, ((0, 0),) * 4 + ((0, pad - spots), (0, 0)))
+    cots = cots.transpose(2, 3, 0, 1, 4, 5).reshape(n_line, 4 * frames * pad, head)
+    held = [
+        jnp.concatenate(
+            [feats_home, lax.dynamic_index_in_dim(cots, (line + step) % n_line, 0, keepdims=False)], axis=0
+        )
+        for step in range(n_line)
+    ]
+    moved = []
+    for step in range(1, n_line):
+        moved.append(turned(held[step], "y", step))
+    held = jnp.stack([held[0]] + moved)
+    feats_near = held[:, :tokens]
+    cots_near = held[:, tokens:].reshape(n_line, 2, 2 * frames * pad, head)
+    keep = lax.dynamic_index_in_dim(cots_near, core, 1, keepdims=False)
+    give = lax.dynamic_index_in_dim(cots_near, 1 - core, 1, keepdims=False)
+    other = turned(jnp.concatenate([feats_near, give], axis=1), "c", 1)
+    flat = jnp.concatenate([feats_near, other[:, :tokens]], axis=0).reshape(clip_tokens, head)
+    cots = jnp.stack([keep, other[:, tokens:]]).reshape(2, n_line, 2, frames * pad, head)
     wide = flat.astype(f32)
     square = jnp.sum(nn(wide, gram[:head, :head], **exact) * wide, axis=-1, keepdims=True)
-    factor_one = lax.rsqrt(square + epsilon)
-    scaled = (wide * factor_one).astype(bf16)
-    feats_own = lax.dynamic_slice_in_dim(feats, slot, spots, 1).reshape(own, head)
-    scaled_own = lax.dynamic_slice_in_dim(scaled.reshape(FR, places, head), slot, spots, 1).reshape(own, head)
-    factor_own = lax.dynamic_slice_in_dim(factor_one.reshape(FR, places, 1), slot, spots, 1).reshape(own, 1)
-
-    q = (nt(feats_own, map_s[:head]) * factor_own).astype(bf16).reshape(FR, spots, head)
-    kv = (nt(flat, map_s[head:]) * factor_one).astype(bf16).reshape(FR, places, 2 * head)
-    k, v = kv[..., :head], kv[..., head:]
-    scores = jnp.einsum("fqd,fkd->fqk", q, k, preferred_element_type=f32) * scale
-    attend = softmax_rows(scores)
-    rounded = attend.astype(bf16)
-    mix = jnp.einsum("fqk,fkd->fqd", rounded, v, preferred_element_type=f32).astype(bf16)
-
-    mix_own = mix.reshape(own, head)
-    g = cots[..., head:].reshape(own, head)
-    x = jnp.concatenate([feats_own, mix_own], axis=-1)
-    xw = x.astype(f32)
-    xg = nn(xw, gram, **exact)
-    factor_two = lax.rsqrt(jnp.sum(xg * xw, axis=-1, keepdims=True) + epsilon)
-    raw = nt(feats_own, map_te) + nt(mix_own, map_to)
-    packed_t = (raw * factor_two).astype(bf16)
-    qt, kt, vt = packed_t[:, :head], packed_t[:, head : 2 * head], packed_t[:, 2 * head :]
-    row = lax.broadcasted_iota(jnp.int32, (own, own), 0)
-    col = lax.broadcasted_iota(jnp.int32, (own, own), 1)
-    allowed = (row >= col) & (row % spots == col % spots)
-    att_t = softmax_rows(jnp.where(allowed, nt(qt, kt) * scale, masked))
-    rnd_t = att_t.astype(bf16)
-    mix_t = nn(rnd_t, vt).astype(bf16)
-    d_att = nt(g, vt)
-    d_v = tn(rnd_t, g)
-    d_sc = (att_t * (d_att - jnp.sum(d_att * att_t, axis=-1, keepdims=True))).astype(bf16)
-    d_q = nn(d_sc, kt) * scale
-    d_k = tn(d_sc, qt) * scale
-    gpt = jnp.concatenate([d_q, d_k, d_v], axis=-1).astype(bf16)
-    inner = jnp.sum(gpt.astype(f32) * raw, axis=-1, keepdims=True)
-    corr = factor_two * nn(gpt, map_to) - (factor_two**3 * inner) * xg[:, head:]
-
-    up = (cots[..., :head].astype(f32) + corr.reshape(FR, spots, head)).astype(bf16)
-    d_att = jnp.einsum("fqd,fkd->fqk", up, v, preferred_element_type=f32)
-    d_v = jnp.einsum("fqk,fqd->fkd", rounded, up, preferred_element_type=f32).astype(bf16)
-    d_sc = (attend * (d_att - jnp.sum(d_att * attend, axis=-1, keepdims=True))).astype(bf16)
-    d_q = (jnp.einsum("fqk,fkd->fqd", d_sc, k, preferred_element_type=f32) * scale).astype(bf16)
-    d_k = (jnp.einsum("fqk,fqd->fkd", d_sc, q, preferred_element_type=f32) * scale).astype(bf16)
-    total = jnp.concatenate(
-        [
-            tn(d_q.reshape(own, head), scaled_own),
-            tn(d_k.reshape(clip_tokens, head), scaled),
-            tn(d_v.reshape(clip_tokens, head), scaled),
-            jnp.zeros((head, head), f32),
-        ],
-        axis=0,
-    ).astype(bf16)
-    total = summed_everywhere(total)[:triple]
-    grad = nt(e_mine, total) * g_mine
-
-    back = jnp.concatenate([mix, mix_t.reshape(FR, spots, head)], axis=-1)
-    home = lax.all_to_all(back, CLIP, split_axis=0, concat_axis=1, tiled=True).reshape(tokens, 2 * head)
+    scaled = (wide * lax.rsqrt(square + epsilon)).astype(bf16)
+
+    place = jnp.stack([line, core, lax.axis_index(CLIP) * spots, jnp.int32(spots)]).astype(jnp.int32)
+    total, mix, mix_t = attend_all(place, flat, scaled, gram, cots, maps, pad)
+
+    share = scattered(total)
+    share, mix, mix_t = lax.optimization_barrier((share, mix, mix_t))
+    total = gathered(share, total.shape)
+    grad = jnp.concatenate([nn(e_mine, total[b * head : (b + 1) * head]) for b in range(3)], axis=1) * g_mine
+
+    back = jnp.concatenate([mix, mix_t], axis=-1).reshape(2, n_line, frames, pad, 2 * head)[:, :, :, :spots]
+    moved = []
+    for step in range(1, n_line):
+        moved.append(turned(back[:, step], "y", -step))
+    back = jnp.stack([back[:, 0]] + moved)
+    away = turned(back[:, 1], "c", 1)
+    home = jnp.stack([back[:, 0], away], axis=1)
+    home = jnp.where(core == 0, home, home[:, ::-1])
+    home = lax.dynamic_slice_in_dim(jnp.concatenate([home, home], axis=0), (n_line - line) % n_line, n_line, 0)
+    home = home.transpose(2, 0, 1, 3, 4).reshape(tokens, 2 * head)
     layer = output_rows(
         feats_home, home[:, :head], home[:, head:], embed_weight, output_spatial, output_temporal
     )
@@ -310,10 +422,4 @@
     rows = P(ALL, None)
     blocks = P(ALL, None, None, None)
     placed = (blocks, P(), P(), P(), P(), rows, rows, P(), P(), blocks)
-    return jax.shard_map(
-        shards,
-        mesh=split,
-        in_specs=placed,
-        out_specs=(blocks, rows),
-        check_vma=False,
-    )
+    return jax.shard_map(shards, mesh=split, in_specs=placed, out_specs=(blocks, rows), check_vma=False)

time: 159 us -> 131 us (0.82)
  waiting for transfers between devices: 46.8 us -> 32.8 us
  matrix products: 19 us -> 5.52 us
  blocking collectives: 0 us -> 11.4 us
  starting transfers between devices: 52.6 us -> 41.8 us
  Pallas kernels: 17.5 us -> 25.4 us
  local copies, waits for them, and re-layouts: 12.4 us -> 4.69 us
    all_to_all x7 -> x5, starting transfers between devices: 39.5 us -> 26.5 us  [exchange(): return lax.all_to_all(parts, axes, 0, 0, tiled=True)]
    all_to_all x0 -> x1, blocking collectives: none -> 11.4 us  [exchange(): return lax.all_to_all(parts, axes, 0, 0, tiled=True)]
    all_to_all x2 -> x0, waiting for transfers between devices: 11.2 us -> none  [the longest x1 5.84 us: shards(): lax.all_to_all(back, CLIP, split_axis=0, concat_axis=1, tiled=True)]
    ppermute x0 -> x8, starting transfers between devices: none -> 10.6 us  [turned(): return lax.ppermute(value, axis, [(i, (i + step) % n) for i in range(n)])]
    dot_general x17 -> x0, matrix products: 9.16 us -> none  [the longest x1 2.84 us: shards(): jnp.einsum('fqk,fqd->fkd', rounded, up, preferred_element_type=f32)]
    all_to_all x2 -> x0, starting transfers between devices: 8.51 us -> none  [the longest x1 4.83 us: shards(): cots = lax.all_to_all(sent, CLIP, split_axis=1, concat_axis=0, tiled=True)]
    all_to_all x7 -> x5, waiting for transfers between devices: 35.6 us -> 27.8 us  [exchange(): return lax.all_to_all(parts, axes, 0, 0, tiled=True)]
    pallas_call x1 -> x2, Pallas kernels: 6.73 us -> 14.4 us  [the longest x1 7.66 us: attend_all(): pl.pallas_call(attend_kernel, in_specs=[pl.BlockSpec(memory_space=pltpu.S...]
  transfers between devices with their start and end apart: 10 -> 14, of which waited for: 8 -> 7; matrix products, arithmetic and copies ran while one was open for 10% -> 6% of each run, Pallas kernels for 11% -> 8%
where the time goes in v3:
time: 131 us; the launch traced here: 130 us
  starting transfers between devices  41.8 us (32%)
  waiting for transfers between devices  32.8 us (25%)
  Pallas kernels  25.4 us (19%)
  blocking collectives  11.4 us (9%)
  other arithmetic  7.53 us (6%)
  matrix products  5.52 us (4%)
  local copies, waits for them, and re-layouts  4.69 us (4%)
    all_to_all x5, waiting for transfers between devices, exchange(): return lax.all_to_all(parts, axes, 0, 0, tiled=True)  27.8 us
    all_to_all x5, starting transfers between devices, exchange(): return lax.all_to_all(parts, axes, 0, 0, tiled=True)  26.5 us
    all_to_all x1, blocking collectives, exchange(): return lax.all_to_all(parts, axes, 0, 0, tiled=True)  11.4 us
    ppermute x8, starting transfers between devices, turned(): return lax.ppermute(value, axis, [(i, (i + step) % n) for i in range(n)])  10.6 us
    pallas_call x1, Pallas kernels, attend_all(): pl.pallas_call(attend_kernel, in_specs=[pl.BlockSpec(memory_space=pltpu.S...  7.66 us
    pallas_call x1, Pallas kernels, output_rows(): pl.pallas_call(output_kernel, grid=(width // block,), in_specs=[full, ful...  6.83 us
    pallas_call x1, Pallas kernels, products(): pl.pallas_call(products_kernel, grid=(width // block,), in_specs=[full(*a...  6.76 us
    dot_general x31, matrix products, nn(): lax.dot_general(a, b, (((1,), (0,)), ((), ())), preferred_element_type=f3...  5.52 us
  transfers between devices with their start and end apart: 14, of which 7 were waited for; matrix products, arithmetic and copies ran while one was open for 6% of the time, Pallas kernels for 8%

profile of v3, /device:TPU:1, one launch (start us, length us, event | category | flops | bytes accessed | tf_op | source)
XLA Modules:
  0.0 130.1 jit_solution(12683640969197106650)
XLA Ops:
  0.6 4.6 %collective-permute-start = (bf16[2,4,40,128]{3,2,1,0:T(8,128)(2,1)}, bf16[2,4,40,128]{3,2,1,0:T(8,128)(2,1)S(1)}, u32[]{:S(2)}, u32[]{:S(2)}) collective-permute-start(bf16[2,4,40,128]{3,2,1,0:T(8,128)(2,1)} %param.10), channel_id=1, source_target_pairs={{0,1},{1,2},{2,3},{3,4},{4,5},{5,6},{6,7},{7,8},{8,9},{9,10},{10,1... | collective-permute-start | bytes 245768 | tf_op jit(solution)/shard_map/ppermute | solution.py:353
  6.0 4.1 %local_maps.1 = (bf16[1280,128]{1,0:T(8,128)(2,1)}, bf16[20,128]{1,0:T(8,128)(2,1)}, f32[20,384]{1,0:T(8,128)}) custom-call(s32[2]{0:T(128)} %pad_add_fusion.at_ref, bf16[20,384]{1,0:T(8,128)(2,1)} %ws_ref.1, bf16[20,384]{1,0:T(8,128)(2,1)} %wt_ref.1, bf16[128,5120]{1,0:T(8,128)(2,1)} %e_ref.5, bf16[128,5120]{1,0:T(8,128)(2,1)} %os_ref.5, ...), custom_call_target="tpu_custom_call" | custom-call | tf_op jit(solution)/shard_map/local_maps/pallas_call | solution.py:157
  10.4 6.8 %products.1 = (f32[256,256]{1,0:T(8,128)}, f32[320,128]{1,0:T(8,128)}, f32[320,128]{1,0:T(8,128)}) custom-call(f32[20,384]{1,0:T(8,128)} %get-tuple-element.18.after_ref, bf16[128,5120]{1,0:T(8,128)(2,1)} %e_ref.5, bf16[128,5120]{1,0:T(8,128)(2,1)} %os_ref.5, bf16[128,5120]{1,0:T(8,128)(2,1)} %ot_ref.3, bf16[320,5120]{1,0:T(8,128)(2,1)} %bitcast.210), custom_call_target="tpu_custom_call" | custom-call | tf_op jit(solution)/shard_map/products/pallas_call | solution.py:87
  17.2 1.0 convert.12
  18.2 0.9 convert.13
  23.8 1.4 %collective-permute-start.1 = (bf16[576,128]{1,0:T(8,128)(2,1)S(1)}, bf16[576,128]{1,0:T(8,128)(2,1)S(1)}, u32[]{:S(2)}, u32[]{:S(2)}) collective-permute-start(bf16[576,128]{1,0:T(8,128)(2,1)S(1)} %get-tuple-element.73), channel_id=1, source_target_pairs={{0,2},{2,4},{4,6},{6,0},{1,3},{3,5},{5,7},{7,1},{8,10},{10,12},{12... | collective-permute-start | bytes 442376 | tf_op jit(solution)/shard_map/ppermute | solution.py:328
  25.2 2.6 %collective-permute-start.2 = (bf16[576,128]{1,0:T(8,128)(2,1)S(1)}, bf16[576,128]{1,0:T(8,128)(2,1)S(1)}, u32[]{:S(2)}, u32[]{:S(2)}) collective-permute-start(bf16[576,128]{1,0:T(8,128)(2,1)S(1)} %get-tuple-element.74), channel_id=1, source_target_pairs={{0,4},{2,6},{4,0},{6,2},{1,5},{3,7},{5,1},{7,3},{8,12},{10,14},{12... | collective-permute-start | bytes 442376 | tf_op jit(solution)/shard_map/ppermute | solution.py:328
  27.8 0.8 collective-permute-start.3
  28.6 5.0 %all-to-all-start = ((bf16[32,40,128]{2,1,0:T(8,128)(2,1)}), bf16[32,40,128]{2,1,0:T(8,128)(2,1)S(1)}, u32[]{:S(2)}, u32[]{:S(2)}) async-start(bf16[32,40,128]{2,1,0:T(8,128)(2,1)} %bitcast.77), calls=%async_computation | async-start | bytes 655360 | tf_op jit(solution)/shard_map/all_to_all | solution.py:36
  33.5 0.8 collective-permute-done.2
  34.6 1.0 collective-permute-start.4
  36.2 7.0 %all-to-all-done = bf16[32,40,128]{2,1,0:T(8,128)(2,1)S(1)} async-done(((bf16[32,40,128]{2,1,0:T(8,128)(2,1)}), bf16[32,40,128]{2,1,0:T(8,128)(2,1)S(1)}, u32[]{:S(2)}, u32[]{:S(2)}) %all-to-all-start) | async-done | bytes 327712 | tf_op jit(solution)/shard_map/all_to_all | solution.py:36
  43.9 8.2 %all-to-all-start.1 = ((bf16[8,40,128]{2,1,0:T(8,128)(2,1)}), bf16[8,40,128]{2,1,0:T(8,128)(2,1)S(1)}, u32[]{:S(2)}, u32[]{:S(2)}) async-start(bf16[8,40,128]{2,1,0:T(8,128)(2,1)} %broadcast_in_dim.13), calls=%async_computation.1 | async-start | bytes 163840 | tf_op jit(solution)/shard_map/all_to_all | solution.py:36
  52.2 7.2 %all-to-all-done.1 = bf16[8,40,128]{2,1,0:T(8,128)(2,1)S(1)} async-done(((bf16[8,40,128]{2,1,0:T(8,128)(2,1)}), bf16[8,40,128]{2,1,0:T(8,128)(2,1)S(1)}, u32[]{:S(2)}, u32[]{:S(2)}) %all-to-all-start.1) | async-done | bytes 81952 | tf_op jit(solution)/shard_map/all_to_all | solution.py:36
  59.4 0.8 broadcast_in_dim.14
  60.2 5.3 %all-to-all-start.2 = ((bf16[32,40,128]{2,1,0:T(8,128)(2,1)}), bf16[32,40,128]{2,1,0:T(8,128)(2,1)S(1)}, u32[]{:S(2)}, u32[]{:S(2)}) async-start(bf16[32,40,128]{2,1,0:T(8,128)(2,1)} %broadcast_in_dim.14), calls=%async_computation.2 | async-start | bytes 655360 | tf_op jit(solution)/shard_map/all_to_all | solution.py:36
  65.6 0.8 fusion.1
  66.4 1.3 fusion.scaled_ref
  67.7 0.7 pad_maximum_fusion.4.cots_ref
  68.4 6.8 %all-to-all-done.2 = bf16[32,40,128]{2,1,0:T(8,128)(2,1)S(1)} async-done(((bf16[32,40,128]{2,1,0:T(8,128)(2,1)}), bf16[32,40,128]{2,1,0:T(8,128)(2,1)S(1)}, u32[]{:S(2)}, u32[]{:S(2)}) %all-to-all-start.2) | async-done | bytes 327712 | tf_op jit(solution)/shard_map/all_to_all | solution.py:36
  75.9 7.7 %attend_all.1 = (bf16[512,128]{1,0:T(8,128)(2,1)}, bf16[512,128]{1,0:T(8,128)(2,1)}, bf16[512,128]{1,0:T(8,128)(2,1)}) custom-call(s32[4]{0:T(128)} %pad_add_fusion.1.at_ref, bf16[2560,128]{1,0:T(8,128)(2,1)} %bitcast.208, bf16[2560,128]{1,0:T(8,128)(2,1)} %fusion.scaled_ref, f32[256,256]{1,0:T(8,128)} %copy-done.2, ...), custom_call_target="tpu_custom_call" | custom-call | tf_op jit(solution)/shard_map/attend_all/pallas_call | solution.py:304
  83.6 11.4 %all_to_all.30 = bf16[32,16,128]{2,1,0:T(8,128)(2,1)S(1)} all-to-all(bf16[32,16,128]{2,1,0:T(8,128)(2,1)} %bitcast.249), channel_id=1, replica_groups=mesh['x'=4,'zh'=2,'zl'=4,'y'=4,'c'=2] {'x','y','c'}, dimensions={0} | all-to-all | bytes 262144 | tf_op jit(solution)/shard_map/all_to_all | solution.py:36
  95.0 1.0 pad_maximum_fusion.5
  96.0 0.8 collective-permute-start.6
  96.8 1.9 %collective-permute-start.5 = (bf16[2,2,20,256]{3,2,1,0:T(8,128)(2,1)S(1)}, bf16[2,2,20,256]{3,2,1,0:T(8,128)(2,1)S(1)}, u32[]{:S(2)}, u32[]{:S(2)}) collective-permute-start(bf16[2,2,20,256]{3,2,1,0:T(8,128)(2,1)S(1)} %get-tuple-element.32), channel_id=1, source_target_pairs={{0,6},{2,0},{4,2},{6,4},{1,7},{3,1},{5,3},{7,5},{8,14},{10,8},{12,... | collective-permute-start | bytes 122888 | tf_op jit(solution)/shard_map/ppermute | solution.py:328
  98.8 1.8 %collective-permute-done.6 = bf16[2,2,20,256]{3,2,1,0:T(8,128)(2,1)S(1)} collective-permute-done((bf16[2,2,20,256]{3,2,1,0:T(8,128)(2,1)S(1)}, bf16[2,2,20,256]{3,2,1,0:T(8,128)(2,1)S(1)}, u32[]{:S(2)}, u32[]{:S(2)}) %collective-permute-start.6) | collective-permute-done | bytes 40992 | tf_op jit(solution)/shard_map/ppermute | solution.py:328
  100.6 2.3 %collective-permute-done.7 = bf16[2,2,20,256]{3,2,1,0:T(8,128)(2,1)S(1)} collective-permute-done((bf16[2,2,20,256]{3,2,1,0:T(8,128)(2,1)S(1)}, bf16[2,2,20,256]{3,2,1,0:T(8,128)(2,1)S(1)}, u32[]{:S(2)}, u32[]{:S(2)}) %collective-permute-start.7) | collective-permute-done | bytes 40992 | tf_op jit(solution)/shard_map/ppermute | solution.py:328
  103.0 2.2 %collective-permute-start.8 = (bf16[4,2,20,256]{3,2,0,1:T(8,128)(2,1)S(1)}, bf16[4,2,20,256]{3,2,0,1:T(8,128)(2,1)S(1)}, u32[]{:S(2)}, u32[]{:S(2)}) collective-permute-start(bf16[4,2,20,256]{3,2,0,1:T(8,128)(2,1)S(1)} %get-tuple-element.41), channel_id=1, source_target_pairs={{0,1},{1,0},{2,3},{3,2},{4,5},{5,4},{6,7},{7,6},{8,9},{9,8},{10,11... | collective-permute-start | bytes 245768 | tf_op jit(solution)/shard_map/ppermute | solution.py:328
  105.8 3.3 %all-to-all-start.4 = ((bf16[8,16,128]{2,1,0:T(8,128)(2,1)}), bf16[8,16,128]{2,1,0:T(8,128)(2,1)S(1)}, u32[]{:S(2)}, u32[]{:S(2)}) async-start(bf16[8,16,128]{2,1,0:T(8,128)(2,1)} %broadcast_in_dim.15), calls=%async_computation.4 | async-start | bytes 65536 | tf_op jit(solution)/shard_map/all_to_all | solution.py:36
  109.2 6.8 %all-to-all-done.4 = bf16[8,16,128]{2,1,0:T(8,128)(2,1)S(1)} async-done(((bf16[8,16,128]{2,1,0:T(8,128)(2,1)}), bf16[8,16,128]{2,1,0:T(8,128)(2,1)S(1)}, u32[]{:S(2)}, u32[]{:S(2)}) %all-to-all-start.4) | async-done | bytes 32800 | tf_op jit(solution)/shard_map/all_to_all | solution.py:36
  116.6 4.7 %all-to-all-start.5 = ((bf16[32,16,128]{2,1,0:T(8,128)(2,1)}), bf16[32,16,128]{2,1,0:T(8,128)(2,1)S(1)}, u32[]{:S(2)}, u32[]{:S(2)}) async-start(bf16[32,16,128]{2,1,0:T(8,128)(2,1)} %broadcast_in_dim.16), calls=%async_computation.5 | async-start | bytes 262144 | tf_op jit(solution)/shard_map/all_to_all | solution.py:36
  122.2 6.8 %output_rows.1 = bf16[320,5120]{1,0:T(8,128)(2,1)} custom-call(bf16[320,128]{1,0:T(8,128)(2,1)} %copy-done.4, bf16[320,128]{1,0:T(8,128)(2,1)} %get-tuple-element.43.m_ref, bf16[320,128]{1,0:T(8,128)(2,1)} %get-tuple-element.42.t_ref, bf16[128,5120]{1,0:T(8,128)(2,1)} %e_ref.5, bf16[128,5120]{1,0:T(8,128)(2,1)} %os_ref.5, bf16[128,5120]{1,0:T(8,128)(2,1)} %ot_ref.3), custom_call_target="tpu_custom_call" | custom-call | tf_op jit(solution)/shard_map/output_rows/pallas_call | solution.py:112
  (95 shorter events, 11.3 us)
Async XLA Ops:
  0.6 9.4 %collective-permute-start = (bf16[2,4,40,128]{3,2,1,0:T(8,128)(2,1)}, bf16[2,4,40,128]{3,2,1,0:T(8,128)(2,1)S(1)}, u32[]{:S(2)}, u32[]{:S(2)}) collective-permute-start(bf16[2,4,40,128]{3,2,1,0:T(8,128)(2,1)} %param.10), channel_id=1, source_target_pairs={{0,1},{1,2},{2,3},{3,4},{4,5},{5,6},{6,7},{7,8},{8,9},{9,10},{10,1... | collective-permute-start | bytes 245768 | tf_op jit(solution)/shard_map/ppermute | solution.py:353
  6.0 4.1 %copy-start.5 = (bf16[2,4,40,128]{3,2,1,0:T(8,128)(2,1)S(1)}, bf16[2,4,40,128]{3,2,1,0:T(8,128)(2,1)}, u32[]{:S(2)}) copy-start(bf16[2,4,40,128]{3,2,1,0:T(8,128)(2,1)} %param.10) | copy-start | bytes 245764
  17.2 2.1 %copy-start.3 = (bf16[3,3,3,128,128]{4,3,2,1,0:T(8,128)(2,1)S(1)}, bf16[3,3,3,128,128]{4,3,2,1,0:T(8,128)(2,1)}, u32[]{:S(2)}) copy-start(bf16[3,3,3,128,128]{4,3,2,1,0:T(8,128)(2,1)} %param.11) | copy-start | bytes 2654212
  23.7 10.7 %copy-start.4 = (bf16[320,128]{1,0:T(8,128)(2,1)}, bf16[320,128]{1,0:T(8,128)(2,1)S(1)}, u32[]{:S(2)}) copy-start(bf16[320,128]{1,0:T(8,128)(2,1)S(1)} %fusion.15.f_ref) | copy-start | bytes 245764
  23.8 9.8 %collective-permute-start.1 = (bf16[576,128]{1,0:T(8,128)(2,1)S(1)}, bf16[576,128]{1,0:T(8,128)(2,1)S(1)}, u32[]{:S(2)}, u32[]{:S(2)}) collective-permute-start(bf16[576,128]{1,0:T(8,128)(2,1)S(1)} %get-tuple-element.73), channel_id=1, source_target_pairs={{0,2},{2,4},{4,6},{6,0},{1,3},{3,5},{5,7},{7,1},{8,10},{10,12},{12... | collective-permute-start | bytes 442376 | tf_op jit(solution)/shard_map/ppermute | solution.py:328
  25.2 9.2 %collective-permute-start.2 = (bf16[576,128]{1,0:T(8,128)(2,1)S(1)}, bf16[576,128]{1,0:T(8,128)(2,1)S(1)}, u32[]{:S(2)}, u32[]{:S(2)}) collective-permute-start(bf16[576,128]{1,0:T(8,128)(2,1)S(1)} %get-tuple-element.74), channel_id=1, source_target_pairs={{0,4},{2,6},{4,0},{6,2},{1,5},{3,7},{5,1},{7,3},{8,12},{10,14},{12... | collective-permute-start | bytes 442376 | tf_op jit(solution)/shard_map/ppermute | solution.py:328
  27.8 6.6 %collective-permute-start.3 = (bf16[576,128]{1,0:T(8,128)(2,1)S(1)}, bf16[576,128]{1,0:T(8,128)(2,1)S(1)}, u32[]{:S(2)}, u32[]{:S(2)}) collective-permute-start(bf16[576,128]{1,0:T(8,128)(2,1)S(1)} %get-tuple-element.75), channel_id=1, source_target_pairs={{0,6},{2,0},{4,2},{6,4},{1,7},{3,1},{5,3},{7,5},{8,14},{10,8},{12,... | collective-permute-start | bytes 442376 | tf_op jit(solution)/shard_map/ppermute | solution.py:328
  28.6 14.6 %all-to-all-start = ((bf16[32,40,128]{2,1,0:T(8,128)(2,1)}), bf16[32,40,128]{2,1,0:T(8,128)(2,1)S(1)}, u32[]{:S(2)}, u32[]{:S(2)}) async-start(bf16[32,40,128]{2,1,0:T(8,128)(2,1)} %bitcast.77), calls=%async_computation | async-start | bytes 655360 | tf_op jit(solution)/shard_map/all_to_all | solution.py:36
  34.5 17.7 %copy-start.6 = (f32[256,256]{1,0:T(8,128)S(1)}, f32[256,256]{1,0:T(8,128)}, u32[]{:S(2)}) copy-start(f32[256,256]{1,0:T(8,128)} %get-tuple-element.21) | copy-start | bytes 786436
  34.6 30.9 %collective-permute-start.4 = (bf16[4,448,128]{2,1,0:T(8,128)(2,1)S(1)}, bf16[4,448,128]{2,1,0:T(8,128)(2,1)S(1)}, u32[]{:S(2)}, u32[]{:S(2)}) collective-permute-start(bf16[4,448,128]{2,1,0:T(8,128)(2,1)S(1)} %pad_maximum_fusion.2), channel_id=1, source_target_pairs={{0,1},{1,0},{2,3},{3,2},{4,5},{5,4},{6,7},{7,6},{8,9},{9,8},{10,11... | collective-permute-start | bytes 1376264 | tf_op jit(solution)/shard_map/ppermute | solution.py:328
  43.9 15.5 %all-to-all-start.1 = ((bf16[8,40,128]{2,1,0:T(8,128)(2,1)}), bf16[8,40,128]{2,1,0:T(8,128)(2,1)S(1)}, u32[]{:S(2)}, u32[]{:S(2)}) async-start(bf16[8,40,128]{2,1,0:T(8,128)(2,1)} %broadcast_in_dim.13), calls=%async_computation.1 | async-start | bytes 163840 | tf_op jit(solution)/shard_map/all_to_all | solution.py:36
  52.1 13.5 %copy-start.2 = (f32[256,256]{1,0:T(8,128)}, f32[256,256]{1,0:T(8,128)S(1)}, u32[]{:S(2)}) copy-start(f32[256,256]{1,0:T(8,128)S(1)} %broadcast_multiply_fusion.gram_ref) | copy-start | bytes 786436
  60.2 15.0 %all-to-all-start.2 = ((bf16[32,40,128]{2,1,0:T(8,128)(2,1)}), bf16[32,40,128]{2,1,0:T(8,128)(2,1)S(1)}, u32[]{:S(2)}, u32[]{:S(2)}) async-start(bf16[32,40,128]{2,1,0:T(8,128)(2,1)} %broadcast_in_dim.14), calls=%async_computation.2 | async-start | bytes 655360 | tf_op jit(solution)/shard_map/all_to_all | solution.py:36
  65.6 2.8 %copy-start = (bf16[8,320,128]{2,1,0:T(8,128)(2,1)}, bf16[8,320,128]{2,1,0:T(8,128)(2,1)S(1)}, u32[]{:S(2)}) copy-start(bf16[8,320,128]{2,1,0:T(8,128)(2,1)S(1)} %pad_maximum_fusion) | copy-start | bytes 1966084
  75.2 0.7 copy-start.1
  96.0 4.5 %collective-permute-start.6 = (bf16[2,2,20,256]{3,2,1,0:T(8,128)(2,1)S(1)}, bf16[2,2,20,256]{3,2,1,0:T(8,128)(2,1)S(1)}, u32[]{:S(2)}, u32[]{:S(2)}) collective-permute-start(bf16[2,2,20,256]{3,2,1,0:T(8,128)(2,1)S(1)} %get-tuple-element.31), channel_id=1, source_target_pairs={{0,4},{2,6},{4,0},{6,2},{1,5},{3,7},{5,1},{7,3},{8,12},{10,14},{12... | collective-permute-start | bytes 122888 | tf_op jit(solution)/shard_map/ppermute | solution.py:328
  96.8 3.8 %collective-permute-start.5 = (bf16[2,2,20,256]{3,2,1,0:T(8,128)(2,1)S(1)}, bf16[2,2,20,256]{3,2,1,0:T(8,128)(2,1)S(1)}, u32[]{:S(2)}, u32[]{:S(2)}) collective-permute-start(bf16[2,2,20,256]{3,2,1,0:T(8,128)(2,1)S(1)} %get-tuple-element.32), channel_id=1, source_target_pairs={{0,6},{2,0},{4,2},{6,4},{1,7},{3,1},{5,3},{7,5},{8,14},{10,8},{12,... | collective-permute-start | bytes 122888 | tf_op jit(solution)/shard_map/ppermute | solution.py:328
  98.8 4.2 %collective-permute-start.7 = (bf16[2,2,20,256]{3,2,1,0:T(8,128)(2,1)S(1)}, bf16[2,2,20,256]{3,2,1,0:T(8,128)(2,1)S(1)}, u32[]{:S(2)}, u32[]{:S(2)}) collective-permute-start(bf16[2,2,20,256]{3,2,1,0:T(8,128)(2,1)S(1)} %get-tuple-element.33), channel_id=1, source_target_pairs={{0,2},{2,4},{4,6},{6,0},{1,3},{3,5},{5,7},{7,1},{8,10},{10,12},{12... | collective-permute-start | bytes 122888 | tf_op jit(solution)/shard_map/ppermute | solution.py:328
  103.0 18.3 %collective-permute-start.8 = (bf16[4,2,20,256]{3,2,0,1:T(8,128)(2,1)S(1)}, bf16[4,2,20,256]{3,2,0,1:T(8,128)(2,1)S(1)}, u32[]{:S(2)}, u32[]{:S(2)}) collective-permute-start(bf16[4,2,20,256]{3,2,0,1:T(8,128)(2,1)S(1)} %get-tuple-element.41), channel_id=1, source_target_pairs={{0,1},{1,0},{2,3},{3,2},{4,5},{5,4},{6,7},{7,6},{8,9},{9,8},{10,11... | collective-permute-start | bytes 245768 | tf_op jit(solution)/shard_map/ppermute | solution.py:328
  105.8 10.1 %all-to-all-start.4 = ((bf16[8,16,128]{2,1,0:T(8,128)(2,1)}), bf16[8,16,128]{2,1,0:T(8,128)(2,1)S(1)}, u32[]{:S(2)}, u32[]{:S(2)}) async-start(bf16[8,16,128]{2,1,0:T(8,128)(2,1)} %broadcast_in_dim.15), calls=%async_computation.4 | async-start | bytes 65536 | tf_op jit(solution)/shard_map/all_to_all | solution.py:36
  116.6 12.5 %all-to-all-start.5 = ((bf16[32,16,128]{2,1,0:T(8,128)(2,1)}), bf16[32,16,128]{2,1,0:T(8,128)(2,1)S(1)}, u32[]{:S(2)}, u32[]{:S(2)}) async-start(bf16[32,16,128]{2,1,0:T(8,128)(2,1)} %broadcast_in_dim.16), calls=%async_computation.5 | async-start | bytes 262144 | tf_op jit(solution)/shard_map/all_to_all | solution.py:36
  122.2 6.9 %copy-start.8 = (bf16[20,128]{1,0:T(8,128)(2,1)S(1)}, bf16[20,128]{1,0:T(8,128)(2,1)}, u32[]{:S(2)}) copy-start(bf16[20,128]{1,0:T(8,128)(2,1)} %get-tuple-element.28) | copy-start | bytes 15364
  122.2 7.3 %copy-start.7 = (f32[20,384]{1,0:T(8,128)S(1)}, f32[20,384]{1,0:T(8,128)}, u32[]{:S(2)}) copy-start(f32[20,384]{1,0:T(8,128)} %get-tuple-element.18.after_ref) | copy-start | bytes 92164

commit v4 on v3

--- a/solution.py
+++ b/solution.py
@@ -43,80 +43,157 @@
     return exchange(jnp.broadcast_to(value, (size,) + value.shape), axes)
 
 
-def conv_local(volume, weight, count):
-    _, height, columns, channels = volume.shape
-    out_channels = weight.shape[-1]
-    padded = jnp.pad(volume, ((0, 0), (1, 1), (1, 1), (0, 0)))
-    summed = jnp.zeros((count * height * columns, out_channels), f32)
-    for time_tap in range(3):
-        for row_tap in range(3):
-            for col_tap in range(3):
-                window = padded[
-                    2 - time_tap : 2 - time_tap + count,
-                    row_tap : row_tap + height,
-                    col_tap : col_tap + columns,
-                    :,
-                ]
-                summed = summed + nn(
-                    window.reshape(-1, channels), weight[time_tap, row_tap, col_tap]
-                )
-    return summed
-
-
-def products_kernel(after_ref, e_ref, os_ref, ot_ref, cot_ref, gram_ref, cots_ref, cott_ref):
-    @pl.when(pl.program_id(0) == 0)
-    def _():
-        gram_ref[...] = jnp.zeros_like(gram_ref)
-        cots_ref[...] = jnp.zeros_like(cots_ref)
-        cott_ref[...] = jnp.zeros_like(cott_ref)
-
-    e, o, t, c = e_ref[...], os_ref[...], ot_ref[...], cot_ref[...]
-    both = jnp.concatenate([e, o], axis=0)
-    gram_ref[...] += nt(both, both)
-    cots_ref[...] += nt(c, o)
-    cott_ref[...] += nt(c, t)
-
-
-def products(after, embed, out_s, out_t, cot):
-    width = embed.shape[1]
-    head = embed.shape[0]
+def conv_kernel(prior_ref, here_ref, weight_ref, out_ref):
+    tokens = here_ref.shape[0]
+    columns = here_ref.shape[0] // 8
+    volume = jnp.concatenate([prior_ref[...].astype(f32), here_ref[...].astype(f32)], axis=0)
+    rows = volume.shape[0]
+    place = lax.broadcasted_iota(jnp.int32, (rows, 1), 0) % columns
+    left = jnp.where(place == 0, 0.0, pltpu.roll(volume, 1, 0))
+    right = jnp.where(place == columns - 1, 0.0, pltpu.roll(volume, rows - 1, 0))
+    taps = jnp.concatenate([left, volume, right], axis=1).astype(bf16)
+    frame = tokens // 2
+    sums = [None, None, None]
+    for back in range(3):
+        start = (2 - back) * frame
+        window = taps[start : start + tokens]
+        for up in range(3):
+            got = nn(window, weight_ref[back * 3 + up])
+            sums[up] = got if sums[up] is None else sums[up] + got
+    gap = jnp.zeros((columns, sums[0].shape[1]), f32)
+    above, same, below = sums
+    for f in range(2):
+        lo, hi = f * frame, (f + 1) * frame
+        total = (
+            same[lo:hi]
+            + jnp.concatenate([gap, above[lo : hi - columns]], axis=0)
+            + jnp.concatenate([below[lo + columns : hi], gap], axis=0)
+        )
+        out_ref[lo:hi] = jax.nn.gelu(total, approximate=True).astype(bf16)
+
+
+def conv_rows(prior, here, weight):
+    tokens, channels = here.shape
+    vmem = pl.BlockSpec(memory_space=pltpu.VMEM)
+    return pl.pallas_call(
+        conv_kernel,
+        in_specs=[vmem] * 3,
+        out_specs=vmem,
+        out_shape=jax.ShapeDtypeStruct((tokens, weight.shape[-1]), bf16),
+        name="conv_rows",
+    )(prior, here, weight.reshape(9, 3 * channels, weight.shape[-1]))
+
+
+CHUNK = 1024
+
+
+def products_kernel(
+    e_ref, os_ref, ot_ref, cot_ref, gram_ref, cots_ref, weights, cotangents, gram_sum, cots_sum, arrived
+):
+    head, width = e_ref.shape
+    copies = []
+    for i in range(width // CHUNK):
+        cols = pl.ds(i * CHUNK, CHUNK)
+        group = [
+            pltpu.make_async_copy(ref.at[:, cols], weights.at[pl.ds(k * head, head), cols], arrived.at[i, k])
+            for k, ref in enumerate((e_ref, os_ref, ot_ref))
+        ]
+        group.append(pltpu.make_async_copy(cot_ref.at[:, cols], cotangents.at[:, cols], arrived.at[i, 3]))
+        for copy in group:
+            copy.start()
+        copies.append(group)
+    for i, group in enumerate(copies):
+        for copy in group:
+            copy.wait()
+        cols = slice(i * CHUNK, (i + 1) * CHUNK)
+        first = weights[: 2 * head, cols]
+        gram = nt(first, first)
+        cots = nt(cotangents[:, cols], weights[head:, cols])
+        gram_sum[...] = gram if i == 0 else gram_sum[...] + gram
+        cots_sum[...] = cots if i == 0 else cots_sum[...] + cots
+    gram_ref[...] = gram_sum[...] * (1.0 / width)
+    slots, kinds, frames, pad, _ = cots_ref.shape
+    places = cots_sum.shape[0] // frames
+    spots = places // slots
+    r = lax.broadcasted_iota(jnp.int32, (slots * pad, places), 0)
+    c = lax.broadcasted_iota(jnp.int32, (slots * pad, places), 1)
+    spread = jnp.where((c == (r // pad) * spots + r % pad) & (r % pad < spots), 1.0, 0.0).astype(bf16)
+    for f in range(frames):
+        got = nn(spread, cots_sum[f * places : (f + 1) * places].astype(bf16)).astype(bf16)
+        for slot in range(slots):
+            for kind in range(kinds):
+                cots_ref[slot, kind, f] = got[slot * pad : (slot + 1) * pad, kind * head : (kind + 1) * head]
+
+
+def products(embed, out_s, out_t, cot, frames, slots, pad):
+    head, width = embed.shape
     tokens = cot.shape[0]
-    block = 1024
-    row = lambda rows: pl.BlockSpec((rows, block), lambda i: (0, i))
-    full = lambda r, c: pl.BlockSpec((r, c), lambda i: (0, 0))
+    hbm = pl.BlockSpec(memory_space=pl.ANY)
+    vmem = pl.BlockSpec(memory_space=pltpu.VMEM)
     return pl.pallas_call(
         products_kernel,
-        grid=(width // block,),
-        in_specs=[full(*after.shape), row(head), row(head), row(head), row(tokens)],
-        out_specs=[full(2 * head, 2 * head), full(tokens, head), full(tokens, head)],
+        in_specs=[hbm] * 4,
+        out_specs=[vmem, vmem],
         out_shape=[
             jax.ShapeDtypeStruct((2 * head, 2 * head), f32),
-            jax.ShapeDtypeStruct((tokens, head), f32),
-            jax.ShapeDtypeStruct((tokens, head), f32),
+            jax.ShapeDtypeStruct((slots, 2, frames, pad, head), bf16),
+        ],
+        scratch_shapes=[
+            pltpu.VMEM((3 * head, width), bf16),
+            pltpu.VMEM((tokens, width), bf16),
+            pltpu.VMEM((2 * head, 2 * head), f32),
+            pltpu.VMEM((tokens, 2 * head), f32),
+            pltpu.SemaphoreType.DMA((width // CHUNK, 4)),
         ],
         name="products",
-    )(after, embed, out_s, out_t, cot)
-
-
-def output_kernel(f_ref, m_ref, t_ref, e_ref, os_ref, ot_ref, out_ref):
-    total = nn(f_ref[...], e_ref[...]) + nn(m_ref[...], os_ref[...]) + nn(t_ref[...], ot_ref[...])
-    out_ref[...] = total.astype(bf16)
-
-
-def output_rows(feats, mix_s, mix_t, embed, out_s, out_t):
+    )(embed, out_s, out_t, cot)
+
+
+def output_kernel(f_ref, mixes_ref, e_ref, os_ref, ot_ref, out_ref, weights, rows, arrived, sent):
+    head, width = e_ref.shape
+    copies = []
+    for i in range(width // CHUNK):
+        cols = pl.ds(i * CHUNK, CHUNK)
+        group = [
+            pltpu.make_async_copy(ref.at[:, cols], weights.at[pl.ds(k * head, head), cols], arrived.at[i, k])
+            for k, ref in enumerate((e_ref, os_ref, ot_ref))
+        ]
+        for copy in group:
+            copy.start()
+        copies.append(group)
+    x = jnp.concatenate([f_ref[...], mixes_ref[...]], axis=1)
+    leaving = []
+    for i, group in enumerate(copies):
+        for copy in group:
+            copy.wait()
+        cols = slice(i * CHUNK, (i + 1) * CHUNK)
+        rows[:, cols] = nn(x, weights[:, cols]).astype(bf16)
+        cols = pl.ds(i * CHUNK, CHUNK)
+        copy = pltpu.make_async_copy(rows.at[:, cols], out_ref.at[:, cols], sent.at[i])
+        copy.start()
+        leaving.append(copy)
+    for copy in leaving:
+        copy.wait()
+
+
+def output_rows(feats, mixes, embed, out_s, out_t):
     tokens, head = feats.shape
     width = embed.shape[1]
-    block = 1024
-    row = lambda rows: pl.BlockSpec((rows, block), lambda i: (0, i))
-    full = pl.BlockSpec((tokens, head), lambda i: (0, 0))
+    hbm = pl.BlockSpec(memory_space=pl.ANY)
+    vmem = pl.BlockSpec(memory_space=pltpu.VMEM)
     return pl.pallas_call(
         output_kernel,
-        grid=(width // block,),
-        in_specs=[full, full, full, row(head), row(head), row(head)],
-        out_specs=row(tokens),
+        in_specs=[vmem, vmem, hbm, hbm, hbm],
+        out_specs=hbm,
         out_shape=jax.ShapeDtypeStruct((tokens, width), bf16),
+        scratch_shapes=[
+            pltpu.VMEM((3 * head, width), bf16),
+            pltpu.VMEM((tokens, width), bf16),
+            pltpu.SemaphoreType.DMA((width // CHUNK, 3)),
+            pltpu.SemaphoreType.DMA((width // CHUNK,)),
+        ],
         name="output_rows",
-    )(feats, mix_s, mix_t, embed, out_s, out_t)
+    )(feats, mixes, embed, out_s, out_t)
 
 
 def maps_kernel(at_ref, ws_ref, wt_ref, e_ref, os_ref, gs_ref, gt_ref, maps_ref, e_mine_ref, g_mine_ref):
@@ -340,7 +417,7 @@
     output_temporal,
     cotangent,
 ):
-    frames, height, columns, _ = clip_video.shape
+    frames, height, columns, channels = clip_video.shape
     places = height * columns
     tokens = frames * places
     head, width = embed_weight.shape
@@ -356,22 +433,25 @@
     maps, e_mine, g_mine = local_maps(
         at, input_spatial, input_temporal, embed_weight, output_spatial, gain_spatial, gain_temporal, 10 * head
     )
-    prior, g_mine = lax.optimization_barrier((prior, g_mine))
     maps = gathered(scattered(maps), maps.shape)
 
-    volume = jnp.concatenate([prior, clip_video], axis=0)
-    feats_home = jax.nn.gelu(conv_local(volume, conv_weight, frames), approximate=True).astype(bf16)
-    gram, cot_s, cot_t = products(
-        g_mine, embed_weight, output_spatial, output_temporal, cotangent.reshape(tokens, width)
+    feats_home = conv_rows(
+        prior.reshape(tokens, channels), clip_video.reshape(tokens, channels), conv_weight
     )
-    gram = gram * (1.0 / width)
     n_line = lax.axis_size("y")
     line = lax.axis_index("y")
     core = lax.axis_index("c")
     pad = 32
-    cots = jnp.stack([cot_s, cot_t]).astype(bf16).reshape(2, frames, n_line, 2, spots, head)
-    cots = jnp.pad(cots, ((0, 0),) * 4 + ((0, pad - spots), (0, 0)))
-    cots = cots.transpose(2, 3, 0, 1, 4, 5).reshape(n_line, 4 * frames * pad, head)
+    gram, cots = products(
+        embed_weight,
+        output_spatial,
+        output_temporal,
+        cotangent.reshape(tokens, width),
+        frames,
+        n_clip,
+        pad,
+    )
+    cots = cots.reshape(n_line, 4 * frames * pad, head)
     held = [
         jnp.concatenate(
             [feats_home, lax.dynamic_index_in_dim(cots, (line + step) % n_line, 0, keepdims=False)], axis=0
@@ -411,9 +491,7 @@
     home = jnp.where(core == 0, home, home[:, ::-1])
     home = lax.dynamic_slice_in_dim(jnp.concatenate([home, home], axis=0), (n_line - line) % n_line, n_line, 0)
     home = home.transpose(2, 0, 1, 3, 4).reshape(tokens, 2 * head)
-    layer = output_rows(
-        feats_home, home[:, :head], home[:, head:], embed_weight, output_spatial, output_temporal
-    )
+    layer = output_rows(feats_home, home, embed_weight, output_spatial, output_temporal)
     return (layer.reshape(frames, height, columns, width), grad)
 
 

time: 131 us -> 127 us (0.969)
  matrix products: 5.52 us -> 2.06 us
    dot_general x31 -> x4, matrix products: 5.52 us -> 2.06 us  [nn(): lax.dot_general(a, b, (((1,), (0,)), ((), ())), preferred_element_type=f3...]
    another operation x2 -> x0, other arithmetic: 1.93 us -> none
    all_to_all x5, waiting for transfers between devices: 27.8 us -> 29.6 us  [exchange(): return lax.all_to_all(parts, axes, 0, 0, tiled=True)]
    pallas_call x2 -> x3, Pallas kernels: 13.6 us -> 13.2 us  [the longest x1 5.64 us: output_rows(): pl.pallas_call(output_kernel, in_specs=[vmem, vmem, hbm, hbm, hbm], out_s...]
  transfers between devices with their start and end apart: 14 -> 14, of which waited for: 7 -> 7; matrix products, arithmetic and copies ran while one was open for 6% -> 8% of each run, Pallas kernels for 8% -> 11%
where the time goes in v4:
time: 127 us; the launch traced here: 126 us
  starting transfers between devices  40.7 us (32%)
  waiting for transfers between devices  33.8 us (27%)
  Pallas kernels  24.8 us (20%)
  blocking collectives  11.4 us (9%)
  other arithmetic  6.28 us (5%)
  local copies, waits for them, and re-layouts  5.92 us (5%)
  matrix products  2.06 us (2%)
    all_to_all x5, waiting for transfers between devices, exchange(): return lax.all_to_all(parts, axes, 0, 0, tiled=True)  29.6 us
    all_to_all x5, starting transfers between devices, exchange(): return lax.all_to_all(parts, axes, 0, 0, tiled=True)  26.1 us
    all_to_all x1, blocking collectives, exchange(): return lax.all_to_all(parts, axes, 0, 0, tiled=True)  11.4 us
    ppermute x8, starting transfers between devices, turned(): return lax.ppermute(value, axis, [(i, (i + step) % n) for i in range(n)])  10 us
    pallas_call x1, Pallas kernels, attend_all(): pl.pallas_call(attend_kernel, in_specs=[pl.BlockSpec(memory_space=pltpu.S...  7.66 us
    pallas_call x1, Pallas kernels, output_rows(): pl.pallas_call(output_kernel, in_specs=[vmem, vmem, hbm, hbm, hbm], out_s...  5.64 us
    pallas_call x1, Pallas kernels, products(): pl.pallas_call(products_kernel, in_specs=[hbm] * 4, out_specs=[vmem, vmem...  4.84 us
    ppermute x1, starting transfers between devices, shards(): prior = lax.ppermute(clip_video, TS, [(i, i + 1) for i in range(n_ts - 1)])  4.59 us
  transfers between devices with their start and end apart: 14, of which 7 were waited for; matrix products, arithmetic and copies ran while one was open for 8% of the time, Pallas kernels for 11%

profile of v4, /device:TPU:1, one launch (start us, length us, event | category | flops | bytes accessed | tf_op | source)
XLA Modules:
  0.0 126.0 jit_solution(3383845901666883028)
XLA Ops:
  0.6 4.6 %collective-permute-start = (bf16[2,4,40,128]{3,2,1,0:T(8,128)(2,1)}, bf16[2,4,40,128]{3,2,1,0:T(8,128)(2,1)S(1)}, u32[]{:S(2)}, u32[]{:S(2)}) collective-permute-start(bf16[2,4,40,128]{3,2,1,0:T(8,128)(2,1)} %param.10), channel_id=1, source_target_pairs={{0,1},{1,2},{2,3},{3,4},{4,5},{5,6},{6,7},{7,8},{8,9},{9,10},{10,1... | collective-permute-start | bytes 245768 | tf_op jit(solution)/shard_map/ppermute | solution.py:430
  5.3 4.8 %products.1 = (f32[256,256]{1,0:T(8,128)}, bf16[8,2,2,32,128]{4,3,2,1,0:T(8,128)(2,1)}) custom-call(bf16[128,5120]{1,0:T(8,128)(2,1)} %e_ref.5, bf16[128,5120]{1,0:T(8,128)(2,1)} %os_ref.5, bf16[128,5120]{1,0:T(8,128)(2,1)} %ot_ref.3, bf16[320,5120]{1,0:T(8,128)(2,1)} %bitcast.77), custom_call_target="tpu_custom_call" | custom-call | tf_op jit(solution)/shard_map/products/pallas_call | solution.py:133
  10.1 1.0 dynamic-slice_bitcast_fusion.4
  11.7 2.7 %conv_rows.1.f_ref = bf16[320,128]{1,0:T(8,128)(2,1)} custom-call(bf16[320,128]{1,0:T(8,128)(2,1)} %bitcast.99, bf16[320,128]{1,0:T(8,128)(2,1)} %bitcast.98, bf16[9,384,128]{2,1,0:T(8,128)(2,1)} %bitcast.81), custom_call_target="tpu_custom_call" | custom-call | tf_op jit(solution)/shard_map/conv_rows/pallas_call | solution.py:78
  14.4 0.9 fusion.4
  15.4 1.4 %collective-permute-start.1 = (bf16[576,128]{1,0:T(8,128)(2,1)S(1)}, bf16[576,128]{1,0:T(8,128)(2,1)S(1)}, u32[]{:S(2)}, u32[]{:S(2)}) collective-permute-start(bf16[576,128]{1,0:T(8,128)(2,1)S(1)} %get-tuple-element.40), channel_id=1, source_target_pairs={{0,2},{2,4},{4,6},{6,0},{1,3},{3,5},{5,7},{7,1},{8,10},{10,12},{12... | collective-permute-start | bytes 442376 | tf_op jit(solution)/shard_map/ppermute | solution.py:405
  16.8 2.6 %collective-permute-start.2 = (bf16[576,128]{1,0:T(8,128)(2,1)S(1)}, bf16[576,128]{1,0:T(8,128)(2,1)S(1)}, u32[]{:S(2)}, u32[]{:S(2)}) collective-permute-start(bf16[576,128]{1,0:T(8,128)(2,1)S(1)} %get-tuple-element.41), channel_id=1, source_target_pairs={{0,4},{2,6},{4,0},{6,2},{1,5},{3,7},{5,1},{7,3},{8,12},{10,14},{12... | collective-permute-start | bytes 442376 | tf_op jit(solution)/shard_map/ppermute | solution.py:405
  19.4 0.8 collective-permute-start.3
  20.7 4.0 %local_maps.1 = (bf16[1280,128]{1,0:T(8,128)(2,1)}, bf16[20,128]{1,0:T(8,128)(2,1)}, f32[20,384]{1,0:T(8,128)}) custom-call(s32[2]{0:T(128)} %pad_add_fusion.1.at_ref, bf16[20,384]{1,0:T(8,128)(2,1)} %ws_ref.1, bf16[20,384]{1,0:T(8,128)(2,1)} %wt_ref.1, bf16[128,5120]{1,0:T(8,128)(2,1)} %e_ref.5, bf16[128,5120]{1,0:T(8,128)(2,1)} %os_ref.5, ...), custom_call_target="tpu_custom_call" | custom-call | tf_op jit(solution)/shard_map/local_maps/pallas_call | solution.py:234
  24.7 5.0 %all-to-all-start = ((bf16[32,40,128]{2,1,0:T(8,128)(2,1)}), bf16[32,40,128]{2,1,0:T(8,128)(2,1)S(1)}, u32[]{:S(2)}, u32[]{:S(2)}) async-start(bf16[32,40,128]{2,1,0:T(8,128)(2,1)} %bitcast.91), calls=%async_computation | async-start | bytes 655360 | tf_op jit(solution)/shard_map/all_to_all | solution.py:36
  30.3 9.0 %all-to-all-done = bf16[32,40,128]{2,1,0:T(8,128)(2,1)S(1)} async-done(((bf16[32,40,128]{2,1,0:T(8,128)(2,1)}), bf16[32,40,128]{2,1,0:T(8,128)(2,1)S(1)}, u32[]{:S(2)}, u32[]{:S(2)}) %all-to-all-start) | async-done | bytes 327712 | tf_op jit(solution)/shard_map/all_to_all | solution.py:36
  40.0 7.8 %all-to-all-start.1 = ((bf16[8,40,128]{2,1,0:T(8,128)(2,1)}), bf16[8,40,128]{2,1,0:T(8,128)(2,1)S(1)}, u32[]{:S(2)}, u32[]{:S(2)}) async-start(bf16[8,40,128]{2,1,0:T(8,128)(2,1)} %broadcast_in_dim.13), calls=%async_computation.1 | async-start | bytes 163840 | tf_op jit(solution)/shard_map/all_to_all | solution.py:36
  48.5 6.7 %all-to-all-done.1 = bf16[8,40,128]{2,1,0:T(8,128)(2,1)S(1)} async-done(((bf16[8,40,128]{2,1,0:T(8,128)(2,1)}), bf16[8,40,128]{2,1,0:T(8,128)(2,1)S(1)}, u32[]{:S(2)}, u32[]{:S(2)}) %all-to-all-start.1) | async-done | bytes 81952 | tf_op jit(solution)/shard_map/all_to_all | solution.py:36
  55.2 0.8 broadcast_in_dim.14
  56.0 5.3 %all-to-all-start.2 = ((bf16[32,40,128]{2,1,0:T(8,128)(2,1)}), bf16[32,40,128]{2,1,0:T(8,128)(2,1)S(1)}, u32[]{:S(2)}, u32[]{:S(2)}) async-start(bf16[32,40,128]{2,1,0:T(8,128)(2,1)} %broadcast_in_dim.14), calls=%async_computation.2 | async-start | bytes 655360 | tf_op jit(solution)/shard_map/all_to_all | solution.py:36
  61.4 1.7 %fusion.1 = f32[2560]{0:T(1024)S(1)} fusion(bf16[2560,128]{1,0:T(8,128)(2,1)S(1)} %bitcast.75, f32[256,256]{1,0:T(8,128)} %get-tuple-element.14.gram_ref), kind=kOutput, calls=%fused_computation.3 | convolution fusion | flops 504296960 | bytes 1386496 | tf_op jit(solution)/shard_map/dot_general | solution.py:32
  63.1 1.2 fusion.scaled_ref
  65.1 5.9 %all-to-all-done.2 = bf16[32,40,128]{2,1,0:T(8,128)(2,1)S(1)} async-done(((bf16[32,40,128]{2,1,0:T(8,128)(2,1)}), bf16[32,40,128]{2,1,0:T(8,128)(2,1)S(1)}, u32[]{:S(2)}, u32[]{:S(2)}) %all-to-all-start.2) | async-done | bytes 327712 | tf_op jit(solution)/shard_map/all_to_all | solution.py:36
  71.0 0.7 copy-done.1
  71.7 7.7 %attend_all.1 = (bf16[512,128]{1,0:T(8,128)(2,1)}, bf16[512,128]{1,0:T(8,128)(2,1)}, bf16[512,128]{1,0:T(8,128)(2,1)}) custom-call(s32[4]{0:T(128)} %pad_add_fusion.at_ref, bf16[2560,128]{1,0:T(8,128)(2,1)} %bitcast.76, bf16[2560,128]{1,0:T(8,128)(2,1)} %fusion.scaled_ref, f32[256,256]{1,0:T(8,128)} %get-tuple-element.14.gram_ref, ...), custom_call_target="tpu_custom_call" | custom-call | tf_op jit(solution)/shard_map/attend_all/pallas_call | solution.py:381
  79.4 11.4 %all_to_all.30 = bf16[32,16,128]{2,1,0:T(8,128)(2,1)S(1)} all-to-all(bf16[32,16,128]{2,1,0:T(8,128)(2,1)} %bitcast.93), channel_id=1, replica_groups=mesh['x'=4,'zh'=2,'zl'=4,'y'=4,'c'=2] {'x','y','c'}, dimensions={0} | all-to-all | bytes 262144 | tf_op jit(solution)/shard_map/all_to_all | solution.py:36
  90.8 1.0 pad_maximum_fusion.5
  91.8 0.8 collective-permute-start.6
  92.6 1.9 %collective-permute-start.5 = (bf16[2,2,20,256]{3,2,1,0:T(8,128)(2,1)S(1)}, bf16[2,2,20,256]{3,2,1,0:T(8,128)(2,1)S(1)}, u32[]{:S(2)}, u32[]{:S(2)}) collective-permute-start(bf16[2,2,20,256]{3,2,1,0:T(8,128)(2,1)S(1)} %get-tuple-element.26), channel_id=1, source_target_pairs={{0,6},{2,0},{4,2},{6,4},{1,7},{3,1},{5,3},{7,5},{8,14},{10,8},{12,... | collective-permute-start | bytes 122888 | tf_op jit(solution)/shard_map/ppermute | solution.py:405
  94.6 1.8 %collective-permute-done.6 = bf16[2,2,20,256]{3,2,1,0:T(8,128)(2,1)S(1)} collective-permute-done((bf16[2,2,20,256]{3,2,1,0:T(8,128)(2,1)S(1)}, bf16[2,2,20,256]{3,2,1,0:T(8,128)(2,1)S(1)}, u32[]{:S(2)}, u32[]{:S(2)}) %collective-permute-start.6) | collective-permute-done | bytes 40992 | tf_op jit(solution)/shard_map/ppermute | solution.py:405
  96.4 2.3 %collective-permute-done.7 = bf16[2,2,20,256]{3,2,1,0:T(8,128)(2,1)S(1)} collective-permute-done((bf16[2,2,20,256]{3,2,1,0:T(8,128)(2,1)S(1)}, bf16[2,2,20,256]{3,2,1,0:T(8,128)(2,1)S(1)}, u32[]{:S(2)}, u32[]{:S(2)}) %collective-permute-start.7) | collective-permute-done | bytes 40992 | tf_op jit(solution)/shard_map/ppermute | solution.py:405
  98.8 2.2 %collective-permute-start.8 = (bf16[4,2,20,256]{3,2,0,1:T(8,128)(2,1)S(1)}, bf16[4,2,20,256]{3,2,0,1:T(8,128)(2,1)S(1)}, u32[]{:S(2)}, u32[]{:S(2)}) collective-permute-start(bf16[4,2,20,256]{3,2,0,1:T(8,128)(2,1)S(1)} %get-tuple-element.35), channel_id=1, source_target_pairs={{0,1},{1,0},{2,3},{3,2},{4,5},{5,4},{6,7},{7,6},{8,9},{9,8},{10,11... | collective-permute-start | bytes 245768 | tf_op jit(solution)/shard_map/ppermute | solution.py:405
  101.6 3.3 %all-to-all-start.4 = ((bf16[8,16,128]{2,1,0:T(8,128)(2,1)}), bf16[8,16,128]{2,1,0:T(8,128)(2,1)S(1)}, u32[]{:S(2)}, u32[]{:S(2)}) async-start(bf16[8,16,128]{2,1,0:T(8,128)(2,1)} %broadcast_in_dim.15), calls=%async_computation.4 | async-start | bytes 65536 | tf_op jit(solution)/shard_map/all_to_all | solution.py:36
  105.0 6.8 %all-to-all-done.4 = bf16[8,16,128]{2,1,0:T(8,128)(2,1)S(1)} async-done(((bf16[8,16,128]{2,1,0:T(8,128)(2,1)}), bf16[8,16,128]{2,1,0:T(8,128)(2,1)S(1)}, u32[]{:S(2)}, u32[]{:S(2)}) %all-to-all-start.4) | async-done | bytes 32800 | tf_op jit(solution)/shard_map/all_to_all | solution.py:36
  112.4 4.7 %all-to-all-start.5 = ((bf16[32,16,128]{2,1,0:T(8,128)(2,1)}), bf16[32,16,128]{2,1,0:T(8,128)(2,1)S(1)}, u32[]{:S(2)}, u32[]{:S(2)}) async-start(bf16[32,16,128]{2,1,0:T(8,128)(2,1)} %broadcast_in_dim.16), calls=%async_computation.5 | async-start | bytes 262144 | tf_op jit(solution)/shard_map/all_to_all | solution.py:36
  118.0 5.6 %output_rows.1 = bf16[320,5120]{1,0:T(8,128)(2,1)} custom-call(bf16[320,128]{1,0:T(8,128)(2,1)} %conv_rows.1.f_ref, bf16[320,256]{1,0:T(8,128)(2,1)} %reshape.78.mixes_ref, bf16[128,5120]{1,0:T(8,128)(2,1)} %e_ref.5, bf16[128,5120]{1,0:T(8,128)(2,1)} %os_ref.5, bf16[128,5120]{1,0:T(8,128)(2,1)} %ot_ref.3), custom_call_target="tpu_custom_call" | custom-call | tf_op jit(solution)/shard_map/output_rows/pallas_call | solution.py:184
  123.7 1.2 all-to-all-done.5
  (49 shorter events, 7.2 us)
Async XLA Ops:
  0.6 10.5 %collective-permute-start = (bf16[2,4,40,128]{3,2,1,0:T(8,128)(2,1)}, bf16[2,4,40,128]{3,2,1,0:T(8,128)(2,1)S(1)}, u32[]{:S(2)}, u32[]{:S(2)}) collective-permute-start(bf16[2,4,40,128]{3,2,1,0:T(8,128)(2,1)} %param.10), channel_id=1, source_target_pairs={{0,1},{1,2},{2,3},{3,4},{4,5},{5,6},{6,7},{7,8},{8,9},{9,10},{10,1... | collective-permute-start | bytes 245768 | tf_op jit(solution)/shard_map/ppermute | solution.py:430
  11.1 0.6 copy-start.2
  15.4 14.3 %collective-permute-start.1 = (bf16[576,128]{1,0:T(8,128)(2,1)S(1)}, bf16[576,128]{1,0:T(8,128)(2,1)S(1)}, u32[]{:S(2)}, u32[]{:S(2)}) collective-permute-start(bf16[576,128]{1,0:T(8,128)(2,1)S(1)} %get-tuple-element.40), channel_id=1, source_target_pairs={{0,2},{2,4},{4,6},{6,0},{1,3},{3,5},{5,7},{7,1},{8,10},{10,12},{12... | collective-permute-start | bytes 442376 | tf_op jit(solution)/shard_map/ppermute | solution.py:405
  16.8 12.9 %collective-permute-start.2 = (bf16[576,128]{1,0:T(8,128)(2,1)S(1)}, bf16[576,128]{1,0:T(8,128)(2,1)S(1)}, u32[]{:S(2)}, u32[]{:S(2)}) collective-permute-start(bf16[576,128]{1,0:T(8,128)(2,1)S(1)} %get-tuple-element.41), channel_id=1, source_target_pairs={{0,4},{2,6},{4,0},{6,2},{1,5},{3,7},{5,1},{7,3},{8,12},{10,14},{12... | collective-permute-start | bytes 442376 | tf_op jit(solution)/shard_map/ppermute | solution.py:405
  19.4 10.3 %collective-permute-start.3 = (bf16[576,128]{1,0:T(8,128)(2,1)S(1)}, bf16[576,128]{1,0:T(8,128)(2,1)S(1)}, u32[]{:S(2)}, u32[]{:S(2)}) collective-permute-start(bf16[576,128]{1,0:T(8,128)(2,1)S(1)} %get-tuple-element.42), channel_id=1, source_target_pairs={{0,6},{2,0},{4,2},{6,4},{1,7},{3,1},{5,3},{7,5},{8,14},{10,8},{12,... | collective-permute-start | bytes 442376 | tf_op jit(solution)/shard_map/ppermute | solution.py:405
  24.7 14.6 %all-to-all-start = ((bf16[32,40,128]{2,1,0:T(8,128)(2,1)}), bf16[32,40,128]{2,1,0:T(8,128)(2,1)S(1)}, u32[]{:S(2)}, u32[]{:S(2)}) async-start(bf16[32,40,128]{2,1,0:T(8,128)(2,1)} %bitcast.91), calls=%async_computation | async-start | bytes 655360 | tf_op jit(solution)/shard_map/all_to_all | solution.py:36
  29.9 31.3 %collective-permute-start.4 = (bf16[4,448,128]{2,1,0:T(8,128)(2,1)S(1)}, bf16[4,448,128]{2,1,0:T(8,128)(2,1)S(1)}, u32[]{:S(2)}, u32[]{:S(2)}) collective-permute-start(bf16[4,448,128]{2,1,0:T(8,128)(2,1)S(1)} %pad_maximum_fusion.2), channel_id=1, source_target_pairs={{0,1},{1,0},{2,3},{3,2},{4,5},{5,4},{6,7},{7,6},{8,9},{9,8},{10,11... | collective-permute-start | bytes 1376264 | tf_op jit(solution)/shard_map/ppermute | solution.py:405
  40.0 15.1 %all-to-all-start.1 = ((bf16[8,40,128]{2,1,0:T(8,128)(2,1)}), bf16[8,40,128]{2,1,0:T(8,128)(2,1)S(1)}, u32[]{:S(2)}, u32[]{:S(2)}) async-start(bf16[8,40,128]{2,1,0:T(8,128)(2,1)} %broadcast_in_dim.13), calls=%async_computation.1 | async-start | bytes 163840 | tf_op jit(solution)/shard_map/all_to_all | solution.py:36
  56.0 15.0 %all-to-all-start.2 = ((bf16[32,40,128]{2,1,0:T(8,128)(2,1)}), bf16[32,40,128]{2,1,0:T(8,128)(2,1)S(1)}, u32[]{:S(2)}, u32[]{:S(2)}) async-start(bf16[32,40,128]{2,1,0:T(8,128)(2,1)} %broadcast_in_dim.14), calls=%async_computation.2 | async-start | bytes 655360 | tf_op jit(solution)/shard_map/all_to_all | solution.py:36
  61.4 3.7 %copy-start = (bf16[8,320,128]{2,1,0:T(8,128)(2,1)}, bf16[8,320,128]{2,1,0:T(8,128)(2,1)S(1)}, u32[]{:S(2)}) copy-start(bf16[8,320,128]{2,1,0:T(8,128)(2,1)S(1)} %pad_maximum_fusion) | copy-start | bytes 1966084
  71.0 0.7 copy-start.1
  91.8 4.5 %collective-permute-start.6 = (bf16[2,2,20,256]{3,2,1,0:T(8,128)(2,1)S(1)}, bf16[2,2,20,256]{3,2,1,0:T(8,128)(2,1)S(1)}, u32[]{:S(2)}, u32[]{:S(2)}) collective-permute-start(bf16[2,2,20,256]{3,2,1,0:T(8,128)(2,1)S(1)} %get-tuple-element.25), channel_id=1, source_target_pairs={{0,4},{2,6},{4,0},{6,2},{1,5},{3,7},{5,1},{7,3},{8,12},{10,14},{12... | collective-permute-start | bytes 122888 | tf_op jit(solution)/shard_map/ppermute | solution.py:405
  92.6 3.8 %collective-permute-start.5 = (bf16[2,2,20,256]{3,2,1,0:T(8,128)(2,1)S(1)}, bf16[2,2,20,256]{3,2,1,0:T(8,128)(2,1)S(1)}, u32[]{:S(2)}, u32[]{:S(2)}) collective-permute-start(bf16[2,2,20,256]{3,2,1,0:T(8,128)(2,1)S(1)} %get-tuple-element.26), channel_id=1, source_target_pairs={{0,6},{2,0},{4,2},{6,4},{1,7},{3,1},{5,3},{7,5},{8,14},{10,8},{12,... | collective-permute-start | bytes 122888 | tf_op jit(solution)/shard_map/ppermute | solution.py:405
  94.6 4.2 %collective-permute-start.7 = (bf16[2,2,20,256]{3,2,1,0:T(8,128)(2,1)S(1)}, bf16[2,2,20,256]{3,2,1,0:T(8,128)(2,1)S(1)}, u32[]{:S(2)}, u32[]{:S(2)}) collective-permute-start(bf16[2,2,20,256]{3,2,1,0:T(8,128)(2,1)S(1)} %get-tuple-element.27), channel_id=1, source_target_pairs={{0,2},{2,4},{4,6},{6,0},{1,3},{3,5},{5,7},{7,1},{8,10},{10,12},{12... | collective-permute-start | bytes 122888 | tf_op jit(solution)/shard_map/ppermute | solution.py:405
  98.8 18.3 %collective-permute-start.8 = (bf16[4,2,20,256]{3,2,0,1:T(8,128)(2,1)S(1)}, bf16[4,2,20,256]{3,2,0,1:T(8,128)(2,1)S(1)}, u32[]{:S(2)}, u32[]{:S(2)}) collective-permute-start(bf16[4,2,20,256]{3,2,0,1:T(8,128)(2,1)S(1)} %get-tuple-element.35), channel_id=1, source_target_pairs={{0,1},{1,0},{2,3},{3,2},{4,5},{5,4},{6,7},{7,6},{8,9},{9,8},{10,11... | collective-permute-start | bytes 245768 | tf_op jit(solution)/shard_map/ppermute | solution.py:405
  101.6 10.1 %all-to-all-start.4 = ((bf16[8,16,128]{2,1,0:T(8,128)(2,1)}), bf16[8,16,128]{2,1,0:T(8,128)(2,1)S(1)}, u32[]{:S(2)}, u32[]{:S(2)}) async-start(bf16[8,16,128]{2,1,0:T(8,128)(2,1)} %broadcast_in_dim.15), calls=%async_computation.4 | async-start | bytes 65536 | tf_op jit(solution)/shard_map/all_to_all | solution.py:36
  112.4 12.5 %all-to-all-start.5 = ((bf16[32,16,128]{2,1,0:T(8,128)(2,1)}), bf16[32,16,128]{2,1,0:T(8,128)(2,1)S(1)}, u32[]{:S(2)}, u32[]{:S(2)}) async-start(bf16[32,16,128]{2,1,0:T(8,128)(2,1)} %broadcast_in_dim.16), calls=%async_computation.5 | async-start | bytes 262144 | tf_op jit(solution)/shard_map/all_to_all | solution.py:36
  118.0 6.9 %copy-start.3 = (bf16[20,128]{1,0:T(8,128)(2,1)S(1)}, bf16[20,128]{1,0:T(8,128)(2,1)}, u32[]{:S(2)}) copy-start(bf16[20,128]{1,0:T(8,128)(2,1)} %get-tuple-element.21) | copy-start | bytes 15364
  118.0 7.3 %copy-start.4 = (f32[20,384]{1,0:T(8,128)S(1)}, f32[20,384]{1,0:T(8,128)}, u32[]{:S(2)}) copy-start(f32[20,384]{1,0:T(8,128)} %get-tuple-element.23) | copy-start | bytes 92164

commit v5 on v4

--- a/solution.py
+++ b/solution.py
@@ -196,32 +196,46 @@
     )(feats, mixes, embed, out_s, out_t)
 
 
-def maps_kernel(at_ref, ws_ref, wt_ref, e_ref, os_ref, gs_ref, gt_ref, maps_ref, e_mine_ref, g_mine_ref):
+def maps_kernel(
+    at_ref, ws_ref, wt_ref, e_ref, os_ref, gs_ref, gt_ref,
+    maps_ref, e_mine_ref, g_mine_ref, factors, gains, arrived,
+):
     rows, triple = ws_ref.shape
-    head, wide = e_ref.shape
+    head = e_ref.shape[0]
+    wide = factors.shape[1]
+    cols = pl.ds(pl.multiple_of(at_ref[0] * wide, 128), wide)
+    copies = [
+        pltpu.make_async_copy(e_ref.at[:, cols], factors.at[pl.ds(0, head)], arrived.at[0]),
+        pltpu.make_async_copy(os_ref.at[:, cols], factors.at[pl.ds(head, head)], arrived.at[1]),
+        pltpu.make_async_copy(gs_ref.at[:, cols], gains.at[0], arrived.at[2]),
+        pltpu.make_async_copy(gt_ref.at[:, cols], gains.at[1], arrived.at[3]),
+    ]
+    for copy in copies:
+        copy.start()
     first = at_ref[1] * rows
     r = lax.broadcasted_iota(jnp.int32, (rows, wide), 0)
     c = lax.broadcasted_iota(jnp.int32, (rows, wide), 1)
     chosen = jnp.where(c == r + first, 1.0, 0.0)
     pick = chosen.astype(bf16)
-    e = e_ref[...]
-    e32 = e.astype(f32)
-    o32 = os_ref[...].astype(f32)
-
-    def product(weight, scaled):
-        placed = tn(weight, pick).astype(bf16)
+    placed_s = tn(ws_ref[...], pick).astype(bf16)
+    placed_t = tn(wt_ref[...], pick).astype(bf16)
+    maps_ref[3 * triple :] = jnp.zeros((maps_ref.shape[0] - 3 * triple, head), bf16)
+    for copy in copies:
+        copy.wait()
+
+    def product(placed, scaled):
         high = scaled.astype(bf16)
         low = (scaled - high.astype(f32)).astype(bf16)
         return nt(placed, high) + nt(placed, low)
 
-    gs = gs_ref[...]
-    gt = gt_ref[...]
-    maps_ref[:triple] = product(ws_ref[...], e32 * gs).astype(bf16)
-    later = product(wt_ref[...], jnp.concatenate([e32, o32], axis=0) * gt)
+    gs = gains[0]
+    gt = gains[1]
+    both = factors[...].astype(f32)
+    maps_ref[:triple] = product(placed_s, both[:head] * gs).astype(bf16)
+    later = product(placed_t, both * gt)
     maps_ref[triple : 2 * triple] = later[:, :head].astype(bf16)
     maps_ref[2 * triple : 3 * triple] = later[:, head:].astype(bf16)
-    maps_ref[3 * triple :] = jnp.zeros((maps_ref.shape[0] - 3 * triple, head), bf16)
-    e_mine_ref[...] = nt(pick, e).astype(bf16)
+    e_mine_ref[...] = nt(pick, factors[:head]).astype(bf16)
     g_mine_ref[...] = jnp.broadcast_to(jnp.sum(chosen * gs, axis=1, keepdims=True), g_mine_ref.shape)
 
 
@@ -229,23 +243,69 @@
     rows, triple = w_s.shape
     head, width = embed.shape
     wide = width // lax.axis_size(DP[0]) // lax.axis_size(DP[1])
-    full = lambda r, c: pl.BlockSpec((r, c), lambda i, at: (0, 0))
-    cut = lambda r: pl.BlockSpec((r, wide), lambda i, at: (0, at[0]))
+    hbm = pl.BlockSpec(memory_space=pl.ANY)
+    vmem = pl.BlockSpec(memory_space=pltpu.VMEM)
     return pl.pallas_call(
         maps_kernel,
-        grid_spec=pltpu.PrefetchScalarGridSpec(
-            num_scalar_prefetch=1,
-            grid=(1,),
-            in_specs=[full(rows, triple), full(rows, triple), cut(head), cut(head), cut(1), cut(1)],
-            out_specs=[full(padded, head), full(rows, head), full(rows, triple)],
-        ),
+        in_specs=[pl.BlockSpec(memory_space=pltpu.SMEM), vmem, vmem, hbm, hbm, hbm, hbm],
+        out_specs=[vmem, vmem, vmem],
         out_shape=[
             jax.ShapeDtypeStruct((padded, head), bf16),
             jax.ShapeDtypeStruct((rows, head), bf16),
             jax.ShapeDtypeStruct((rows, triple), f32),
         ],
+        scratch_shapes=[
+            pltpu.VMEM((2 * head, wide), bf16),
+            pltpu.VMEM((2, 1, wide), f32),
+            pltpu.SemaphoreType.DMA((4,)),
+        ],
         name="local_maps",
     )(at, w_s, w_t, embed, out_s, gain_s.reshape(1, width), gain_t.reshape(1, width))
+
+
+def norm_kernel(at_ref, held_ref, one_ref, two_ref, three_ref, other_ref, gram_ref, flat_ref, scaled_ref, cots_ref):
+    head = flat_ref.shape[1]
+    kinds, span = cots_ref.shape[2], cots_ref.shape[3]
+    tokens = other_ref.shape[1] - kinds * span
+    gram = gram_ref[:head, :head]
+    first = gram.astype(bf16)
+    rest = gram - first.astype(f32)
+    second = rest.astype(bf16)
+    third = (rest - second.astype(f32)).astype(bf16)
+    kept = pl.multiple_of(tokens + at_ref[3] * (kinds * span), 16)
+    near = (held_ref, one_ref, two_ref, three_ref)
+    for side in range(2):
+        for step in range(4):
+            x = near[step][:tokens] if side == 0 else other_ref[step, :tokens]
+            xg = nn(x, first) + (nn(x, second) + nn(x, third))
+            wide = x.astype(f32)
+            factor = lax.rsqrt(jnp.sum(xg * wide, axis=-1, keepdims=True) + epsilon)
+            to = (side * 4 + step) * tokens
+            flat_ref[to : to + tokens] = x
+            scaled_ref[to : to + tokens] = (wide * factor).astype(bf16)
+            if side == 0:
+                got = near[step][pl.ds(kept, kinds * span)]
+            else:
+                got = other_ref[step, tokens:]
+            for kind in range(kinds):
+                cots_ref[side, step, kind] = got[kind * span : (kind + 1) * span]
+
+
+def norm_rows(at, near, other, gram, span):
+    n_line, rows, head = other.shape
+    tokens = rows - 2 * span
+    vmem = pl.BlockSpec(memory_space=pltpu.VMEM)
+    return pl.pallas_call(
+        norm_kernel,
+        in_specs=[pl.BlockSpec(memory_space=pltpu.SMEM)] + [vmem] * 6,
+        out_specs=[vmem] * 3,
+        out_shape=[
+            jax.ShapeDtypeStruct((2 * n_line * tokens, head), bf16),
+            jax.ShapeDtypeStruct((2 * n_line * tokens, head), bf16),
+            jax.ShapeDtypeStruct((2, n_line, 2, span, head), bf16),
+        ],
+        name="norm_rows",
+    )(at, *near, other, gram)
 
 
 def group_size(axes):
@@ -275,7 +335,7 @@
 
 def attend_kernel(
     at_ref, flat_ref, scaled_ref, gram_ref, cots_ref, maps_ref,
-    total_ref, mix_ref, mix_t_ref, qkv_ref, att_ref, dkv_ref, up_ref, score_ref, rounded_ref, slope_ref,
+    total_ref, back_ref, mix_ref, qkv_ref, att_ref, dkv_ref, up_ref, score_ref, rounded_ref, slope_ref,
 ):
     frames = FR
     head = flat_ref.shape[1]
@@ -284,7 +344,7 @@
     triple = 3 * head
     own = frames * pad
     scale = head**-0.5
-    line, core, slot, spots = at_ref[0], at_ref[1], at_ref[2], at_ref[3]
+    line, core, slot, spots = at_ref[2], at_ref[3], at_ref[4], at_ref[5]
 
     qkv_ref[...] = nt(scaled_ref[...], maps_ref[:triple]).astype(bf16)
     r = lax.broadcasted_iota(jnp.int32, (pad, places), 0)
@@ -339,7 +399,12 @@
     allowed = (row_spot == col_spot) & (row_frame >= col_frame)
     att = softmax_rows(jnp.where(allowed, nt(q, k) * scale, masked))
     rounded = att.astype(bf16)
-    mix_t_ref[...] = nn(rounded, v).astype(bf16)
+    mix_t = nn(rounded, v).astype(bf16)
+    span = back_ref.shape[2]
+    for side in range(2):
+        for step in range(4):
+            mine = slice((side * 4 + step) * span, (side * 4 + step + 1) * span)
+            back_ref[step, side] = jnp.concatenate([mix[mine], mix_t[mine]], axis=1)
     d_att = nt(g, v)
     d_sc = (att * (d_att - jnp.sum(d_att * att, axis=-1, keepdims=True))).astype(bf16)
     d_packed = jnp.concatenate(
@@ -381,13 +446,13 @@
     return pl.pallas_call(
         attend_kernel,
         in_specs=[pl.BlockSpec(memory_space=pltpu.SMEM)] + [vmem] * 5,
-        out_specs=[vmem] * 3,
+        out_specs=[vmem] * 2,
         out_shape=[
             jax.ShapeDtypeStruct((4 * head, head), bf16),
-            jax.ShapeDtypeStruct((own, head), bf16),
-            jax.ShapeDtypeStruct((own, head), bf16),
+            jax.ShapeDtypeStruct((4, 2, own // 8, 2 * head), bf16),
         ],
         scratch_shapes=[
+            pltpu.VMEM((own, head), bf16),
             pltpu.VMEM((rows, 3 * head), bf16),
             pltpu.VMEM((own, places), f32),
             pltpu.VMEM((rows, 2 * head), bf16),
@@ -421,15 +486,19 @@
     places = height * columns
     tokens = frames * places
     head, width = embed_weight.shape
-    exact = dict(precision=lax.Precision.HIGHEST)
     n_ts = group_size(TS)
     n_clip = group_size(CLIP)
     spots = places // n_clip
-    clip_tokens = FR * places
 
     prior = lax.ppermute(clip_video, TS, [(i, i + 1) for i in range(n_ts - 1)])
 
-    at = jnp.stack([lax.axis_index(DP), lax.axis_index(TS)]).astype(jnp.int32)
+    n_line = lax.axis_size("y")
+    line = lax.axis_index("y")
+    core = lax.axis_index("c")
+    pad = 32
+    at = jnp.stack(
+        [lax.axis_index(DP), lax.axis_index(TS), line, core, lax.axis_index(CLIP) * spots, jnp.int32(spots)]
+    ).astype(jnp.int32)
     maps, e_mine, g_mine = local_maps(
         at, input_spatial, input_temporal, embed_weight, output_spatial, gain_spatial, gain_temporal, 10 * head
     )
@@ -438,10 +507,6 @@
     feats_home = conv_rows(
         prior.reshape(tokens, channels), clip_video.reshape(tokens, channels), conv_weight
     )
-    n_line = lax.axis_size("y")
-    line = lax.axis_index("y")
-    core = lax.axis_index("c")
-    pad = 32
     gram, cots = products(
         embed_weight,
         output_spatial,
@@ -461,35 +526,29 @@
     moved = []
     for step in range(1, n_line):
         moved.append(turned(held[step], "y", step))
-    held = jnp.stack([held[0]] + moved)
-    feats_near = held[:, :tokens]
-    cots_near = held[:, tokens:].reshape(n_line, 2, 2 * frames * pad, head)
-    keep = lax.dynamic_index_in_dim(cots_near, core, 1, keepdims=False)
-    give = lax.dynamic_index_in_dim(cots_near, 1 - core, 1, keepdims=False)
-    other = turned(jnp.concatenate([feats_near, give], axis=1), "c", 1)
-    flat = jnp.concatenate([feats_near, other[:, :tokens]], axis=0).reshape(clip_tokens, head)
-    cots = jnp.stack([keep, other[:, tokens:]]).reshape(2, n_line, 2, frames * pad, head)
-    wide = flat.astype(f32)
-    square = jnp.sum(nn(wide, gram[:head, :head], **exact) * wide, axis=-1, keepdims=True)
-    scaled = (wide * lax.rsqrt(square + epsilon)).astype(bf16)
-
-    place = jnp.stack([line, core, lax.axis_index(CLIP) * spots, jnp.int32(spots)]).astype(jnp.int32)
-    total, mix, mix_t = attend_all(place, flat, scaled, gram, cots, maps, pad)
-
-    share = scattered(total)
-    share, mix, mix_t = lax.optimization_barrier((share, mix, mix_t))
-    total = gathered(share, total.shape)
+    near = [held[0]] + moved
+    span = frames * pad
+    give = tokens + (1 - core) * 2 * span
+    payload = [
+        jnp.concatenate([part[:tokens], lax.dynamic_slice_in_dim(part, give, 2 * span, 0)], axis=0)
+        for part in near
+    ]
+    other = turned(jnp.stack(payload), "c", 1)
+    flat, scaled, cots = norm_rows(at, near, other, gram, span)
+
+    total, back = attend_all(at, flat, scaled, gram, cots, maps, pad)
+    total = gathered(scattered(total), total.shape)
     grad = jnp.concatenate([nn(e_mine, total[b * head : (b + 1) * head]) for b in range(3)], axis=1) * g_mine
 
-    back = jnp.concatenate([mix, mix_t], axis=-1).reshape(2, n_line, frames, pad, 2 * head)[:, :, :, :spots]
     moved = []
     for step in range(1, n_line):
-        moved.append(turned(back[:, step], "y", -step))
-    back = jnp.stack([back[:, 0]] + moved)
+        moved.append(turned(back[step], "y", -step))
+    back = jnp.stack([back[0]] + moved)
     away = turned(back[:, 1], "c", 1)
     home = jnp.stack([back[:, 0], away], axis=1)
     home = jnp.where(core == 0, home, home[:, ::-1])
     home = lax.dynamic_slice_in_dim(jnp.concatenate([home, home], axis=0), (n_line - line) % n_line, n_line, 0)
+    home = home.reshape(n_line, 2, frames, pad, 2 * head)[:, :, :, :spots]
     home = home.transpose(2, 0, 1, 3, 4).reshape(tokens, 2 * head)
     layer = output_rows(feats_home, home, embed_weight, output_spatial, output_temporal)
     return (layer.reshape(frames, height, columns, width), grad)

time: 127 us -> 126 us (level)
  starting transfers between devices: 40.7 us -> 52.8 us
  blocking collectives: 11.4 us -> 0 us
  waiting for transfers between devices: 33.8 us -> 31 us
  Pallas kernels: 24.8 us -> 27.5 us
  other arithmetic: 6.28 us -> 3.65 us
  local copies, waits for them, and re-layouts: 5.92 us -> 8.25 us
  matrix products: 2.06 us -> 0.39 us
    all_to_all x5 -> x6, starting transfers between devices: 26.1 us -> 38 us  [exchange(): return lax.all_to_all(parts, axes, 0, 0, tiled=True)]
    all_to_all x1 -> x0, blocking collectives: 11.4 us -> none  [exchange(): return lax.all_to_all(parts, axes, 0, 0, tiled=True)]
    all_to_all x5 -> x6, waiting for transfers between devices: 29.6 us -> 25.4 us  [exchange(): return lax.all_to_all(parts, axes, 0, 0, tiled=True)]
    pallas_call x1 -> x2, Pallas kernels: 3.97 us -> 6.64 us  [the longest x1 3.49 us: local_maps(): pl.pallas_call(maps_kernel, in_specs=[pl.BlockSpec(memory_space=pltpu.SME...]
    another operation x6, other arithmetic: 2.98 us -> 1.02 us  [the longest x5 0.99 us: shards(): other = turned(jnp.stack(payload), 'c', 1)]
    dot_general x4 -> x3, matrix products: 2.06 us -> 0.39 us  [nn(): lax.dot_general(a, b, (((1,), (0,)), ((), ())), preferred_element_type=f3...]
    ppermute x8, waiting for transfers between devices: 4.16 us -> 5.64 us  [turned(): return lax.ppermute(value, axis, [(i, (i + step) % n) for i in range(n)])]
  transfers between devices with their start and end apart: 14 -> 15, of which waited for: 7 -> 7; matrix products, arithmetic and copies ran while one was open for 8% -> 6% of each run, Pallas kernels for 11% -> 16%
where the time goes in v5:
time: 126 us; the launch traced here: 125 us
  starting transfers between devices  52.8 us (42%)
  waiting for transfers between devices  31 us (25%)
  Pallas kernels  27.5 us (22%)
  local copies, waits for them, and re-layouts  8.25 us (7%)
  other arithmetic  3.65 us (3%)
    all_to_all x6, starting transfers between devices, exchange(): return lax.all_to_all(parts, axes, 0, 0, tiled=True)  38 us
    all_to_all x6, waiting for transfers between devices, exchange(): return lax.all_to_all(parts, axes, 0, 0, tiled=True)  25.4 us
    ppermute x8, starting transfers between devices, turned(): return lax.ppermute(value, axis, [(i, (i + step) % n) for i in range(n)])  10.2 us
    pallas_call x1, Pallas kernels, attend_all(): pl.pallas_call(attend_kernel, in_specs=[pl.BlockSpec(memory_space=pltpu.S...  7.66 us
    pallas_call x1, Pallas kernels, output_rows(): pl.pallas_call(output_kernel, in_specs=[vmem, vmem, hbm, hbm, hbm], out_s...  5.64 us
    ppermute x8, waiting for transfers between devices, turned(): return lax.ppermute(value, axis, [(i, (i + step) % n) for i in range(n)])  5.64 us
    pallas_call x1, Pallas kernels, products(): pl.pallas_call(products_kernel, in_specs=[hbm] * 4, out_specs=[vmem, vmem...  4.83 us
    ppermute x1, starting transfers between devices, shards(): prior = lax.ppermute(clip_video, TS, [(i, i + 1) for i in range(n_ts - 1)])  4.59 us
  transfers between devices with their start and end apart: 15, of which 7 were waited for; matrix products, arithmetic and copies ran while one was open for 6% of the time, Pallas kernels for 16%

profile of v5, /device:TPU:1, one launch (start us, length us, event | category | flops | bytes accessed | tf_op | source)
XLA Modules:
  0.0 124.7 jit_solution(10379464132221291428)
XLA Ops:
  0.6 4.6 %collective-permute-start = (bf16[2,4,40,128]{3,2,1,0:T(8,128)(2,1)}, bf16[2,4,40,128]{3,2,1,0:T(8,128)(2,1)S(1)}, u32[]{:S(2)}, u32[]{:S(2)}) collective-permute-start(bf16[2,4,40,128]{3,2,1,0:T(8,128)(2,1)} %param.10), channel_id=1, source_target_pairs={{0,1},{1,2},{2,3},{3,4},{4,5},{5,6},{6,7},{7,8},{8,9},{9,10},{10,1... | collective-permute-start | bytes 245768 | tf_op jit(solution)/shard_map/ppermute | solution.py:493
  5.9 3.5 %local_maps.1 = (bf16[1280,128]{1,0:T(8,128)(2,1)}, bf16[20,128]{1,0:T(8,128)(2,1)}, f32[20,384]{1,0:T(8,128)}) custom-call(s32[6]{0:T(128)} %stack.56.at_ref, bf16[20,384]{1,0:T(8,128)(2,1)} %ws_ref.1, bf16[20,384]{1,0:T(8,128)(2,1)} %wt_ref.1, bf16[128,5120]{1,0:T(8,128)(2,1)} %e_ref.5, bf16[128,5120]{1,0:T(8,128)(2,1)} %os_ref.5, f32[1,5120]{1,0:T(1,128)} %bitcast.75, ...), custom_call_target="tpu_custom_call" | custom-call | tf_op jit(solution)/shard_map/local_maps/pallas_call | solution.py:248
  9.4 7.0 %all-to-all-start = ((bf16[32,40,128]{2,1,0:T(8,128)(2,1)}), bf16[32,40,128]{2,1,0:T(8,128)(2,1)S(1)}, u32[]{:S(2)}, u32[]{:S(2)}) async-start(bf16[32,40,128]{2,1,0:T(8,128)(2,1)} %bitcast.63), calls=%async_computation | async-start | bytes 655360 | tf_op jit(solution)/shard_map/all_to_all | solution.py:36
  16.5 4.8 %products.1 = (f32[256,256]{1,0:T(8,128)}, bf16[8,2,2,32,128]{4,3,2,1,0:T(8,128)(2,1)}) custom-call(bf16[128,5120]{1,0:T(8,128)(2,1)} %e_ref.5, bf16[128,5120]{1,0:T(8,128)(2,1)} %os_ref.5, bf16[128,5120]{1,0:T(8,128)(2,1)} %ot_ref.3, bf16[320,5120]{1,0:T(8,128)(2,1)} %bitcast.58), custom_call_target="tpu_custom_call" | custom-call | tf_op jit(solution)/shard_map/products/pallas_call | solution.py:133
  21.4 1.0 dynamic-slice_bitcast_fusion
  23.0 2.7 %conv_rows.1.f_ref = bf16[320,128]{1,0:T(8,128)(2,1)} custom-call(bf16[320,128]{1,0:T(8,128)(2,1)} %bitcast.71, bf16[320,128]{1,0:T(8,128)(2,1)} %bitcast.70, bf16[9,384,128]{2,1,0:T(8,128)(2,1)} %bitcast.61), custom_call_target="tpu_custom_call" | custom-call | tf_op jit(solution)/shard_map/conv_rows/pallas_call | solution.py:78
  25.7 1.6 %pad_maximum_fusion.3 = (bf16[576,128]{1,0:T(8,128)(2,1)S(1)}, bf16[576,128]{1,0:T(8,128)(2,1)S(1)}, bf16[576,128]{1,0:T(8,128)(2,1)S(1)}, bf16[576,128]{1,0:T(8,128)(2,1)}) fusion(bf16[320,128]{1,0:T(8,128)(2,1)} %conv_rows.1.f_ref, bf16[256,128]{1,0:T(8,128)(2,1)S(1)} %get-tuple-element.28, bf16[256,128]{1,0:T(8,128)(2,1)S(1)} %get-tuple-element.30, ...), kind=kLoop, calls=%fused_computation.8 | loop fusion | flops 958464 | bytes 933888 | tf_op jit(solution)/shard_map/concatenate | solution.py:521
  27.3 2.6 %collective-permute-start.3 = (bf16[576,128]{1,0:T(8,128)(2,1)S(1)}, bf16[576,128]{1,0:T(8,128)(2,1)S(1)}, u32[]{:S(2)}, u32[]{:S(2)}) collective-permute-start(bf16[576,128]{1,0:T(8,128)(2,1)S(1)} %get-tuple-element.35), channel_id=1, source_target_pairs={{0,6},{2,0},{4,2},{6,4},{1,7},{3,1},{5,3},{7,5},{8,14},{10,8},{12,... | collective-permute-start | bytes 442376 | tf_op jit(solution)/shard_map/ppermute | solution.py:470
  30.0 0.9 maximum_bitcast_fusion
  30.9 1.7 %collective-permute-start.2 = (bf16[576,128]{1,0:T(8,128)(2,1)S(1)}, bf16[576,128]{1,0:T(8,128)(2,1)S(1)}, u32[]{:S(2)}, u32[]{:S(2)}) collective-permute-start(bf16[576,128]{1,0:T(8,128)(2,1)S(1)} %get-tuple-element.37), channel_id=1, source_target_pairs={{0,4},{2,6},{4,0},{6,2},{1,5},{3,7},{5,1},{7,3},{8,12},{10,14},{12... | collective-permute-start | bytes 442376 | tf_op jit(solution)/shard_map/ppermute | solution.py:470
  32.7 4.1 %collective-permute-done.1.one_ref = bf16[576,128]{1,0:T(8,128)(2,1)S(1)} collective-permute-done((bf16[576,128]{1,0:T(8,128)(2,1)S(1)}, bf16[576,128]{1,0:T(8,128)(2,1)S(1)}, u32[]{:S(2)}, u32[]{:S(2)}) %collective-permute-start.1) | collective-permute-done | bytes 147488 | tf_op jit(solution)/shard_map/ppermute | solution.py:470
  36.8 1.5 %collective-permute-done.2.two_ref = bf16[576,128]{1,0:T(8,128)(2,1)S(1)} collective-permute-done((bf16[576,128]{1,0:T(8,128)(2,1)S(1)}, bf16[576,128]{1,0:T(8,128)(2,1)S(1)}, u32[]{:S(2)}, u32[]{:S(2)}) %collective-permute-start.2) | collective-permute-done | bytes 147488 | tf_op jit(solution)/shard_map/ppermute | solution.py:470
  39.1 8.1 %all-to-all-start.1 = ((bf16[8,40,128]{2,1,0:T(8,128)(2,1)}), bf16[8,40,128]{2,1,0:T(8,128)(2,1)S(1)}, u32[]{:S(2)}, u32[]{:S(2)}) async-start(bf16[8,40,128]{2,1,0:T(8,128)(2,1)} %broadcast_in_dim.12), calls=%async_computation.1 | async-start | bytes 163840 | tf_op jit(solution)/shard_map/all_to_all | solution.py:36
  47.3 2.7 %collective-permute-start.4 = (bf16[4,448,128]{2,1,0:T(8,128)(2,1)S(1)}, bf16[4,448,128]{2,1,0:T(8,128)(2,1)S(1)}, u32[]{:S(2)}, u32[]{:S(2)}) collective-permute-start(bf16[4,448,128]{2,1,0:T(8,128)(2,1)S(1)} %pad_maximum_fusion), channel_id=1, source_target_pairs={{0,1},{1,0},{2,3},{3,2},{4,5},{5,4},{6,7},{7,6},{8,9},{9,8},{10,11... | collective-permute-start | bytes 1376264 | tf_op jit(solution)/shard_map/ppermute | solution.py:470
  50.0 4.6 %all-to-all-done.1 = bf16[8,40,128]{2,1,0:T(8,128)(2,1)S(1)} async-done(((bf16[8,40,128]{2,1,0:T(8,128)(2,1)}), bf16[8,40,128]{2,1,0:T(8,128)(2,1)S(1)}, u32[]{:S(2)}, u32[]{:S(2)}) %all-to-all-start.1) | async-done | bytes 81952 | tf_op jit(solution)/shard_map/all_to_all | solution.py:36
  54.6 0.8 broadcast_in_dim.13
  55.4 8.6 %all-to-all-start.2 = ((bf16[32,40,128]{2,1,0:T(8,128)(2,1)}), bf16[32,40,128]{2,1,0:T(8,128)(2,1)S(1)}, u32[]{:S(2)}, u32[]{:S(2)}) async-start(bf16[32,40,128]{2,1,0:T(8,128)(2,1)} %broadcast_in_dim.13), calls=%async_computation.2 | async-start | bytes 655360 | tf_op jit(solution)/shard_map/all_to_all | solution.py:36
  64.0 0.8 copy-done.4
  64.8 3.2 %norm_rows.1 = (bf16[2560,128]{1,0:T(8,128)(2,1)}, bf16[2560,128]{1,0:T(8,128)(2,1)}, bf16[2,4,2,64,128]{4,3,2,1,0:T(8,128)(2,1)}) custom-call(s32[6]{0:T(128)} %stack.56.at_ref, bf16[576,128]{1,0:T(8,128)(2,1)} %get-tuple-element.38.held_ref, bf16[576,128]{1,0:T(8,128)(2,1)} %copy-done.2, bf16[576,128]{1,0:T(8,128)(2,1)} %copy-done.3, ...), custom_call_target="tpu_custom_call" | custom-call | tf_op jit(solution)/shard_map/norm_rows/pallas_call | solution.py:298
  67.9 5.7 %all-to-all-done.2 = bf16[32,40,128]{2,1,0:T(8,128)(2,1)S(1)} async-done(((bf16[32,40,128]{2,1,0:T(8,128)(2,1)}), bf16[32,40,128]{2,1,0:T(8,128)(2,1)S(1)}, u32[]{:S(2)}, u32[]{:S(2)}) %all-to-all-start.2) | async-done | bytes 327712 | tf_op jit(solution)/shard_map/all_to_all | solution.py:36
  73.6 0.7 copy-done
  74.3 7.7 %attend_all.1 = (bf16[512,128]{1,0:T(8,128)(2,1)}, bf16[4,2,64,256]{3,2,1,0:T(8,128)(2,1)}) custom-call(s32[6]{0:T(128)} %stack.56.at_ref, bf16[2560,128]{1,0:T(8,128)(2,1)} %get-tuple-element.14.flat_ref, bf16[2560,128]{1,0:T(8,128)(2,1)} %get-tuple-element.15.scaled_ref, f32[256,256]{1,0:T(8,128)} %get-tuple-element.13.gram_ref, ...), custom_call_target="tpu_custom_call" | custom-call | tf_op jit(solution)/shard_map/attend_all/pallas_call | solution.py:446
  82.0 1.0 fusion.2
  83.2 2.0 %collective-permute-start.6 = (bf16[2,64,256]{2,1,0:T(8,128)(2,1)S(1)}, bf16[2,64,256]{2,1,0:T(8,128)(2,1)S(1)}, u32[]{:S(2)}, u32[]{:S(2)}) collective-permute-start(bf16[2,64,256]{2,1,0:T(8,128)(2,1)S(1)} %get-tuple-element.26), channel_id=1, source_target_pairs={{0,4},{2,6},{4,0},{6,2},{1,5},{3,7},{5,1},{7,3},{8,12},{10,14},{12... | collective-permute-start | bytes 196616 | tf_op jit(solution)/shard_map/ppermute | solution.py:470
  85.7 5.9 %all-to-all-start.3 = ((bf16[32,16,128]{2,1,0:T(8,128)(2,1)}), bf16[32,16,128]{2,1,0:T(8,128)(2,1)S(1)}, u32[]{:S(2)}, u32[]{:S(2)}) async-start(bf16[32,16,128]{2,1,0:T(8,128)(2,1)} %bitcast.65), calls=%async_computation.3 | async-start | bytes 262144 | tf_op jit(solution)/shard_map/all_to_all | solution.py:36
  92.0 7.2 %all-to-all-done.3 = bf16[32,16,128]{2,1,0:T(8,128)(2,1)S(1)} async-done(((bf16[32,16,128]{2,1,0:T(8,128)(2,1)}), bf16[32,16,128]{2,1,0:T(8,128)(2,1)S(1)}, u32[]{:S(2)}, u32[]{:S(2)}) %all-to-all-start.3) | async-done | bytes 131104 | tf_op jit(solution)/shard_map/all_to_all | solution.py:36
  99.9 3.3 %all-to-all-start.4 = ((bf16[8,16,128]{2,1,0:T(8,128)(2,1)}), bf16[8,16,128]{2,1,0:T(8,128)(2,1)S(1)}, u32[]{:S(2)}, u32[]{:S(2)}) async-start(bf16[8,16,128]{2,1,0:T(8,128)(2,1)} %broadcast_in_dim.14), calls=%async_computation.4 | async-start | bytes 65536 | tf_op jit(solution)/shard_map/all_to_all | solution.py:36
  103.3 6.8 %all-to-all-done.4 = bf16[8,16,128]{2,1,0:T(8,128)(2,1)S(1)} async-done(((bf16[8,16,128]{2,1,0:T(8,128)(2,1)}), bf16[8,16,128]{2,1,0:T(8,128)(2,1)S(1)}, u32[]{:S(2)}, u32[]{:S(2)}) %all-to-all-start.4) | async-done | bytes 32800 | tf_op jit(solution)/shard_map/all_to_all | solution.py:36
  110.8 5.0 %all-to-all-start.5 = ((bf16[32,16,128]{2,1,0:T(8,128)(2,1)}), bf16[32,16,128]{2,1,0:T(8,128)(2,1)S(1)}, u32[]{:S(2)}, u32[]{:S(2)}) async-start(bf16[32,16,128]{2,1,0:T(8,128)(2,1)} %broadcast_in_dim.15), calls=%async_computation.5 | async-start | bytes 262144 | tf_op jit(solution)/shard_map/all_to_all | solution.py:36
  116.1 0.7 reshape.57.mixes_ref
  116.8 5.6 %output_rows.1 = bf16[320,5120]{1,0:T(8,128)(2,1)} custom-call(bf16[320,128]{1,0:T(8,128)(2,1)} %conv_rows.1.f_ref, bf16[320,256]{1,0:T(8,128)(2,1)} %reshape.57.mixes_ref, bf16[128,5120]{1,0:T(8,128)(2,1)} %e_ref.5, bf16[128,5120]{1,0:T(8,128)(2,1)} %os_ref.5, bf16[128,5120]{1,0:T(8,128)(2,1)} %ot_ref.3), custom_call_target="tpu_custom_call" | custom-call | tf_op jit(solution)/shard_map/output_rows/pallas_call | solution.py:184
  122.5 1.1 all-to-all-done.5
  (58 shorter events, 6.1 us)
Async XLA Ops:
  0.6 21.7 %collective-permute-start = (bf16[2,4,40,128]{3,2,1,0:T(8,128)(2,1)}, bf16[2,4,40,128]{3,2,1,0:T(8,128)(2,1)S(1)}, u32[]{:S(2)}, u32[]{:S(2)}) collective-permute-start(bf16[2,4,40,128]{3,2,1,0:T(8,128)(2,1)} %param.10), channel_id=1, source_target_pairs={{0,1},{1,2},{2,3},{3,4},{4,5},{5,6},{6,7},{7,8},{8,9},{9,10},{10,1... | collective-permute-start | bytes 245768 | tf_op jit(solution)/shard_map/ppermute | solution.py:493
  9.4 29.0 %all-to-all-start = ((bf16[32,40,128]{2,1,0:T(8,128)(2,1)}), bf16[32,40,128]{2,1,0:T(8,128)(2,1)S(1)}, u32[]{:S(2)}, u32[]{:S(2)}) async-start(bf16[32,40,128]{2,1,0:T(8,128)(2,1)} %bitcast.63), calls=%async_computation | async-start | bytes 655360 | tf_op jit(solution)/shard_map/all_to_all | solution.py:36
  22.3 0.6 copy-start.5
  27.3 5.4 %collective-permute-start.3 = (bf16[576,128]{1,0:T(8,128)(2,1)S(1)}, bf16[576,128]{1,0:T(8,128)(2,1)S(1)}, u32[]{:S(2)}, u32[]{:S(2)}) collective-permute-start(bf16[576,128]{1,0:T(8,128)(2,1)S(1)} %get-tuple-element.35), channel_id=1, source_target_pairs={{0,6},{2,0},{4,2},{6,4},{1,7},{3,1},{5,3},{7,5},{8,14},{10,8},{12,... | collective-permute-start | bytes 442376 | tf_op jit(solution)/shard_map/ppermute | solution.py:470
  29.9 6.8 %collective-permute-start.1 = (bf16[576,128]{1,0:T(8,128)(2,1)S(1)}, bf16[576,128]{1,0:T(8,128)(2,1)S(1)}, u32[]{:S(2)}, u32[]{:S(2)}) collective-permute-start(bf16[576,128]{1,0:T(8,128)(2,1)S(1)} %get-tuple-element.36), channel_id=1, source_target_pairs={{0,2},{2,4},{4,6},{6,0},{1,3},{3,5},{5,7},{7,1},{8,10},{10,12},{12... | collective-permute-start | bytes 442376 | tf_op jit(solution)/shard_map/ppermute | solution.py:470
  30.9 7.4 %collective-permute-start.2 = (bf16[576,128]{1,0:T(8,128)(2,1)S(1)}, bf16[576,128]{1,0:T(8,128)(2,1)S(1)}, u32[]{:S(2)}, u32[]{:S(2)}) collective-permute-start(bf16[576,128]{1,0:T(8,128)(2,1)S(1)} %get-tuple-element.37), channel_id=1, source_target_pairs={{0,4},{2,6},{4,0},{6,2},{1,5},{3,7},{5,1},{7,3},{8,12},{10,14},{12... | collective-permute-start | bytes 442376 | tf_op jit(solution)/shard_map/ppermute | solution.py:470
  32.7 14.6 %copy-start.1 = (bf16[576,128]{1,0:T(8,128)(2,1)}, bf16[576,128]{1,0:T(8,128)(2,1)S(1)}, u32[]{:S(2)}) copy-start(bf16[576,128]{1,0:T(8,128)(2,1)S(1)} %collective-permute-done.3.three_ref) | copy-start | bytes 442372
  36.8 10.5 %copy-start.2 = (bf16[576,128]{1,0:T(8,128)(2,1)}, bf16[576,128]{1,0:T(8,128)(2,1)S(1)}, u32[]{:S(2)}) copy-start(bf16[576,128]{1,0:T(8,128)(2,1)S(1)} %collective-permute-done.1.one_ref) | copy-start | bytes 442372
  38.3 17.0 %copy-start.3 = (bf16[576,128]{1,0:T(8,128)(2,1)}, bf16[576,128]{1,0:T(8,128)(2,1)S(1)}, u32[]{:S(2)}) copy-start(bf16[576,128]{1,0:T(8,128)(2,1)S(1)} %collective-permute-done.2.two_ref) | copy-start | bytes 442372
  39.1 15.5 %all-to-all-start.1 = ((bf16[8,40,128]{2,1,0:T(8,128)(2,1)}), bf16[8,40,128]{2,1,0:T(8,128)(2,1)S(1)}, u32[]{:S(2)}, u32[]{:S(2)}) async-start(bf16[8,40,128]{2,1,0:T(8,128)(2,1)} %broadcast_in_dim.12), calls=%async_computation.1 | async-start | bytes 163840 | tf_op jit(solution)/shard_map/all_to_all | solution.py:36
  47.3 16.7 %collective-permute-start.4 = (bf16[4,448,128]{2,1,0:T(8,128)(2,1)S(1)}, bf16[4,448,128]{2,1,0:T(8,128)(2,1)S(1)}, u32[]{:S(2)}, u32[]{:S(2)}) collective-permute-start(bf16[4,448,128]{2,1,0:T(8,128)(2,1)S(1)} %pad_maximum_fusion), channel_id=1, source_target_pairs={{0,1},{1,0},{2,3},{3,2},{4,5},{5,4},{6,7},{7,6},{8,9},{9,8},{10,11... | collective-permute-start | bytes 1376264 | tf_op jit(solution)/shard_map/ppermute | solution.py:470
  55.4 18.2 %all-to-all-start.2 = ((bf16[32,40,128]{2,1,0:T(8,128)(2,1)}), bf16[32,40,128]{2,1,0:T(8,128)(2,1)S(1)}, u32[]{:S(2)}, u32[]{:S(2)}) async-start(bf16[32,40,128]{2,1,0:T(8,128)(2,1)} %broadcast_in_dim.13), calls=%async_computation.2 | async-start | bytes 655360 | tf_op jit(solution)/shard_map/all_to_all | solution.py:36
  64.0 0.8 copy-start.4
  73.6 0.7 copy-start
  82.9 8.7 %collective-permute-start.7 = (bf16[2,64,256]{2,1,0:T(8,128)(2,1)S(1)}, bf16[2,64,256]{2,1,0:T(8,128)(2,1)S(1)}, u32[]{:S(2)}, u32[]{:S(2)}) collective-permute-start(bf16[2,64,256]{2,1,0:T(8,128)(2,1)S(1)} %get-tuple-element.25), channel_id=1, source_target_pairs={{0,2},{2,4},{4,6},{6,0},{1,3},{3,5},{5,7},{7,1},{8,10},{10,12},{12... | collective-permute-start | bytes 196616 | tf_op jit(solution)/shard_map/ppermute | solution.py:470
  83.2 8.4 %collective-permute-start.6 = (bf16[2,64,256]{2,1,0:T(8,128)(2,1)S(1)}, bf16[2,64,256]{2,1,0:T(8,128)(2,1)S(1)}, u32[]{:S(2)}, u32[]{:S(2)}) collective-permute-start(bf16[2,64,256]{2,1,0:T(8,128)(2,1)S(1)} %get-tuple-element.26), channel_id=1, source_target_pairs={{0,4},{2,6},{4,0},{6,2},{1,5},{3,7},{5,1},{7,3},{8,12},{10,14},{12... | collective-permute-start | bytes 196616 | tf_op jit(solution)/shard_map/ppermute | solution.py:470
  85.2 6.4 %collective-permute-start.5 = (bf16[2,64,256]{2,1,0:T(8,128)(2,1)S(1)}, bf16[2,64,256]{2,1,0:T(8,128)(2,1)S(1)}, u32[]{:S(2)}, u32[]{:S(2)}) collective-permute-start(bf16[2,64,256]{2,1,0:T(8,128)(2,1)S(1)} %get-tuple-element.27), channel_id=1, source_target_pairs={{0,6},{2,0},{4,2},{6,4},{1,7},{3,1},{5,3},{7,5},{8,14},{10,8},{12,... | collective-permute-start | bytes 196616 | tf_op jit(solution)/shard_map/ppermute | solution.py:470
  85.7 13.6 %all-to-all-start.3 = ((bf16[32,16,128]{2,1,0:T(8,128)(2,1)}), bf16[32,16,128]{2,1,0:T(8,128)(2,1)S(1)}, u32[]{:S(2)}, u32[]{:S(2)}) async-start(bf16[32,16,128]{2,1,0:T(8,128)(2,1)} %bitcast.65), calls=%async_computation.3 | async-start | bytes 262144 | tf_op jit(solution)/shard_map/all_to_all | solution.py:36
  91.7 24.1 %collective-permute-start.8 = (bf16[4,64,256]{2,1,0:T(8,128)(2,1)S(1)}, bf16[4,64,256]{2,1,0:T(8,128)(2,1)S(1)}, u32[]{:S(2)}, u32[]{:S(2)}) collective-permute-start(bf16[4,64,256]{2,1,0:T(8,128)(2,1)S(1)} %get-tuple-element.23), channel_id=1, source_target_pairs={{0,1},{1,0},{2,3},{3,2},{4,5},{5,4},{6,7},{7,6},{8,9},{9,8},{10,11... | collective-permute-start | bytes 393224 | tf_op jit(solution)/shard_map/ppermute | solution.py:470
  99.9 10.1 %all-to-all-start.4 = ((bf16[8,16,128]{2,1,0:T(8,128)(2,1)}), bf16[8,16,128]{2,1,0:T(8,128)(2,1)S(1)}, u32[]{:S(2)}, u32[]{:S(2)}) async-start(bf16[8,16,128]{2,1,0:T(8,128)(2,1)} %broadcast_in_dim.14), calls=%async_computation.4 | async-start | bytes 65536 | tf_op jit(solution)/shard_map/all_to_all | solution.py:36
  110.8 12.8 %all-to-all-start.5 = ((bf16[32,16,128]{2,1,0:T(8,128)(2,1)}), bf16[32,16,128]{2,1,0:T(8,128)(2,1)S(1)}, u32[]{:S(2)}, u32[]{:S(2)}) async-start(bf16[32,16,128]{2,1,0:T(8,128)(2,1)} %broadcast_in_dim.15), calls=%async_computation.5 | async-start | bytes 262144 | tf_op jit(solution)/shard_map/all_to_all | solution.py:36
  116.8 6.8 %copy-start.6 = (bf16[20,128]{1,0:T(8,128)(2,1)S(1)}, bf16[20,128]{1,0:T(8,128)(2,1)}, u32[]{:S(2)}) copy-start(bf16[20,128]{1,0:T(8,128)(2,1)} %get-tuple-element.19) | copy-start | bytes 15364
  116.8 7.2 %copy-start.7 = (f32[20,384]{1,0:T(8,128)S(1)}, f32[20,384]{1,0:T(8,128)}, u32[]{:S(2)}) copy-start(f32[20,384]{1,0:T(8,128)} %get-tuple-element.21) | copy-start | bytes 92164

commit v6 on v5

--- a/solution.py
+++ b/solution.py
@@ -43,7 +43,8 @@
     return exchange(jnp.broadcast_to(value, (size,) + value.shape), axes)
 
 
-def conv_kernel(prior_ref, here_ref, weight_ref, out_ref):
+def conv_kernel(at_ref, prior_ref, here_ref, weight_ref, cots_ref, own_ref, one_ref, two_ref, three_ref):
+    payloads = (own_ref, one_ref, two_ref, three_ref)
     tokens = here_ref.shape[0]
     columns = here_ref.shape[0] // 8
     volume = jnp.concatenate([prior_ref[...].astype(f32), here_ref[...].astype(f32)], axis=0)
@@ -69,19 +70,25 @@
             + jnp.concatenate([gap, above[lo : hi - columns]], axis=0)
             + jnp.concatenate([below[lo + columns : hi], gap], axis=0)
         )
-        out_ref[lo:hi] = jax.nn.gelu(total, approximate=True).astype(bf16)
-
-
-def conv_rows(prior, here, weight):
+        feats = jax.nn.gelu(total, approximate=True).astype(bf16)
+        for ref in payloads:
+            ref[lo:hi] = feats
+    for step, ref in enumerate(payloads):
+        ref[tokens:] = cots_ref[(at_ref[2] + step) % 4]
+
+
+def conv_rows(at, prior, here, weight, cots):
     tokens, channels = here.shape
+    n_line, extra, head = cots.shape
     vmem = pl.BlockSpec(memory_space=pltpu.VMEM)
     return pl.pallas_call(
         conv_kernel,
-        in_specs=[vmem] * 3,
-        out_specs=vmem,
-        out_shape=jax.ShapeDtypeStruct((tokens, weight.shape[-1]), bf16),
+        in_specs=[pl.BlockSpec(memory_space=pltpu.SMEM)] + [vmem] * 4,
+        out_specs=[vmem] * n_line,
+        out_shape=[jax.ShapeDtypeStruct((tokens + extra, head), bf16)] * n_line,
+        compiler_params=pltpu.CompilerParams(vmem_limit_bytes=12 << 20),
         name="conv_rows",
-    )(prior, here, weight.reshape(9, 3 * channels, weight.shape[-1]))
+    )(at, prior, here, weight.reshape(9, 3 * channels, weight.shape[-1]), cots)
 
 
 CHUNK = 1024
@@ -161,7 +168,7 @@
         for copy in group:
             copy.start()
         copies.append(group)
-    x = jnp.concatenate([f_ref[...], mixes_ref[...]], axis=1)
+    x = jnp.concatenate([f_ref[: rows.shape[0]], mixes_ref[...]], axis=1)
     leaving = []
     for i, group in enumerate(copies):
         for copy in group:
@@ -177,8 +184,8 @@
 
 
 def output_rows(feats, mixes, embed, out_s, out_t):
-    tokens, head = feats.shape
-    width = embed.shape[1]
+    tokens = mixes.shape[0]
+    head, width = embed.shape
     hbm = pl.BlockSpec(memory_space=pl.ANY)
     vmem = pl.BlockSpec(memory_space=pltpu.VMEM)
     return pl.pallas_call(
@@ -263,49 +270,44 @@
     )(at, w_s, w_t, embed, out_s, gain_s.reshape(1, width), gain_t.reshape(1, width))
 
 
-def norm_kernel(at_ref, held_ref, one_ref, two_ref, three_ref, other_ref, gram_ref, flat_ref, scaled_ref, cots_ref):
+def norm_kernel(at_ref, *refs):
+    payloads, (gram_ref, flat_ref, scaled_ref, cots_ref) = refs[:8], refs[8:]
     head = flat_ref.shape[1]
     kinds, span = cots_ref.shape[2], cots_ref.shape[3]
-    tokens = other_ref.shape[1] - kinds * span
+    tokens = flat_ref.shape[0] // len(payloads)
     gram = gram_ref[:head, :head]
     first = gram.astype(bf16)
     rest = gram - first.astype(f32)
     second = rest.astype(bf16)
     third = (rest - second.astype(f32)).astype(bf16)
     kept = pl.multiple_of(tokens + at_ref[3] * (kinds * span), 16)
-    near = (held_ref, one_ref, two_ref, three_ref)
-    for side in range(2):
-        for step in range(4):
-            x = near[step][:tokens] if side == 0 else other_ref[step, :tokens]
-            xg = nn(x, first) + (nn(x, second) + nn(x, third))
-            wide = x.astype(f32)
-            factor = lax.rsqrt(jnp.sum(xg * wide, axis=-1, keepdims=True) + epsilon)
-            to = (side * 4 + step) * tokens
-            flat_ref[to : to + tokens] = x
-            scaled_ref[to : to + tokens] = (wide * factor).astype(bf16)
-            if side == 0:
-                got = near[step][pl.ds(kept, kinds * span)]
-            else:
-                got = other_ref[step, tokens:]
-            for kind in range(kinds):
-                cots_ref[side, step, kind] = got[kind * span : (kind + 1) * span]
-
-
-def norm_rows(at, near, other, gram, span):
-    n_line, rows, head = other.shape
-    tokens = rows - 2 * span
+    for i, ref in enumerate(payloads):
+        x = ref[:tokens]
+        xg = nn(x, first) + (nn(x, second) + nn(x, third))
+        wide = x.astype(f32)
+        factor = lax.rsqrt(jnp.sum(xg * wide, axis=-1, keepdims=True) + epsilon)
+        flat_ref[i * tokens : (i + 1) * tokens] = x
+        scaled_ref[i * tokens : (i + 1) * tokens] = (wide * factor).astype(bf16)
+        got = ref[pl.ds(kept, kinds * span)]
+        for kind in range(kinds):
+            cots_ref[i // 4, i % 4, kind] = got[kind * span : (kind + 1) * span]
+
+
+def norm_rows(at, payloads, gram, span):
+    rows, head = payloads[0].shape
+    tokens = rows - 4 * span
     vmem = pl.BlockSpec(memory_space=pltpu.VMEM)
     return pl.pallas_call(
         norm_kernel,
-        in_specs=[pl.BlockSpec(memory_space=pltpu.SMEM)] + [vmem] * 6,
+        in_specs=[pl.BlockSpec(memory_space=pltpu.SMEM)] + [vmem] * 9,
         out_specs=[vmem] * 3,
         out_shape=[
-            jax.ShapeDtypeStruct((2 * n_line * tokens, head), bf16),
-            jax.ShapeDtypeStruct((2 * n_line * tokens, head), bf16),
-            jax.ShapeDtypeStruct((2, n_line, 2, span, head), bf16),
+            jax.ShapeDtypeStruct((8 * tokens, head), bf16),
+            jax.ShapeDtypeStruct((8 * tokens, head), bf16),
+            jax.ShapeDtypeStruct((2, 4, 2, span, head), bf16),
         ],
         name="norm_rows",
-    )(at, *near, other, gram)
+    )(at, *payloads, gram)
 
 
 def group_size(axes):
@@ -335,7 +337,7 @@
 
 def attend_kernel(
     at_ref, flat_ref, scaled_ref, gram_ref, cots_ref, maps_ref,
-    total_ref, back_ref, mix_ref, qkv_ref, att_ref, dkv_ref, up_ref, score_ref, rounded_ref, slope_ref,
+    total_ref, own_ref, one_ref, two_ref, three_ref, mix_ref, qkv_ref, att_ref, dkv_ref, up_ref, score_ref, rounded_ref, slope_ref,
 ):
     frames = FR
     head = flat_ref.shape[1]
@@ -400,11 +402,11 @@
     att = softmax_rows(jnp.where(allowed, nt(q, k) * scale, masked))
     rounded = att.astype(bf16)
     mix_t = nn(rounded, v).astype(bf16)
-    span = back_ref.shape[2]
+    span = own_ref.shape[1]
     for side in range(2):
-        for step in range(4):
+        for step, ref in enumerate((own_ref, one_ref, two_ref, three_ref)):
             mine = slice((side * 4 + step) * span, (side * 4 + step + 1) * span)
-            back_ref[step, side] = jnp.concatenate([mix[mine], mix_t[mine]], axis=1)
+            ref[side] = jnp.concatenate([mix[mine], mix_t[mine]], axis=1)
     d_att = nt(g, v)
     d_sc = (att * (d_att - jnp.sum(d_att * att, axis=-1, keepdims=True))).astype(bf16)
     d_packed = jnp.concatenate(
@@ -446,11 +448,9 @@
     return pl.pallas_call(
         attend_kernel,
         in_specs=[pl.BlockSpec(memory_space=pltpu.SMEM)] + [vmem] * 5,
-        out_specs=[vmem] * 2,
-        out_shape=[
-            jax.ShapeDtypeStruct((4 * head, head), bf16),
-            jax.ShapeDtypeStruct((4, 2, own // 8, 2 * head), bf16),
-        ],
+        out_specs=[vmem] * 5,
+        out_shape=[jax.ShapeDtypeStruct((4 * head, head), bf16)]
+        + [jax.ShapeDtypeStruct((2, own // 8, 2 * head), bf16)] * 4,
         scratch_shapes=[
             pltpu.VMEM((own, head), bf16),
             pltpu.VMEM((rows, 3 * head), bf16),
@@ -504,9 +504,6 @@
     )
     maps = gathered(scattered(maps), maps.shape)
 
-    feats_home = conv_rows(
-        prior.reshape(tokens, channels), clip_video.reshape(tokens, channels), conv_weight
-    )
     gram, cots = products(
         embed_weight,
         output_spatial,
@@ -517,26 +514,19 @@
         pad,
     )
     cots = cots.reshape(n_line, 4 * frames * pad, head)
-    held = [
-        jnp.concatenate(
-            [feats_home, lax.dynamic_index_in_dim(cots, (line + step) % n_line, 0, keepdims=False)], axis=0
-        )
-        for step in range(n_line)
-    ]
-    moved = []
+    held = conv_rows(
+        at, prior.reshape(tokens, channels), clip_video.reshape(tokens, channels), conv_weight, cots
+    )
+    feats_home = held[0]
+    near = [held[0]]
     for step in range(1, n_line):
-        moved.append(turned(held[step], "y", step))
-    near = [held[0]] + moved
-    span = frames * pad
-    give = tokens + (1 - core) * 2 * span
-    payload = [
-        jnp.concatenate([part[:tokens], lax.dynamic_slice_in_dim(part, give, 2 * span, 0)], axis=0)
-        for part in near
-    ]
-    other = turned(jnp.stack(payload), "c", 1)
-    flat, scaled, cots = norm_rows(at, near, other, gram, span)
-
-    total, back = attend_all(at, flat, scaled, gram, cots, maps, pad)
+        near.append(turned(held[step], "y", step))
+    other = []
+    for step in range(n_line):
+        other.append(turned(near[step], "c", 1))
+    flat, scaled, cots = norm_rows(at, near + other, gram, frames * pad)
+
+    total, *back = attend_all(at, flat, scaled, gram, cots, maps, pad)
     total = gathered(scattered(total), total.shape)
     grad = jnp.concatenate([nn(e_mine, total[b * head : (b + 1) * head]) for b in range(3)], axis=1) * g_mine
 

time: 126 us -> 123 us (0.976)
  blocking collectives: 0 us -> 18.2 us
  starting transfers between devices: 52.8 us -> 43.8 us
  waiting for transfers between devices: 31 us -> 23.8 us
  other arithmetic: 3.65 us -> 1.83 us
  local copies, waits for them, and re-layouts: 8.25 us -> 6.47 us
    all_to_all x0 -> x1, blocking collectives: none -> 18.2 us  [exchange(): return lax.all_to_all(parts, axes, 0, 0, tiled=True)]
    all_to_all x6 -> x5, starting transfers between devices: 38 us -> 29.6 us  [exchange(): return lax.all_to_all(parts, axes, 0, 0, tiled=True)]
    all_to_all x6 -> x5, waiting for transfers between devices: 25.4 us -> 19.6 us  [exchange(): return lax.all_to_all(parts, axes, 0, 0, tiled=True)]
    ppermute x1, starting transfers between devices: 4.59 us -> 2 us  [shards(): prior = lax.ppermute(clip_video, TS, [(i, i + 1) for i in range(n_ts - 1)])]
    ppermute x8 -> x11, starting transfers between devices: 10.2 us -> 12.2 us  [turned(): return lax.ppermute(value, axis, [(i, (i + step) % n) for i in range(n)])]
    concatenate x2 -> x0, other arithmetic: 1.67 us -> none  [shards(): jnp.concatenate([feats_home, lax.dynamic_index_in_dim(cots, (line + step)...]
    ppermute x8 -> x11, waiting for transfers between devices: 5.64 us -> 4.19 us  [turned(): return lax.ppermute(value, axis, [(i, (i + step) % n) for i in range(n)])]
    pallas_call x1, Pallas kernels: 2.72 us -> 1.36 us  [conv_rows(): pl.pallas_call(conv_kernel, in_specs=[pl.BlockSpec(memory_space=pltpu.SME...]
  transfers between devices with their start and end apart: 15 -> 17, of which waited for: 7 -> 8; matrix products, arithmetic and copies ran while one was open for 6% -> 3% of each run, Pallas kernels for 16% -> 12%
where the time goes in v6:
time: 123 us; the launch traced here: 122 us
  starting transfers between devices  43.8 us (36%)
  Pallas kernels  26.3 us (21%)
  waiting for transfers between devices  23.8 us (19%)
  blocking collectives  18.2 us (15%)
  local copies, waits for them, and re-layouts  6.47 us (5%)
  other arithmetic  1.83 us (1%)
    all_to_all x5, starting transfers between devices, exchange(): return lax.all_to_all(parts, axes, 0, 0, tiled=True)  29.6 us
    all_to_all x5, waiting for transfers between devices, exchange(): return lax.all_to_all(parts, axes, 0, 0, tiled=True)  19.6 us
    all_to_all x1, blocking collectives, exchange(): return lax.all_to_all(parts, axes, 0, 0, tiled=True)  18.2 us
    ppermute x11, starting transfers between devices, turned(): return lax.ppermute(value, axis, [(i, (i + step) % n) for i in range(n)])  12.2 us
    pallas_call x1, Pallas kernels, attend_all(): pl.pallas_call(attend_kernel, in_specs=[pl.BlockSpec(memory_space=pltpu.S...  7.66 us
    pallas_call x1, Pallas kernels, output_rows(): pl.pallas_call(output_kernel, in_specs=[vmem, vmem, hbm, hbm, hbm], out_s...  5.67 us
    pallas_call x1, Pallas kernels, products(): pl.pallas_call(products_kernel, in_specs=[hbm] * 4, out_specs=[vmem, vmem...  4.9 us
    ppermute x11, waiting for transfers between devices, turned(): return lax.ppermute(value, axis, [(i, (i + step) % n) for i in range(n)])  4.19 us
  transfers between devices with their start and end apart: 17, of which 8 were waited for; matrix products, arithmetic and copies ran while one was open for 3% of the time, Pallas kernels for 12%

profile of v6, /device:TPU:1, one launch (start us, length us, event | category | flops | bytes accessed | tf_op | source)
XLA Modules:
  0.0 121.8 jit_solution(17007134908315258806)
XLA Ops:
  1.2 3.5 %local_maps.1 = (bf16[1280,128]{1,0:T(8,128)(2,1)}, bf16[20,128]{1,0:T(8,128)(2,1)}, f32[20,384]{1,0:T(8,128)}) custom-call(s32[6]{0:T(128)} %stack.44.at_ref, bf16[20,384]{1,0:T(8,128)(2,1)} %ws_ref.1, bf16[20,384]{1,0:T(8,128)(2,1)} %wt_ref.1, bf16[128,5120]{1,0:T(8,128)(2,1)} %e_ref.5, bf16[128,5120]{1,0:T(8,128)(2,1)} %os_ref.5, f32[1,5120]{1,0:T(1,128)} %bitcast.55, ...), custom_call_target="tpu_custom_call" | custom-call | tf_op jit(solution)/shard_map/local_maps/pallas_call | solution.py:255
  4.8 18.2 %all_to_all.30 = bf16[32,40,128]{2,1,0:T(8,128)(2,1)S(1)} all-to-all(bf16[32,40,128]{2,1,0:T(8,128)(2,1)} %bitcast.45), channel_id=1, replica_groups=mesh['x'=4,'zh'=2,'zl'=4,'y'=4,'c'=2] {'x','y','c'}, dimensions={0} | all-to-all | bytes 655360 | tf_op jit(solution)/shard_map/all_to_all | solution.py:36
  23.7 8.2 %all-to-all-start.1 = ((bf16[8,40,128]{2,1,0:T(8,128)(2,1)}), bf16[8,40,128]{2,1,0:T(8,128)(2,1)S(1)}, u32[]{:S(2)}, u32[]{:S(2)}) async-start(bf16[8,40,128]{2,1,0:T(8,128)(2,1)} %broadcast_in_dim.12), calls=%async_computation.1 | async-start | bytes 163840 | tf_op jit(solution)/shard_map/all_to_all | solution.py:36
  31.9 2.0 %collective-permute-start = (bf16[2,4,40,128]{3,2,1,0:T(8,128)(2,1)S(1)}, bf16[2,4,40,128]{3,2,1,0:T(8,128)(2,1)S(1)}, u32[]{:S(2)}, u32[]{:S(2)}) collective-permute-start(bf16[2,4,40,128]{3,2,1,0:T(8,128)(2,1)S(1)} %copy-done.3), channel_id=1, source_target_pairs={{0,1},{1,2},{2,3},{3,4},{4,5},{5,6},{6,7},{7,8},{8,9},{9,10},{10,1... | collective-permute-start | bytes 245768 | tf_op jit(solution)/shard_map/ppermute | solution.py:493
  33.9 5.3 %all-to-all-done.1 = bf16[8,40,128]{2,1,0:T(8,128)(2,1)S(1)} async-done(((bf16[8,40,128]{2,1,0:T(8,128)(2,1)}), bf16[8,40,128]{2,1,0:T(8,128)(2,1)S(1)}, u32[]{:S(2)}, u32[]{:S(2)}) %all-to-all-start.1) | async-done | bytes 81952 | tf_op jit(solution)/shard_map/all_to_all | solution.py:36
  39.2 0.8 broadcast_in_dim.13
  40.0 5.3 %all-to-all-start.2 = ((bf16[32,40,128]{2,1,0:T(8,128)(2,1)}), bf16[32,40,128]{2,1,0:T(8,128)(2,1)S(1)}, u32[]{:S(2)}, u32[]{:S(2)}) async-start(bf16[32,40,128]{2,1,0:T(8,128)(2,1)} %broadcast_in_dim.13), calls=%async_computation.2 | async-start | bytes 655360 | tf_op jit(solution)/shard_map/all_to_all | solution.py:36
  45.3 4.9 %products.1 = (f32[256,256]{1,0:T(8,128)}, bf16[8,2,2,32,128]{4,3,2,1,0:T(8,128)(2,1)}) custom-call(bf16[128,5120]{1,0:T(8,128)(2,1)} %e_ref.5, bf16[128,5120]{1,0:T(8,128)(2,1)} %os_ref.5, bf16[128,5120]{1,0:T(8,128)(2,1)} %ot_ref.3, bf16[320,5120]{1,0:T(8,128)(2,1)} %bitcast.41), custom_call_target="tpu_custom_call" | custom-call | tf_op jit(solution)/shard_map/products/pallas_call | solution.py:140
  50.3 0.9 copy-done.2
  51.2 1.4 %conv_rows.1 = (bf16[576,128]{1,0:T(8,128)(2,1)S(1)}, bf16[576,128]{1,0:T(8,128)(2,1)S(1)}, bf16[576,128]{1,0:T(8,128)(2,1)S(1)}, bf16[576,128]{1,0:T(8,128)(2,1)S(1)}) custom-call(s32[6]{0:T(128)S(1)} %copy-done.4, bf16[320,128]{1,0:T(8,128)(2,1)S(1)} %bitcast.40, bf16[320,128]{1,0:T(8,128)(2,1)S(1)} %bitcast.39, bf16[9,384,128]{2,1,0:T(8,128)(2,1)S(1)} %bitcast.37, ...), custom_call_target="tpu_custom_call" | custom-call | tf_op jit(solution)/shard_map/conv_rows/pallas_call | solution.py:84
  52.6 1.4 %collective-permute-start.1 = (bf16[576,128]{1,0:T(8,128)(2,1)S(1)}, bf16[576,128]{1,0:T(8,128)(2,1)S(1)}, u32[]{:S(2)}, u32[]{:S(2)}) collective-permute-start(bf16[576,128]{1,0:T(8,128)(2,1)S(1)} %get-tuple-element.21), channel_id=1, source_target_pairs={{0,2},{2,4},{4,6},{6,0},{1,3},{3,5},{5,7},{7,1},{8,10},{10,12},{12... | collective-permute-start | bytes 442376 | tf_op jit(solution)/shard_map/ppermute | solution.py:470
  54.0 2.4 %collective-permute-start.2 = (bf16[576,128]{1,0:T(8,128)(2,1)S(1)}, bf16[576,128]{1,0:T(8,128)(2,1)S(1)}, u32[]{:S(2)}, u32[]{:S(2)}) collective-permute-start(bf16[576,128]{1,0:T(8,128)(2,1)S(1)} %get-tuple-element.22), channel_id=1, source_target_pairs={{0,4},{2,6},{4,0},{6,2},{1,5},{3,7},{5,1},{7,3},{8,12},{10,14},{12... | collective-permute-start | bytes 442376 | tf_op jit(solution)/shard_map/ppermute | solution.py:470
  56.5 1.2 collective-permute-start.3
  57.6 1.2 %collective-permute-start.4 = (bf16[576,128]{1,0:T(8,128)(2,1)S(1)}, bf16[576,128]{1,0:T(8,128)(2,1)S(1)}, u32[]{:S(2)}, u32[]{:S(2)}) collective-permute-start(bf16[576,128]{1,0:T(8,128)(2,1)S(1)} %get-tuple-element.20.refs_0_.f_ref), channel_id=1, source_target_pairs={{0,1},{1,0},{2,3},{3,2},{4,5},{5,4},{6,7},{7,6},{8,9},{9,8},{10,11... | collective-permute-start | bytes 442376 | tf_op jit(solution)/shard_map/ppermute | solution.py:470
  58.9 1.2 collective-permute-start.5
  60.1 3.0 %collective-permute-done.2.refs_2_ = bf16[576,128]{1,0:T(8,128)(2,1)S(1)} collective-permute-done((bf16[576,128]{1,0:T(8,128)(2,1)S(1)}, bf16[576,128]{1,0:T(8,128)(2,1)S(1)}, u32[]{:S(2)}, u32[]{:S(2)}) %collective-permute-start.2) | collective-permute-done | bytes 147488 | tf_op jit(solution)/shard_map/ppermute | solution.py:470
  63.2 1.2 %collective-permute-start.6 = (bf16[576,128]{1,0:T(8,128)(2,1)S(1)}, bf16[576,128]{1,0:T(8,128)(2,1)S(1)}, u32[]{:S(2)}, u32[]{:S(2)}) collective-permute-start(bf16[576,128]{1,0:T(8,128)(2,1)S(1)} %collective-permute-done.2.refs_2_), channel_id=1, source_target_pairs={{0,1},{1,0},{2,3},{3,2},{4,5},{5,4},{6,7},{7,6},{8,9},{9,8},{10,11... | collective-permute-start | bytes 442376 | tf_op jit(solution)/shard_map/ppermute | solution.py:470
  64.7 0.7 collective-permute-done.6.refs_6_
  66.5 3.2 %norm_rows.1 = (bf16[2560,128]{1,0:T(8,128)(2,1)}, bf16[2560,128]{1,0:T(8,128)(2,1)}, bf16[2,4,2,64,128]{4,3,2,1,0:T(8,128)(2,1)}) custom-call(s32[6]{0:T(128)} %stack.44.at_ref, bf16[576,128]{1,0:T(8,128)(2,1)} %copy-done.1, bf16[576,128]{1,0:T(8,128)(2,1)} %copy-done.6, bf16[576,128]{1,0:T(8,128)(2,1)} %copy-done.7, bf16[576,128]{1,0:T(8,128)(2,1)} %copy-done.8, ...), custom_call_target="tpu_custom_call" | custom-call | tf_op jit(solution)/shard_map/norm_rows/pallas_call | solution.py:300
  69.7 0.7 copy-done.5
  70.4 7.7 %attend_all.1 = (bf16[512,128]{1,0:T(8,128)(2,1)}, bf16[2,64,256]{2,1,0:T(8,128)(2,1)}, bf16[2,64,256]{2,1,0:T(8,128)(2,1)}, bf16[2,64,256]{2,1,0:T(8,128)(2,1)}, bf16[2,64,256]{2,1,0:T(8,128)(2,1)}) custom-call(s32[6]{0:T(128)} %stack.44.at_ref, bf16[2560,128]{1,0:T(8,128)(2,1)} %get-tuple-element.25.flat_ref, ...), custom_call_target="tpu_custom_call" | custom-call | tf_op jit(solution)/shard_map/attend_all/pallas_call | solution.py:448
  78.1 1.5 %collective-permute-start.8 = (bf16[2,64,256]{2,1,0:T(8,128)(2,1)}, bf16[2,64,256]{2,1,0:T(8,128)(2,1)S(1)}, u32[]{:S(2)}, u32[]{:S(2)}) collective-permute-start(bf16[2,64,256]{2,1,0:T(8,128)(2,1)} %get-tuple-element.30), channel_id=1, source_target_pairs={{0,6},{2,0},{4,2},{6,4},{1,7},{3,1},{5,3},{7,5},{8,14},{10,8},{12,... | collective-permute-start | bytes 196616 | tf_op jit(solution)/shard_map/ppermute | solution.py:470
  79.6 0.9 collective-permute-start.9
  81.0 7.7 %all-to-all-start.3 = ((bf16[32,16,128]{2,1,0:T(8,128)(2,1)}), bf16[32,16,128]{2,1,0:T(8,128)(2,1)S(1)}, u32[]{:S(2)}, u32[]{:S(2)}) async-start(bf16[32,16,128]{2,1,0:T(8,128)(2,1)} %bitcast.46), calls=%async_computation.3 | async-start | bytes 262144 | tf_op jit(solution)/shard_map/all_to_all | solution.py:36
  88.7 0.9 pad_maximum_fusion
  90.0 6.4 %all-to-all-done.3 = bf16[32,16,128]{2,1,0:T(8,128)(2,1)S(1)} async-done(((bf16[32,16,128]{2,1,0:T(8,128)(2,1)}), bf16[32,16,128]{2,1,0:T(8,128)(2,1)S(1)}, u32[]{:S(2)}, u32[]{:S(2)}) %all-to-all-start.3) | async-done | bytes 131104 | tf_op jit(solution)/shard_map/all_to_all | solution.py:36
  97.0 3.3 %all-to-all-start.4 = ((bf16[8,16,128]{2,1,0:T(8,128)(2,1)}), bf16[8,16,128]{2,1,0:T(8,128)(2,1)S(1)}, u32[]{:S(2)}, u32[]{:S(2)}) async-start(bf16[8,16,128]{2,1,0:T(8,128)(2,1)} %broadcast_in_dim.14), calls=%async_computation.4 | async-start | bytes 65536 | tf_op jit(solution)/shard_map/all_to_all | solution.py:36
  100.4 6.8 %all-to-all-done.4 = bf16[8,16,128]{2,1,0:T(8,128)(2,1)S(1)} async-done(((bf16[8,16,128]{2,1,0:T(8,128)(2,1)}), bf16[8,16,128]{2,1,0:T(8,128)(2,1)S(1)}, u32[]{:S(2)}, u32[]{:S(2)}) %all-to-all-start.4) | async-done | bytes 32800 | tf_op jit(solution)/shard_map/all_to_all | solution.py:36
  107.9 5.1 %all-to-all-start.5 = ((bf16[32,16,128]{2,1,0:T(8,128)(2,1)}), bf16[32,16,128]{2,1,0:T(8,128)(2,1)S(1)}, u32[]{:S(2)}, u32[]{:S(2)}) async-start(bf16[32,16,128]{2,1,0:T(8,128)(2,1)} %broadcast_in_dim.15), calls=%async_computation.5 | async-start | bytes 262144 | tf_op jit(solution)/shard_map/all_to_all | solution.py:36
  113.2 0.7 reshape.57.mixes_ref
  113.9 5.7 %output_rows.1 = bf16[320,5120]{1,0:T(8,128)(2,1)} custom-call(bf16[576,128]{1,0:T(8,128)(2,1)} %copy-done.1, bf16[320,256]{1,0:T(8,128)(2,1)} %reshape.57.mixes_ref, bf16[128,5120]{1,0:T(8,128)(2,1)} %e_ref.5, bf16[128,5120]{1,0:T(8,128)(2,1)} %os_ref.5, bf16[128,5120]{1,0:T(8,128)(2,1)} %ot_ref.3), custom_call_target="tpu_custom_call" | custom-call | tf_op jit(solution)/shard_map/output_rows/pallas_call | solution.py:191
  119.6 1.1 all-to-all-done.5
  (62 shorter events, 6.2 us)
Async XLA Ops:
  1.2 30.7 %copy-start.3 = (bf16[2,4,40,128]{3,2,1,0:T(8,128)(2,1)S(1)}, bf16[2,4,40,128]{3,2,1,0:T(8,128)(2,1)}, u32[]{:S(2)}) copy-start(bf16[2,4,40,128]{3,2,1,0:T(8,128)(2,1)} %param.10) | copy-start | bytes 245764
  23.7 15.5 %all-to-all-start.1 = ((bf16[8,40,128]{2,1,0:T(8,128)(2,1)}), bf16[8,40,128]{2,1,0:T(8,128)(2,1)S(1)}, u32[]{:S(2)}, u32[]{:S(2)}) async-start(bf16[8,40,128]{2,1,0:T(8,128)(2,1)} %broadcast_in_dim.12), calls=%async_computation.1 | async-start | bytes 163840 | tf_op jit(solution)/shard_map/all_to_all | solution.py:36
  31.9 18.3 %collective-permute-start = (bf16[2,4,40,128]{3,2,1,0:T(8,128)(2,1)S(1)}, bf16[2,4,40,128]{3,2,1,0:T(8,128)(2,1)S(1)}, u32[]{:S(2)}, u32[]{:S(2)}) collective-permute-start(bf16[2,4,40,128]{3,2,1,0:T(8,128)(2,1)S(1)} %copy-done.3), channel_id=1, source_target_pairs={{0,1},{1,2},{2,3},{3,4},{4,5},{5,6},{6,7},{7,8},{8,9},{9,10},{10,1... | collective-permute-start | bytes 245768 | tf_op jit(solution)/shard_map/ppermute | solution.py:493
  40.0 29.7 %all-to-all-start.2 = ((bf16[32,40,128]{2,1,0:T(8,128)(2,1)}), bf16[32,40,128]{2,1,0:T(8,128)(2,1)S(1)}, u32[]{:S(2)}, u32[]{:S(2)}) async-start(bf16[32,40,128]{2,1,0:T(8,128)(2,1)} %broadcast_in_dim.13), calls=%async_computation.2 | async-start | bytes 655360 | tf_op jit(solution)/shard_map/all_to_all | solution.py:36
  45.3 4.9 %copy-start = (bf16[3,3,3,128,128]{4,3,2,1,0:T(8,128)(2,1)S(1)}, bf16[3,3,3,128,128]{4,3,2,1,0:T(8,128)(2,1)}, u32[]{:S(2)}) copy-start(bf16[3,3,3,128,128]{4,3,2,1,0:T(8,128)(2,1)} %param.11) | copy-start | bytes 2654212
  45.3 4.9 %copy-start.4 = (s32[6]{0:T(128)S(1)}, s32[6]{0:T(128)}, u32[]{:S(2)}) copy-start(s32[6]{0:T(128)} %stack.44.at_ref) | copy-start | bytes 76
  50.3 1.0 copy-start.2
  52.6 13.2 %copy-start.1 = (bf16[576,128]{1,0:T(8,128)(2,1)}, bf16[576,128]{1,0:T(8,128)(2,1)S(1)}, u32[]{:S(2)}) copy-start(bf16[576,128]{1,0:T(8,128)(2,1)S(1)} %get-tuple-element.20.refs_0_.f_ref) | copy-start | bytes 442372
  52.6 6.3 %collective-permute-start.1 = (bf16[576,128]{1,0:T(8,128)(2,1)S(1)}, bf16[576,128]{1,0:T(8,128)(2,1)S(1)}, u32[]{:S(2)}, u32[]{:S(2)}) collective-permute-start(bf16[576,128]{1,0:T(8,128)(2,1)S(1)} %get-tuple-element.21), channel_id=1, source_target_pairs={{0,2},{2,4},{4,6},{6,0},{1,3},{3,5},{5,7},{7,1},{8,10},{10,12},{12... | collective-permute-start | bytes 442376 | tf_op jit(solution)/shard_map/ppermute | solution.py:470
  54.0 9.1 %collective-permute-start.2 = (bf16[576,128]{1,0:T(8,128)(2,1)S(1)}, bf16[576,128]{1,0:T(8,128)(2,1)S(1)}, u32[]{:S(2)}, u32[]{:S(2)}) collective-permute-start(bf16[576,128]{1,0:T(8,128)(2,1)S(1)} %get-tuple-element.22), channel_id=1, source_target_pairs={{0,4},{2,6},{4,0},{6,2},{1,5},{3,7},{5,1},{7,3},{8,12},{10,14},{12... | collective-permute-start | bytes 442376 | tf_op jit(solution)/shard_map/ppermute | solution.py:470
  56.5 8.0 %collective-permute-start.3 = (bf16[576,128]{1,0:T(8,128)(2,1)S(1)}, bf16[576,128]{1,0:T(8,128)(2,1)S(1)}, u32[]{:S(2)}, u32[]{:S(2)}) collective-permute-start(bf16[576,128]{1,0:T(8,128)(2,1)S(1)} %get-tuple-element.23), channel_id=1, source_target_pairs={{0,6},{2,0},{4,2},{6,4},{1,7},{3,1},{5,3},{7,5},{8,14},{10,8},{12,... | collective-permute-start | bytes 442376 | tf_op jit(solution)/shard_map/ppermute | solution.py:470
  57.6 7.1 %collective-permute-start.4 = (bf16[576,128]{1,0:T(8,128)(2,1)S(1)}, bf16[576,128]{1,0:T(8,128)(2,1)S(1)}, u32[]{:S(2)}, u32[]{:S(2)}) collective-permute-start(bf16[576,128]{1,0:T(8,128)(2,1)S(1)} %get-tuple-element.20.refs_0_.f_ref), channel_id=1, source_target_pairs={{0,1},{1,0},{2,3},{3,2},{4,5},{5,4},{6,7},{7,6},{8,9},{9,8},{10,11... | collective-permute-start | bytes 442376 | tf_op jit(solution)/shard_map/ppermute | solution.py:470
  58.9 6.9 %copy-start.6 = (bf16[576,128]{1,0:T(8,128)(2,1)}, bf16[576,128]{1,0:T(8,128)(2,1)S(1)}, u32[]{:S(2)}) copy-start(bf16[576,128]{1,0:T(8,128)(2,1)S(1)} %collective-permute-done.1.refs_1_) | copy-start | bytes 442372
  58.9 5.8 %collective-permute-start.5 = (bf16[576,128]{1,0:T(8,128)(2,1)S(1)}, bf16[576,128]{1,0:T(8,128)(2,1)S(1)}, u32[]{:S(2)}, u32[]{:S(2)}) collective-permute-start(bf16[576,128]{1,0:T(8,128)(2,1)S(1)} %collective-permute-done.1.refs_1_), channel_id=1, source_target_pairs={{0,1},{1,0},{2,3},{3,2},{4,5},{5,4},{6,7},{7,6},{8,9},{9,8},{10,11... | collective-permute-start | bytes 442376 | tf_op jit(solution)/shard_map/ppermute | solution.py:470
  63.2 2.6 %copy-start.7 = (bf16[576,128]{1,0:T(8,128)(2,1)}, bf16[576,128]{1,0:T(8,128)(2,1)S(1)}, u32[]{:S(2)}) copy-start(bf16[576,128]{1,0:T(8,128)(2,1)S(1)} %collective-permute-done.2.refs_2_) | copy-start | bytes 442372
  63.2 2.3 %collective-permute-start.6 = (bf16[576,128]{1,0:T(8,128)(2,1)S(1)}, bf16[576,128]{1,0:T(8,128)(2,1)S(1)}, u32[]{:S(2)}, u32[]{:S(2)}) collective-permute-start(bf16[576,128]{1,0:T(8,128)(2,1)S(1)} %collective-permute-done.2.refs_2_), channel_id=1, source_target_pairs={{0,1},{1,0},{2,3},{3,2},{4,5},{5,4},{6,7},{7,6},{8,9},{9,8},{10,11... | collective-permute-start | bytes 442376 | tf_op jit(solution)/shard_map/ppermute | solution.py:470
  64.4 1.4 %copy-start.8 = (bf16[576,128]{1,0:T(8,128)(2,1)}, bf16[576,128]{1,0:T(8,128)(2,1)S(1)}, u32[]{:S(2)}) copy-start(bf16[576,128]{1,0:T(8,128)(2,1)S(1)} %collective-permute-done.3.refs_3_) | copy-start | bytes 442372
  64.4 1.4 %collective-permute-start.7 = (bf16[576,128]{1,0:T(8,128)(2,1)S(1)}, bf16[576,128]{1,0:T(8,128)(2,1)S(1)}, u32[]{:S(2)}, u32[]{:S(2)}) collective-permute-start(bf16[576,128]{1,0:T(8,128)(2,1)S(1)} %collective-permute-done.3.refs_3_), channel_id=1, source_target_pairs={{0,1},{1,0},{2,3},{3,2},{4,5},{5,4},{6,7},{7,6},{8,9},{9,8},{10,11... | collective-permute-start | bytes 442376 | tf_op jit(solution)/shard_map/ppermute | solution.py:470
  64.7 1.1 copy-start.9
  64.7 1.1 copy-start.10
  65.4 0.7 copy-start.11
  65.8 0.7 copy-start.12
  69.7 0.8 copy-start.5
  78.1 10.6 %collective-permute-start.8 = (bf16[2,64,256]{2,1,0:T(8,128)(2,1)}, bf16[2,64,256]{2,1,0:T(8,128)(2,1)S(1)}, u32[]{:S(2)}, u32[]{:S(2)}) collective-permute-start(bf16[2,64,256]{2,1,0:T(8,128)(2,1)} %get-tuple-element.30), channel_id=1, source_target_pairs={{0,6},{2,0},{4,2},{6,4},{1,7},{3,1},{5,3},{7,5},{8,14},{10,8},{12,... | collective-permute-start | bytes 196616 | tf_op jit(solution)/shard_map/ppermute | solution.py:470
  79.6 9.1 %collective-permute-start.9 = (bf16[2,64,256]{2,1,0:T(8,128)(2,1)}, bf16[2,64,256]{2,1,0:T(8,128)(2,1)S(1)}, u32[]{:S(2)}, u32[]{:S(2)}) collective-permute-start(bf16[2,64,256]{2,1,0:T(8,128)(2,1)} %get-tuple-element.31), channel_id=1, source_target_pairs={{0,4},{2,6},{4,0},{6,2},{1,5},{3,7},{5,1},{7,3},{8,12},{10,14},{12... | collective-permute-start | bytes 196616 | tf_op jit(solution)/shard_map/ppermute | solution.py:470
  80.5 8.3 %collective-permute-start.10 = (bf16[2,64,256]{2,1,0:T(8,128)(2,1)}, bf16[2,64,256]{2,1,0:T(8,128)(2,1)S(1)}, u32[]{:S(2)}, u32[]{:S(2)}) collective-permute-start(bf16[2,64,256]{2,1,0:T(8,128)(2,1)} %get-tuple-element.32), channel_id=1, source_target_pairs={{0,2},{2,4},{4,6},{6,0},{1,3},{3,5},{5,7},{7,1},{8,10},{10,12},{12... | collective-permute-start | bytes 196616 | tf_op jit(solution)/shard_map/ppermute | solution.py:470
  81.0 15.4 %all-to-all-start.3 = ((bf16[32,16,128]{2,1,0:T(8,128)(2,1)}), bf16[32,16,128]{2,1,0:T(8,128)(2,1)S(1)}, u32[]{:S(2)}, u32[]{:S(2)}) async-start(bf16[32,16,128]{2,1,0:T(8,128)(2,1)} %bitcast.46), calls=%async_computation.3 | async-start | bytes 262144 | tf_op jit(solution)/shard_map/all_to_all | solution.py:36
  89.6 23.3 %collective-permute-start.11 = (bf16[4,64,256]{2,1,0:T(8,128)(2,1)S(1)}, bf16[4,64,256]{2,1,0:T(8,128)(2,1)S(1)}, u32[]{:S(2)}, u32[]{:S(2)}) collective-permute-start(bf16[4,64,256]{2,1,0:T(8,128)(2,1)S(1)} %get-tuple-element.37), channel_id=1, source_target_pairs={{0,1},{1,0},{2,3},{3,2},{4,5},{5,4},{6,7},{7,6},{8,9},{9,8},{10,11... | collective-permute-start | bytes 393224 | tf_op jit(solution)/shard_map/ppermute | solution.py:470
  97.0 10.1 %all-to-all-start.4 = ((bf16[8,16,128]{2,1,0:T(8,128)(2,1)}), bf16[8,16,128]{2,1,0:T(8,128)(2,1)S(1)}, u32[]{:S(2)}, u32[]{:S(2)}) async-start(bf16[8,16,128]{2,1,0:T(8,128)(2,1)} %broadcast_in_dim.14), calls=%async_computation.4 | async-start | bytes 65536 | tf_op jit(solution)/shard_map/all_to_all | solution.py:36
  107.9 12.8 %all-to-all-start.5 = ((bf16[32,16,128]{2,1,0:T(8,128)(2,1)}), bf16[32,16,128]{2,1,0:T(8,128)(2,1)S(1)}, u32[]{:S(2)}, u32[]{:S(2)}) async-start(bf16[32,16,128]{2,1,0:T(8,128)(2,1)} %broadcast_in_dim.15), calls=%async_computation.5 | async-start | bytes 262144 | tf_op jit(solution)/shard_map/all_to_all | solution.py:36
  113.9 6.8 %copy-start.13 = (bf16[20,128]{1,0:T(8,128)(2,1)S(1)}, bf16[20,128]{1,0:T(8,128)(2,1)}, u32[]{:S(2)}) copy-start(bf16[20,128]{1,0:T(8,128)(2,1)} %get-tuple-element.33) | copy-start | bytes 15364
  113.9 7.2 %copy-start.14 = (f32[20,384]{1,0:T(8,128)S(1)}, f32[20,384]{1,0:T(8,128)}, u32[]{:S(2)}) copy-start(f32[20,384]{1,0:T(8,128)} %get-tuple-element.35) | copy-start | bytes 92164

commit v7 on v6

--- a/solution.py
+++ b/solution.py
@@ -156,7 +156,9 @@
     )(embed, out_s, out_t, cot)
 
 
-def output_kernel(f_ref, mixes_ref, e_ref, os_ref, ot_ref, out_ref, weights, rows, arrived, sent):
+def output_kernel(at_ref, f_ref, *refs):
+    parts = refs[:8]
+    e_ref, os_ref, ot_ref, out_ref, weights, rows, arrived, sent = refs[8:]
     head, width = e_ref.shape
     copies = []
     for i in range(width // CHUNK):
@@ -168,7 +170,21 @@
         for copy in group:
             copy.start()
         copies.append(group)
-    x = jnp.concatenate([f_ref[: rows.shape[0]], mixes_ref[...]], axis=1)
+    line, core, spots = at_ref[2], at_ref[3], at_ref[5]
+    tokens = rows.shape[0]
+    places = tokens // 2
+    pad = parts[0].shape[1] // 2
+    r = lax.broadcasted_iota(jnp.int32, (places, 8 * pad), 0)
+    c = lax.broadcasted_iota(jnp.int32, (places, 8 * pad), 1)
+    step = (c // pad) % 4
+    side = c // (4 * pad)
+    slot = ((line + step) % 4) * 2 + core + side - 2 * core * side
+    place = jnp.where((r == slot * spots + c % pad) & (c % pad < spots), 1.0, 0.0).astype(bf16)
+    mixes = []
+    for f in range(2):
+        got = jnp.concatenate([ref[i // 4, f * pad : (f + 1) * pad] for i, ref in enumerate(parts)], axis=0)
+        mixes.append(nn(place, got).astype(bf16))
+    x = jnp.concatenate([f_ref[:tokens], jnp.concatenate(mixes, axis=0)], axis=1)
     leaving = []
     for i, group in enumerate(copies):
         for copy in group:
@@ -183,14 +199,13 @@
         copy.wait()
 
 
-def output_rows(feats, mixes, embed, out_s, out_t):
-    tokens = mixes.shape[0]
+def output_rows(at, feats, parts, embed, out_s, out_t, tokens):
     head, width = embed.shape
     hbm = pl.BlockSpec(memory_space=pl.ANY)
     vmem = pl.BlockSpec(memory_space=pltpu.VMEM)
     return pl.pallas_call(
         output_kernel,
-        in_specs=[vmem, vmem, hbm, hbm, hbm],
+        in_specs=[pl.BlockSpec(memory_space=pltpu.SMEM)] + [vmem] * 9 + [hbm] * 3,
         out_specs=hbm,
         out_shape=jax.ShapeDtypeStruct((tokens, width), bf16),
         scratch_shapes=[
@@ -200,18 +215,20 @@
             pltpu.SemaphoreType.DMA((width // CHUNK,)),
         ],
         name="output_rows",
-    )(feats, mixes, embed, out_s, out_t)
+    )(at, feats, *parts, embed, out_s, out_t)
 
 
 def maps_kernel(
     at_ref, ws_ref, wt_ref, e_ref, os_ref, gs_ref, gt_ref,
-    maps_ref, e_mine_ref, g_mine_ref, factors, gains, arrived,
+    maps_ref, e_mine_ref, g_mine_ref, factors, gains, projections, arrived,
 ):
     rows, triple = ws_ref.shape
     head = e_ref.shape[0]
     wide = factors.shape[1]
     cols = pl.ds(pl.multiple_of(at_ref[0] * wide, 128), wide)
     copies = [
+        pltpu.make_async_copy(ws_ref, projections.at[0], arrived.at[4]),
+        pltpu.make_async_copy(wt_ref, projections.at[1], arrived.at[5]),
         pltpu.make_async_copy(e_ref.at[:, cols], factors.at[pl.ds(0, head)], arrived.at[0]),
         pltpu.make_async_copy(os_ref.at[:, cols], factors.at[pl.ds(head, head)], arrived.at[1]),
         pltpu.make_async_copy(gs_ref.at[:, cols], gains.at[0], arrived.at[2]),
@@ -224,11 +241,11 @@
     c = lax.broadcasted_iota(jnp.int32, (rows, wide), 1)
     chosen = jnp.where(c == r + first, 1.0, 0.0)
     pick = chosen.astype(bf16)
-    placed_s = tn(ws_ref[...], pick).astype(bf16)
-    placed_t = tn(wt_ref[...], pick).astype(bf16)
     maps_ref[3 * triple :] = jnp.zeros((maps_ref.shape[0] - 3 * triple, head), bf16)
     for copy in copies:
         copy.wait()
+    placed_s = tn(projections[0], pick).astype(bf16)
+    placed_t = tn(projections[1], pick).astype(bf16)
 
     def product(placed, scaled):
         high = scaled.astype(bf16)
@@ -254,7 +271,7 @@
     vmem = pl.BlockSpec(memory_space=pltpu.VMEM)
     return pl.pallas_call(
         maps_kernel,
-        in_specs=[pl.BlockSpec(memory_space=pltpu.SMEM), vmem, vmem, hbm, hbm, hbm, hbm],
+        in_specs=[pl.BlockSpec(memory_space=pltpu.SMEM)] + [hbm] * 6,
         out_specs=[vmem, vmem, vmem],
         out_shape=[
             jax.ShapeDtypeStruct((padded, head), bf16),
@@ -264,7 +281,8 @@
         scratch_shapes=[
             pltpu.VMEM((2 * head, wide), bf16),
             pltpu.VMEM((2, 1, wide), f32),
-            pltpu.SemaphoreType.DMA((4,)),
+            pltpu.VMEM((2, rows, triple), bf16),
+            pltpu.SemaphoreType.DMA((6,)),
         ],
         name="local_maps",
     )(at, w_s, w_t, embed, out_s, gain_s.reshape(1, width), gain_t.reshape(1, width))
@@ -530,17 +548,13 @@
     total = gathered(scattered(total), total.shape)
     grad = jnp.concatenate([nn(e_mine, total[b * head : (b + 1) * head]) for b in range(3)], axis=1) * g_mine
 
-    moved = []
+    near = [back[0]]
     for step in range(1, n_line):
-        moved.append(turned(back[step], "y", -step))
-    back = jnp.stack([back[0]] + moved)
-    away = turned(back[:, 1], "c", 1)
-    home = jnp.stack([back[:, 0], away], axis=1)
-    home = jnp.where(core == 0, home, home[:, ::-1])
-    home = lax.dynamic_slice_in_dim(jnp.concatenate([home, home], axis=0), (n_line - line) % n_line, n_line, 0)
-    home = home.reshape(n_line, 2, frames, pad, 2 * head)[:, :, :, :spots]
-    home = home.transpose(2, 0, 1, 3, 4).reshape(tokens, 2 * head)
-    layer = output_rows(feats_home, home, embed_weight, output_spatial, output_temporal)
+        near.append(turned(back[step], "y", -step))
+    other = []
+    for step in range(n_line):
+        other.append(turned(near[step], "c", 1))
+    layer = output_rows(at, feats_home, near + other, embed_weight, output_spatial, output_temporal, tokens)
     return (layer.reshape(frames, height, columns, width), grad)
 
 

time: 123 us -> 120 us (0.976)
  blocking collectives: 18.2 us -> 32.5 us
  waiting for transfers between devices: 23.8 us -> 15.2 us
  starting transfers between devices: 43.8 us -> 36.1 us
    all_to_all x1 -> x2, blocking collectives: 18.2 us -> 32.5 us  [exchange(): return lax.all_to_all(parts, axes, 0, 0, tiled=True)]
    all_to_all x5 -> x4, waiting for transfers between devices: 19.6 us -> 9.95 us  [exchange(): return lax.all_to_all(parts, axes, 0, 0, tiled=True)]
    all_to_all x5 -> x4, starting transfers between devices: 29.6 us -> 21.8 us  [exchange(): return lax.all_to_all(parts, axes, 0, 0, tiled=True)]
    ppermute x11 -> x14, waiting for transfers between devices: 4.19 us -> 5.27 us  [turned(): return lax.ppermute(value, axis, [(i, (i + step) % n) for i in range(n)])]
    unnamed x31 -> x44, local copies, waits for them, and re-layouts: 2.38 us -> 3.25 us
    ppermute x11 -> x14, starting transfers between devices: 12.2 us -> 12.2 us  [turned(): return lax.ppermute(value, axis, [(i, (i + step) % n) for i in range(n)])]
  transfers between devices with their start and end apart: 17 -> 19, of which waited for: 8 -> 10; matrix products, arithmetic and copies ran while one was open for 3% -> 1% of each run, Pallas kernels for 12% -> 13%
where the time goes in v7:
time: 120 us; the launch traced here: 119 us
  starting transfers between devices  36.1 us (30%)
  blocking collectives  32.5 us (27%)
  Pallas kernels  26.8 us (22%)
  waiting for transfers between devices  15.2 us (13%)
  local copies, waits for them, and re-layouts  6.6 us (6%)
    all_to_all x2, blocking collectives, exchange(): return lax.all_to_all(parts, axes, 0, 0, tiled=True)  32.5 us
    all_to_all x4, starting transfers between devices, exchange(): return lax.all_to_all(parts, axes, 0, 0, tiled=True)  21.8 us
    ppermute x14, starting transfers between devices, turned(): return lax.ppermute(value, axis, [(i, (i + step) % n) for i in range(n)])  12.2 us
    all_to_all x4, waiting for transfers between devices, exchange(): return lax.all_to_all(parts, axes, 0, 0, tiled=True)  9.95 us
    pallas_call x1, Pallas kernels, attend_all(): pl.pallas_call(attend_kernel, in_specs=[pl.BlockSpec(memory_space=pltpu.S...  7.65 us
    pallas_call x1, Pallas kernels, output_rows(): pl.pallas_call(output_kernel, in_specs=[pl.BlockSpec(memory_space=pltpu.S...  5.81 us
    ppermute x14, waiting for transfers between devices, turned(): return lax.ppermute(value, axis, [(i, (i + step) % n) for i in range(n)])  5.27 us
    pallas_call x1, Pallas kernels, products(): pl.pallas_call(products_kernel, in_specs=[hbm] * 4, out_specs=[vmem, vmem...  4.9 us
  transfers between devices with their start and end apart: 19, of which 10 were waited for; matrix products, arithmetic and copies ran while one was open for 1% of the time, Pallas kernels for 13%

profile of v7, /device:TPU:1, one launch (start us, length us, event | category | flops | bytes accessed | tf_op | source)
XLA Modules:
  0.0 119.2 jit_solution(10749638914055080359)
XLA Ops:
  0.6 0.6 stack.23.at_ref
  1.3 3.9 %local_maps.1 = (bf16[1280,128]{1,0:T(8,128)(2,1)}, bf16[20,128]{1,0:T(8,128)(2,1)}, f32[20,384]{1,0:T(8,128)}) custom-call(s32[6]{0:T(128)} %stack.23.at_ref, bf16[20,384]{1,0:T(8,128)(2,1)} %ws_ref.1, bf16[20,384]{1,0:T(8,128)(2,1)} %wt_ref.1, bf16[128,5120]{1,0:T(8,128)(2,1)} %refs_8_.1, bf16[128,5120]{1,0:T(8,128)(2,1)} %refs_9_.1, f32[1,5120]{1,0:T(1,128)} %bitcast.37, ...), custom_call_target="tpu_custom_call" | custom-call | tf_op jit(solution)/shard_map/local_maps/pallas_call | solution.py:272
  5.2 18.2 %all_to_all.30 = bf16[32,40,128]{2,1,0:T(8,128)(2,1)S(1)} all-to-all(bf16[32,40,128]{2,1,0:T(8,128)(2,1)} %bitcast.32), channel_id=1, replica_groups=mesh['x'=4,'zh'=2,'zl'=4,'y'=4,'c'=2] {'x','y','c'}, dimensions={0} | all-to-all | bytes 655360 | tf_op jit(solution)/shard_map/all_to_all | solution.py:36
  23.4 0.6 broadcast_in_dim.12
  24.1 8.2 %all-to-all-start.1 = ((bf16[8,40,128]{2,1,0:T(8,128)(2,1)}), bf16[8,40,128]{2,1,0:T(8,128)(2,1)S(1)}, u32[]{:S(2)}, u32[]{:S(2)}) async-start(bf16[8,40,128]{2,1,0:T(8,128)(2,1)} %broadcast_in_dim.12), calls=%async_computation.1 | async-start | bytes 163840 | tf_op jit(solution)/shard_map/all_to_all | solution.py:36
  32.3 2.0 %collective-permute-start = (bf16[2,4,40,128]{3,2,1,0:T(8,128)(2,1)S(1)}, bf16[2,4,40,128]{3,2,1,0:T(8,128)(2,1)S(1)}, u32[]{:S(2)}, u32[]{:S(2)}) collective-permute-start(bf16[2,4,40,128]{3,2,1,0:T(8,128)(2,1)S(1)} %copy-done.3), channel_id=1, source_target_pairs={{0,1},{1,2},{2,3},{3,4},{4,5},{5,6},{6,7},{7,8},{8,9},{9,10},{10,1... | collective-permute-start | bytes 245768 | tf_op jit(solution)/shard_map/ppermute | solution.py:511
  34.3 5.3 %all-to-all-done.1 = bf16[8,40,128]{2,1,0:T(8,128)(2,1)S(1)} async-done(((bf16[8,40,128]{2,1,0:T(8,128)(2,1)}), bf16[8,40,128]{2,1,0:T(8,128)(2,1)S(1)}, u32[]{:S(2)}, u32[]{:S(2)}) %all-to-all-start.1) | async-done | bytes 81952 | tf_op jit(solution)/shard_map/all_to_all | solution.py:36
  39.6 0.8 broadcast_in_dim.13
  40.4 5.3 %all-to-all-start.2 = ((bf16[32,40,128]{2,1,0:T(8,128)(2,1)}), bf16[32,40,128]{2,1,0:T(8,128)(2,1)S(1)}, u32[]{:S(2)}, u32[]{:S(2)}) async-start(bf16[32,40,128]{2,1,0:T(8,128)(2,1)} %broadcast_in_dim.13), calls=%async_computation.2 | async-start | bytes 655360 | tf_op jit(solution)/shard_map/all_to_all | solution.py:36
  45.7 4.9 %products.1 = (f32[256,256]{1,0:T(8,128)}, bf16[8,2,2,32,128]{4,3,2,1,0:T(8,128)(2,1)}) custom-call(bf16[128,5120]{1,0:T(8,128)(2,1)} %refs_8_.1, bf16[128,5120]{1,0:T(8,128)(2,1)} %refs_9_.1, bf16[128,5120]{1,0:T(8,128)(2,1)} %refs_10_.1, bf16[320,5120]{1,0:T(8,128)(2,1)} %bitcast.29), custom_call_target="tpu_custom_call" | custom-call | tf_op jit(solution)/shard_map/products/pallas_call | solution.py:140
  50.7 0.9 copy-done.2
  51.6 1.4 %conv_rows.1 = (bf16[576,128]{1,0:T(8,128)(2,1)S(1)}, bf16[576,128]{1,0:T(8,128)(2,1)S(1)}, bf16[576,128]{1,0:T(8,128)(2,1)S(1)}, bf16[576,128]{1,0:T(8,128)(2,1)S(1)}) custom-call(s32[6]{0:T(128)S(1)} %copy-done.4, bf16[320,128]{1,0:T(8,128)(2,1)S(1)} %bitcast.28, bf16[320,128]{1,0:T(8,128)(2,1)S(1)} %bitcast.27, bf16[9,384,128]{2,1,0:T(8,128)(2,1)S(1)} %bitcast.25, ...), custom_call_target="tpu_custom_call" | custom-call | tf_op jit(solution)/shard_map/conv_rows/pallas_call | solution.py:84
  53.0 1.4 %collective-permute-start.1 = (bf16[576,128]{1,0:T(8,128)(2,1)S(1)}, bf16[576,128]{1,0:T(8,128)(2,1)S(1)}, u32[]{:S(2)}, u32[]{:S(2)}) collective-permute-start(bf16[576,128]{1,0:T(8,128)(2,1)S(1)} %get-tuple-element.21), channel_id=1, source_target_pairs={{0,2},{2,4},{4,6},{6,0},{1,3},{3,5},{5,7},{7,1},{8,10},{10,12},{12... | collective-permute-start | bytes 442376 | tf_op jit(solution)/shard_map/ppermute | solution.py:488
  54.4 2.4 %collective-permute-start.2 = (bf16[576,128]{1,0:T(8,128)(2,1)S(1)}, bf16[576,128]{1,0:T(8,128)(2,1)S(1)}, u32[]{:S(2)}, u32[]{:S(2)}) collective-permute-start(bf16[576,128]{1,0:T(8,128)(2,1)S(1)} %get-tuple-element.22), channel_id=1, source_target_pairs={{0,4},{2,6},{4,0},{6,2},{1,5},{3,7},{5,1},{7,3},{8,12},{10,14},{12... | collective-permute-start | bytes 442376 | tf_op jit(solution)/shard_map/ppermute | solution.py:488
  56.8 1.2 collective-permute-start.3
  58.0 1.2 %collective-permute-start.4 = (bf16[576,128]{1,0:T(8,128)(2,1)S(1)}, bf16[576,128]{1,0:T(8,128)(2,1)S(1)}, u32[]{:S(2)}, u32[]{:S(2)}) collective-permute-start(bf16[576,128]{1,0:T(8,128)(2,1)S(1)} %get-tuple-element.20.refs_0_.f_ref), channel_id=1, source_target_pairs={{0,1},{1,0},{2,3},{3,2},{4,5},{5,4},{6,7},{7,6},{8,9},{9,8},{10,11... | collective-permute-start | bytes 442376 | tf_op jit(solution)/shard_map/ppermute | solution.py:488
  59.3 1.2 %collective-permute-start.5 = (bf16[576,128]{1,0:T(8,128)(2,1)S(1)}, bf16[576,128]{1,0:T(8,128)(2,1)S(1)}, u32[]{:S(2)}, u32[]{:S(2)}) collective-permute-start(bf16[576,128]{1,0:T(8,128)(2,1)S(1)} %collective-permute-done.1.refs_1_), channel_id=1, source_target_pairs={{0,1},{1,0},{2,3},{3,2},{4,5},{5,4},{6,7},{7,6},{8,9},{9,8},{10,11... | collective-permute-start | bytes 442376 | tf_op jit(solution)/shard_map/ppermute | solution.py:488
  60.5 3.0 %collective-permute-done.2.refs_2_ = bf16[576,128]{1,0:T(8,128)(2,1)S(1)} collective-permute-done((bf16[576,128]{1,0:T(8,128)(2,1)S(1)}, bf16[576,128]{1,0:T(8,128)(2,1)S(1)}, u32[]{:S(2)}, u32[]{:S(2)}) %collective-permute-start.2) | collective-permute-done | bytes 147488 | tf_op jit(solution)/shard_map/ppermute | solution.py:488
  63.6 1.2 %collective-permute-start.6 = (bf16[576,128]{1,0:T(8,128)(2,1)S(1)}, bf16[576,128]{1,0:T(8,128)(2,1)S(1)}, u32[]{:S(2)}, u32[]{:S(2)}) collective-permute-start(bf16[576,128]{1,0:T(8,128)(2,1)S(1)} %collective-permute-done.2.refs_2_), channel_id=1, source_target_pairs={{0,1},{1,0},{2,3},{3,2},{4,5},{5,4},{6,7},{7,6},{8,9},{9,8},{10,11... | collective-permute-start | bytes 442376 | tf_op jit(solution)/shard_map/ppermute | solution.py:488
  65.1 0.7 collective-permute-done.6.refs_6_
  66.8 3.2 %norm_rows.1 = (bf16[2560,128]{1,0:T(8,128)(2,1)}, bf16[2560,128]{1,0:T(8,128)(2,1)}, bf16[2,4,2,64,128]{4,3,2,1,0:T(8,128)(2,1)}) custom-call(s32[6]{0:T(128)} %stack.23.at_ref, bf16[576,128]{1,0:T(8,128)(2,1)} %copy-done.1, bf16[576,128]{1,0:T(8,128)(2,1)} %copy-done.6, bf16[576,128]{1,0:T(8,128)(2,1)} %copy-done.7, bf16[576,128]{1,0:T(8,128)(2,1)} %copy-done.8, ...), custom_call_target="tpu_custom_call" | custom-call | tf_op jit(solution)/shard_map/norm_rows/pallas_call | solution.py:318
  70.0 0.7 copy-done.5
  70.8 7.6 %attend_all.1 = (bf16[512,128]{1,0:T(8,128)(2,1)}, bf16[2,64,256]{2,1,0:T(8,128)(2,1)}, bf16[2,64,256]{2,1,0:T(8,128)(2,1)}, bf16[2,64,256]{2,1,0:T(8,128)(2,1)}, bf16[2,64,256]{2,1,0:T(8,128)(2,1)}) custom-call(s32[6]{0:T(128)} %stack.23.at_ref, bf16[2560,128]{1,0:T(8,128)(2,1)} %get-tuple-element.25.flat_ref, ...), custom_call_target="tpu_custom_call" | custom-call | tf_op jit(solution)/shard_map/attend_all/pallas_call | solution.py:466
  78.4 14.3 %all_to_all.31 = bf16[32,16,128]{2,1,0:T(8,128)(2,1)S(1)} all-to-all(bf16[32,16,128]{2,1,0:T(8,128)(2,1)} %bitcast.33), channel_id=1, replica_groups=mesh['x'=4,'zh'=2,'zl'=4,'y'=4,'c'=2] {'x','y','c'}, dimensions={0} | all-to-all | bytes 262144 | tf_op jit(solution)/shard_map/all_to_all | solution.py:36
  93.4 3.3 %all-to-all-start.4 = ((bf16[8,16,128]{2,1,0:T(8,128)(2,1)}), bf16[8,16,128]{2,1,0:T(8,128)(2,1)S(1)}, u32[]{:S(2)}, u32[]{:S(2)}) async-start(bf16[8,16,128]{2,1,0:T(8,128)(2,1)} %broadcast_in_dim.14), calls=%async_computation.4 | async-start | bytes 65536 | tf_op jit(solution)/shard_map/all_to_all | solution.py:36
  96.7 1.0 collective-permute-start.8
  97.7 1.1 collective-permute-start.9
  98.8 4.7 %all-to-all-done.4 = bf16[8,16,128]{2,1,0:T(8,128)(2,1)S(1)} async-done(((bf16[8,16,128]{2,1,0:T(8,128)(2,1)}), bf16[8,16,128]{2,1,0:T(8,128)(2,1)S(1)}, u32[]{:S(2)}, u32[]{:S(2)}) %all-to-all-start.4) | async-done | bytes 32800 | tf_op jit(solution)/shard_map/all_to_all | solution.py:36
  103.5 0.7 broadcast_in_dim.15
  104.2 5.0 %all-to-all-start.5 = ((bf16[32,16,128]{2,1,0:T(8,128)(2,1)}), bf16[32,16,128]{2,1,0:T(8,128)(2,1)S(1)}, u32[]{:S(2)}, u32[]{:S(2)}) async-start(bf16[32,16,128]{2,1,0:T(8,128)(2,1)} %broadcast_in_dim.15), calls=%async_computation.5 | async-start | bytes 262144 | tf_op jit(solution)/shard_map/all_to_all | solution.py:36
  112.4 5.8 %output_rows.1 = bf16[320,5120]{1,0:T(8,128)(2,1)} custom-call(s32[6]{0:T(128)} %stack.23.at_ref, bf16[576,128]{1,0:T(8,128)(2,1)} %copy-done.1, bf16[2,64,256]{2,1,0:T(8,128)(2,1)} %get-tuple-element.29.refs_0_, bf16[2,64,256]{2,1,0:T(8,128)(2,1)} %copy-done.13, bf16[2,64,256]{2,1,0:T(8,128)(2,1)} %copy-done.14, bf16[2,64,256]{2,1,0:T(8,128)(2,1)} %copy-done.15, ...), custom_call_target="tpu_custom_call" | custom-call | tf_op jit(solution)/shard_map/output_rows/pallas_call | solution.py:206
  118.6 0.6 maximum_multiply_fusion
  (72 shorter events, 5.7 us)
Async XLA Ops:
  1.3 31.0 %copy-start.3 = (bf16[2,4,40,128]{3,2,1,0:T(8,128)(2,1)S(1)}, bf16[2,4,40,128]{3,2,1,0:T(8,128)(2,1)}, u32[]{:S(2)}) copy-start(bf16[2,4,40,128]{3,2,1,0:T(8,128)(2,1)} %param.10) | copy-start | bytes 245764
  24.1 15.5 %all-to-all-start.1 = ((bf16[8,40,128]{2,1,0:T(8,128)(2,1)}), bf16[8,40,128]{2,1,0:T(8,128)(2,1)S(1)}, u32[]{:S(2)}, u32[]{:S(2)}) async-start(bf16[8,40,128]{2,1,0:T(8,128)(2,1)} %broadcast_in_dim.12), calls=%async_computation.1 | async-start | bytes 163840 | tf_op jit(solution)/shard_map/all_to_all | solution.py:36
  32.3 18.3 %collective-permute-start = (bf16[2,4,40,128]{3,2,1,0:T(8,128)(2,1)S(1)}, bf16[2,4,40,128]{3,2,1,0:T(8,128)(2,1)S(1)}, u32[]{:S(2)}, u32[]{:S(2)}) collective-permute-start(bf16[2,4,40,128]{3,2,1,0:T(8,128)(2,1)S(1)} %copy-done.3), channel_id=1, source_target_pairs={{0,1},{1,2},{2,3},{3,4},{4,5},{5,6},{6,7},{7,8},{8,9},{9,10},{10,1... | collective-permute-start | bytes 245768 | tf_op jit(solution)/shard_map/ppermute | solution.py:511
  40.4 29.6 %all-to-all-start.2 = ((bf16[32,40,128]{2,1,0:T(8,128)(2,1)}), bf16[32,40,128]{2,1,0:T(8,128)(2,1)S(1)}, u32[]{:S(2)}, u32[]{:S(2)}) async-start(bf16[32,40,128]{2,1,0:T(8,128)(2,1)} %broadcast_in_dim.13), calls=%async_computation.2 | async-start | bytes 655360 | tf_op jit(solution)/shard_map/all_to_all | solution.py:36
  45.7 4.9 %copy-start = (bf16[3,3,3,128,128]{4,3,2,1,0:T(8,128)(2,1)S(1)}, bf16[3,3,3,128,128]{4,3,2,1,0:T(8,128)(2,1)}, u32[]{:S(2)}) copy-start(bf16[3,3,3,128,128]{4,3,2,1,0:T(8,128)(2,1)} %param.11) | copy-start | bytes 2654212
  45.7 4.9 %copy-start.4 = (s32[6]{0:T(128)S(1)}, s32[6]{0:T(128)}, u32[]{:S(2)}) copy-start(s32[6]{0:T(128)} %stack.23.at_ref) | copy-start | bytes 76
  53.0 13.2 %copy-start.1 = (bf16[576,128]{1,0:T(8,128)(2,1)}, bf16[576,128]{1,0:T(8,128)(2,1)S(1)}, u32[]{:S(2)}) copy-start(bf16[576,128]{1,0:T(8,128)(2,1)S(1)} %get-tuple-element.20.refs_0_.f_ref) | copy-start | bytes 442372
  53.0 6.3 %collective-permute-start.1 = (bf16[576,128]{1,0:T(8,128)(2,1)S(1)}, bf16[576,128]{1,0:T(8,128)(2,1)S(1)}, u32[]{:S(2)}, u32[]{:S(2)}) collective-permute-start(bf16[576,128]{1,0:T(8,128)(2,1)S(1)} %get-tuple-element.21), channel_id=1, source_target_pairs={{0,2},{2,4},{4,6},{6,0},{1,3},{3,5},{5,7},{7,1},{8,10},{10,12},{12... | collective-permute-start | bytes 442376 | tf_op jit(solution)/shard_map/ppermute | solution.py:488
  54.4 9.1 %collective-permute-start.2 = (bf16[576,128]{1,0:T(8,128)(2,1)S(1)}, bf16[576,128]{1,0:T(8,128)(2,1)S(1)}, u32[]{:S(2)}, u32[]{:S(2)}) collective-permute-start(bf16[576,128]{1,0:T(8,128)(2,1)S(1)} %get-tuple-element.22), channel_id=1, source_target_pairs={{0,4},{2,6},{4,0},{6,2},{1,5},{3,7},{5,1},{7,3},{8,12},{10,14},{12... | collective-permute-start | bytes 442376 | tf_op jit(solution)/shard_map/ppermute | solution.py:488
  56.8 8.0 %collective-permute-start.3 = (bf16[576,128]{1,0:T(8,128)(2,1)S(1)}, bf16[576,128]{1,0:T(8,128)(2,1)S(1)}, u32[]{:S(2)}, u32[]{:S(2)}) collective-permute-start(bf16[576,128]{1,0:T(8,128)(2,1)S(1)} %get-tuple-element.23), channel_id=1, source_target_pairs={{0,6},{2,0},{4,2},{6,4},{1,7},{3,1},{5,3},{7,5},{8,14},{10,8},{12,... | collective-permute-start | bytes 442376 | tf_op jit(solution)/shard_map/ppermute | solution.py:488
  58.0 7.1 %collective-permute-start.4 = (bf16[576,128]{1,0:T(8,128)(2,1)S(1)}, bf16[576,128]{1,0:T(8,128)(2,1)S(1)}, u32[]{:S(2)}, u32[]{:S(2)}) collective-permute-start(bf16[576,128]{1,0:T(8,128)(2,1)S(1)} %get-tuple-element.20.refs_0_.f_ref), channel_id=1, source_target_pairs={{0,1},{1,0},{2,3},{3,2},{4,5},{5,4},{6,7},{7,6},{8,9},{9,8},{10,11... | collective-permute-start | bytes 442376 | tf_op jit(solution)/shard_map/ppermute | solution.py:488
  59.3 6.9 %copy-start.6 = (bf16[576,128]{1,0:T(8,128)(2,1)}, bf16[576,128]{1,0:T(8,128)(2,1)S(1)}, u32[]{:S(2)}) copy-start(bf16[576,128]{1,0:T(8,128)(2,1)S(1)} %collective-permute-done.1.refs_1_) | copy-start | bytes 442372
  59.3 5.8 %collective-permute-start.5 = (bf16[576,128]{1,0:T(8,128)(2,1)S(1)}, bf16[576,128]{1,0:T(8,128)(2,1)S(1)}, u32[]{:S(2)}, u32[]{:S(2)}) collective-permute-start(bf16[576,128]{1,0:T(8,128)(2,1)S(1)} %collective-permute-done.1.refs_1_), channel_id=1, source_target_pairs={{0,1},{1,0},{2,3},{3,2},{4,5},{5,4},{6,7},{7,6},{8,9},{9,8},{10,11... | collective-permute-start | bytes 442376 | tf_op jit(solution)/shard_map/ppermute | solution.py:488
  63.5 2.6 %copy-start.7 = (bf16[576,128]{1,0:T(8,128)(2,1)}, bf16[576,128]{1,0:T(8,128)(2,1)S(1)}, u32[]{:S(2)}) copy-start(bf16[576,128]{1,0:T(8,128)(2,1)S(1)} %collective-permute-done.2.refs_2_) | copy-start | bytes 442372
  63.6 2.3 %collective-permute-start.6 = (bf16[576,128]{1,0:T(8,128)(2,1)S(1)}, bf16[576,128]{1,0:T(8,128)(2,1)S(1)}, u32[]{:S(2)}, u32[]{:S(2)}) collective-permute-start(bf16[576,128]{1,0:T(8,128)(2,1)S(1)} %collective-permute-done.2.refs_2_), channel_id=1, source_target_pairs={{0,1},{1,0},{2,3},{3,2},{4,5},{5,4},{6,7},{7,6},{8,9},{9,8},{10,11... | collective-permute-start | bytes 442376 | tf_op jit(solution)/shard_map/ppermute | solution.py:488
  64.8 1.4 %copy-start.8 = (bf16[576,128]{1,0:T(8,128)(2,1)}, bf16[576,128]{1,0:T(8,128)(2,1)S(1)}, u32[]{:S(2)}) copy-start(bf16[576,128]{1,0:T(8,128)(2,1)S(1)} %collective-permute-done.3.refs_3_) | copy-start | bytes 442372
  64.8 1.4 %collective-permute-start.7 = (bf16[576,128]{1,0:T(8,128)(2,1)S(1)}, bf16[576,128]{1,0:T(8,128)(2,1)S(1)}, u32[]{:S(2)}, u32[]{:S(2)}) collective-permute-start(bf16[576,128]{1,0:T(8,128)(2,1)S(1)} %collective-permute-done.3.refs_3_), channel_id=1, source_target_pairs={{0,1},{1,0},{2,3},{3,2},{4,5},{5,4},{6,7},{7,6},{8,9},{9,8},{10,11... | collective-permute-start | bytes 442376 | tf_op jit(solution)/shard_map/ppermute | solution.py:488
  65.1 1.1 copy-start.10
  93.4 10.1 %all-to-all-start.4 = ((bf16[8,16,128]{2,1,0:T(8,128)(2,1)}), bf16[8,16,128]{2,1,0:T(8,128)(2,1)S(1)}, u32[]{:S(2)}, u32[]{:S(2)}) async-start(bf16[8,16,128]{2,1,0:T(8,128)(2,1)} %broadcast_in_dim.14), calls=%async_computation.4 | async-start | bytes 65536 | tf_op jit(solution)/shard_map/all_to_all | solution.py:36
  96.7 13.0 %collective-permute-start.8 = (bf16[2,64,256]{2,1,0:T(8,128)(2,1)}, bf16[2,64,256]{2,1,0:T(8,128)(2,1)S(1)}, u32[]{:S(2)}, u32[]{:S(2)}) collective-permute-start(bf16[2,64,256]{2,1,0:T(8,128)(2,1)} %get-tuple-element.30), channel_id=1, source_target_pairs={{0,6},{2,0},{4,2},{6,4},{1,7},{3,1},{5,3},{7,5},{8,14},{10,8},{12,... | collective-permute-start | bytes 196616 | tf_op jit(solution)/shard_map/ppermute | solution.py:488
  97.7 12.1 %collective-permute-start.9 = (bf16[2,64,256]{2,1,0:T(8,128)(2,1)}, bf16[2,64,256]{2,1,0:T(8,128)(2,1)S(1)}, u32[]{:S(2)}, u32[]{:S(2)}) collective-permute-start(bf16[2,64,256]{2,1,0:T(8,128)(2,1)} %get-tuple-element.31), channel_id=1, source_target_pairs={{0,4},{2,6},{4,0},{6,2},{1,5},{3,7},{5,1},{7,3},{8,12},{10,14},{12... | collective-permute-start | bytes 196616 | tf_op jit(solution)/shard_map/ppermute | solution.py:488
  98.8 11.4 %collective-permute-start.10 = (bf16[2,64,256]{2,1,0:T(8,128)(2,1)}, bf16[2,64,256]{2,1,0:T(8,128)(2,1)S(1)}, u32[]{:S(2)}, u32[]{:S(2)}) collective-permute-start(bf16[2,64,256]{2,1,0:T(8,128)(2,1)} %get-tuple-element.32), channel_id=1, source_target_pairs={{0,2},{2,4},{4,6},{6,0},{1,3},{3,5},{5,7},{7,1},{8,10},{10,12},{12... | collective-permute-start | bytes 196616 | tf_op jit(solution)/shard_map/ppermute | solution.py:488
  104.2 14.0 %all-to-all-start.5 = ((bf16[32,16,128]{2,1,0:T(8,128)(2,1)}), bf16[32,16,128]{2,1,0:T(8,128)(2,1)S(1)}, u32[]{:S(2)}, u32[]{:S(2)}) async-start(bf16[32,16,128]{2,1,0:T(8,128)(2,1)} %broadcast_in_dim.15), calls=%async_computation.5 | async-start | bytes 262144 | tf_op jit(solution)/shard_map/all_to_all | solution.py:36
  109.2 9.0 %copy-start.20 = (bf16[20,128]{1,0:T(8,128)(2,1)S(1)}, bf16[20,128]{1,0:T(8,128)(2,1)}, u32[]{:S(2)}) copy-start(bf16[20,128]{1,0:T(8,128)(2,1)} %get-tuple-element.33) | copy-start | bytes 15364
  109.2 9.4 %copy-start.21 = (f32[20,384]{1,0:T(8,128)S(1)}, f32[20,384]{1,0:T(8,128)}, u32[]{:S(2)}) copy-start(f32[20,384]{1,0:T(8,128)} %get-tuple-element.35) | copy-start | bytes 92164
  109.2 1.6 %collective-permute-start.11 = (bf16[2,64,256]{2,1,0:T(8,128)(2,1)}, bf16[2,64,256]{2,1,0:T(8,128)(2,1)S(1)}, u32[]{:S(2)}, u32[]{:S(2)}) collective-permute-start(bf16[2,64,256]{2,1,0:T(8,128)(2,1)} %get-tuple-element.29.refs_0_), channel_id=1, source_target_pairs={{0,1},{1,0},{2,3},{3,2},{4,5},{5,4},{6,7},{7,6},{8,9},{9,8},{10,11... | collective-permute-start | bytes 196616 | tf_op jit(solution)/shard_map/ppermute | solution.py:488
  109.7 1.8 %copy-start.13 = (bf16[2,64,256]{2,1,0:T(8,128)(2,1)}, bf16[2,64,256]{2,1,0:T(8,128)(2,1)S(1)}, u32[]{:S(2)}) copy-start(bf16[2,64,256]{2,1,0:T(8,128)(2,1)S(1)} %collective-permute-done.8.refs_1_) | copy-start | bytes 196612
  109.7 1.3 %collective-permute-start.12 = (bf16[2,64,256]{2,1,0:T(8,128)(2,1)S(1)}, bf16[2,64,256]{2,1,0:T(8,128)(2,1)S(1)}, u32[]{:S(2)}, u32[]{:S(2)}) collective-permute-start(bf16[2,64,256]{2,1,0:T(8,128)(2,1)S(1)} %collective-permute-done.8.refs_1_), channel_id=1, source_target_pairs={{0,1},{1,0},{2,3},{3,2},{4,5},{5,4},{6,7},{7,6},{8,9},{9,8},{10,11... | collective-permute-start | bytes 196616 | tf_op jit(solution)/shard_map/ppermute | solution.py:488
  109.8 1.6 %copy-start.14 = (bf16[2,64,256]{2,1,0:T(8,128)(2,1)}, bf16[2,64,256]{2,1,0:T(8,128)(2,1)S(1)}, u32[]{:S(2)}) copy-start(bf16[2,64,256]{2,1,0:T(8,128)(2,1)S(1)} %collective-permute-done.9.refs_2_) | copy-start | bytes 196612
  109.8 1.3 %collective-permute-start.13 = (bf16[2,64,256]{2,1,0:T(8,128)(2,1)S(1)}, bf16[2,64,256]{2,1,0:T(8,128)(2,1)S(1)}, u32[]{:S(2)}, u32[]{:S(2)}) collective-permute-start(bf16[2,64,256]{2,1,0:T(8,128)(2,1)S(1)} %collective-permute-done.9.refs_2_), channel_id=1, source_target_pairs={{0,1},{1,0},{2,3},{3,2},{4,5},{5,4},{6,7},{7,6},{8,9},{9,8},{10,11... | collective-permute-start | bytes 196616 | tf_op jit(solution)/shard_map/ppermute | solution.py:488
  110.2 1.3 %copy-start.15 = (bf16[2,64,256]{2,1,0:T(8,128)(2,1)}, bf16[2,64,256]{2,1,0:T(8,128)(2,1)S(1)}, u32[]{:S(2)}) copy-start(bf16[2,64,256]{2,1,0:T(8,128)(2,1)S(1)} %collective-permute-done.10.refs_3_) | copy-start | bytes 196612
  110.2 1.3 %collective-permute-start.14 = (bf16[2,64,256]{2,1,0:T(8,128)(2,1)S(1)}, bf16[2,64,256]{2,1,0:T(8,128)(2,1)S(1)}, u32[]{:S(2)}, u32[]{:S(2)}) collective-permute-start(bf16[2,64,256]{2,1,0:T(8,128)(2,1)S(1)} %collective-permute-done.10.refs_3_), channel_id=1, source_target_pairs={{0,1},{1,0},{2,3},{3,2},{4,5},{5,4},{6,7},{7,6},{8,9},{9,8},{10,11... | collective-permute-start | bytes 196616 | tf_op jit(solution)/shard_map/ppermute | solution.py:488
  (9 other events, 6.7 us)

commit v8 on v7

--- a/solution.py
+++ b/solution.py
@@ -156,13 +156,16 @@
     )(embed, out_s, out_t, cot)
 
 
+SLAB = 640
+
+
 def output_kernel(at_ref, f_ref, *refs):
     parts = refs[:8]
     e_ref, os_ref, ot_ref, out_ref, weights, rows, arrived, sent = refs[8:]
     head, width = e_ref.shape
     copies = []
-    for i in range(width // CHUNK):
-        cols = pl.ds(i * CHUNK, CHUNK)
+    for i in range(width // SLAB):
+        cols = pl.ds(i * SLAB, SLAB)
         group = [
             pltpu.make_async_copy(ref.at[:, cols], weights.at[pl.ds(k * head, head), cols], arrived.at[i, k])
             for k, ref in enumerate((e_ref, os_ref, ot_ref))
@@ -189,9 +192,9 @@
     for i, group in enumerate(copies):
         for copy in group:
             copy.wait()
-        cols = slice(i * CHUNK, (i + 1) * CHUNK)
+        cols = slice(i * SLAB, (i + 1) * SLAB)
         rows[:, cols] = nn(x, weights[:, cols]).astype(bf16)
-        cols = pl.ds(i * CHUNK, CHUNK)
+        cols = pl.ds(i * SLAB, SLAB)
         copy = pltpu.make_async_copy(rows.at[:, cols], out_ref.at[:, cols], sent.at[i])
         copy.start()
         leaving.append(copy)
@@ -211,9 +214,10 @@
         scratch_shapes=[
             pltpu.VMEM((3 * head, width), bf16),
             pltpu.VMEM((tokens, width), bf16),
-            pltpu.SemaphoreType.DMA((width // CHUNK, 3)),
-            pltpu.SemaphoreType.DMA((width // CHUNK,)),
-        ],
+            pltpu.SemaphoreType.DMA((width // SLAB, 3)),
+            pltpu.SemaphoreType.DMA((width // SLAB,)),
+        ],
+        compiler_params=pltpu.CompilerParams(vmem_limit_bytes=12 << 20),
         name="output_rows",
     )(at, feats, *parts, embed, out_s, out_t)
 

time: 120 us -> 122 us (1.017)
  local copies, waits for them, and re-layouts: 6.6 us -> 7.89 us
    unnamed x44 -> x42, local copies, waits for them, and re-layouts: 3.25 us -> 4.5 us
where the time goes in v8:
time: 122 us; the launch traced here: 121 us
  starting transfers between devices  36.4 us (30%)
  blocking collectives  32.5 us (27%)
  Pallas kernels  27 us (22%)
  waiting for transfers between devices  15.1 us (12%)
  local copies, waits for them, and re-layouts  7.89 us (6%)
    all_to_all x2, blocking collectives, exchange(): return lax.all_to_all(parts, axes, 0, 0, tiled=True)  32.5 us
    all_to_all x4, starting transfers between devices, exchange(): return lax.all_to_all(parts, axes, 0, 0, tiled=True)  22 us
    ppermute x14, starting transfers between devices, turned(): return lax.ppermute(value, axis, [(i, (i + step) % n) for i in range(n)])  12.4 us
    all_to_all x4, waiting for transfers between devices, exchange(): return lax.all_to_all(parts, axes, 0, 0, tiled=True)  9.95 us
    pallas_call x1, Pallas kernels, attend_all(): pl.pallas_call(attend_kernel, in_specs=[pl.BlockSpec(memory_space=pltpu.S...  7.82 us
    pallas_call x1, Pallas kernels, output_rows(): pl.pallas_call(output_kernel, in_specs=[pl.BlockSpec(memory_space=pltpu.S...  5.8 us
    ppermute x14, waiting for transfers between devices, turned(): return lax.ppermute(value, axis, [(i, (i + step) % n) for i in range(n)])  5.12 us
    pallas_call x1, Pallas kernels, products(): pl.pallas_call(products_kernel, in_specs=[hbm] * 4, out_specs=[vmem, vmem...  4.9 us
  transfers between devices with their start and end apart: 19, of which 10 were waited for; matrix products, arithmetic and copies ran while one was open for 1% of the time, Pallas kernels for 13%

profile of v8, /device:TPU:1, one launch (start us, length us, event | category | flops | bytes accessed | tf_op | source)
XLA Modules:
  0.0 120.8 jit_solution(7726391490143766885)
XLA Ops:
  0.6 0.7 stack.23.at_ref
  1.3 3.9 %local_maps.1 = (bf16[1280,128]{1,0:T(8,128)(2,1)}, bf16[20,128]{1,0:T(8,128)(2,1)}, f32[20,384]{1,0:T(8,128)}) custom-call(s32[6]{0:T(128)} %stack.23.at_ref, bf16[20,384]{1,0:T(8,128)(2,1)} %ws_ref.1, bf16[20,384]{1,0:T(8,128)(2,1)} %wt_ref.1, bf16[128,5120]{1,0:T(8,128)(2,1)} %refs_8_.1, bf16[128,5120]{1,0:T(8,128)(2,1)} %refs_9_.1, f32[1,5120]{1,0:T(1,128)} %bitcast.37, ...), custom_call_target="tpu_custom_call" | custom-call | tf_op jit(solution)/shard_map/local_maps/pallas_call | solution.py:276
  5.2 18.2 %all_to_all.30 = bf16[32,40,128]{2,1,0:T(8,128)(2,1)S(1)} all-to-all(bf16[32,40,128]{2,1,0:T(8,128)(2,1)} %bitcast.32), channel_id=1, replica_groups=mesh['x'=4,'zh'=2,'zl'=4,'y'=4,'c'=2] {'x','y','c'}, dimensions={0} | all-to-all | bytes 655360 | tf_op jit(solution)/shard_map/all_to_all | solution.py:36
  24.1 8.2 %all-to-all-start.1 = ((bf16[8,40,128]{2,1,0:T(8,128)(2,1)}), bf16[8,40,128]{2,1,0:T(8,128)(2,1)S(1)}, u32[]{:S(2)}, u32[]{:S(2)}) async-start(bf16[8,40,128]{2,1,0:T(8,128)(2,1)} %broadcast_in_dim.12), calls=%async_computation.1 | async-start | bytes 163840 | tf_op jit(solution)/shard_map/all_to_all | solution.py:36
  32.3 2.0 %collective-permute-start = (bf16[2,4,40,128]{3,2,1,0:T(8,128)(2,1)S(1)}, bf16[2,4,40,128]{3,2,1,0:T(8,128)(2,1)S(1)}, u32[]{:S(2)}, u32[]{:S(2)}) collective-permute-start(bf16[2,4,40,128]{3,2,1,0:T(8,128)(2,1)S(1)} %copy-done.7), channel_id=1, source_target_pairs={{0,1},{1,2},{2,3},{3,4},{4,5},{5,6},{6,7},{7,8},{8,9},{9,10},{10,1... | collective-permute-start | bytes 245768 | tf_op jit(solution)/shard_map/ppermute | solution.py:515
  34.3 5.3 %all-to-all-done.1 = bf16[8,40,128]{2,1,0:T(8,128)(2,1)S(1)} async-done(((bf16[8,40,128]{2,1,0:T(8,128)(2,1)}), bf16[8,40,128]{2,1,0:T(8,128)(2,1)S(1)}, u32[]{:S(2)}, u32[]{:S(2)}) %all-to-all-start.1) | async-done | bytes 81952 | tf_op jit(solution)/shard_map/all_to_all | solution.py:36
  39.6 0.8 broadcast_in_dim.13
  40.4 5.3 %all-to-all-start.2 = ((bf16[32,40,128]{2,1,0:T(8,128)(2,1)}), bf16[32,40,128]{2,1,0:T(8,128)(2,1)S(1)}, u32[]{:S(2)}, u32[]{:S(2)}) async-start(bf16[32,40,128]{2,1,0:T(8,128)(2,1)} %broadcast_in_dim.13), calls=%async_computation.2 | async-start | bytes 655360 | tf_op jit(solution)/shard_map/all_to_all | solution.py:36
  45.7 4.9 %products.1 = (f32[256,256]{1,0:T(8,128)}, bf16[8,2,2,32,128]{4,3,2,1,0:T(8,128)(2,1)}) custom-call(bf16[128,5120]{1,0:T(8,128)(2,1)} %refs_8_.1, bf16[128,5120]{1,0:T(8,128)(2,1)} %refs_9_.1, bf16[128,5120]{1,0:T(8,128)(2,1)} %refs_10_.1, bf16[320,5120]{1,0:T(8,128)(2,1)} %bitcast.29), custom_call_target="tpu_custom_call" | custom-call | tf_op jit(solution)/shard_map/products/pallas_call | solution.py:140
  50.7 0.9 copy-done.6
  51.6 1.4 %conv_rows.1 = (bf16[576,128]{1,0:T(8,128)(2,1)S(1)}, bf16[576,128]{1,0:T(8,128)(2,1)S(1)}, bf16[576,128]{1,0:T(8,128)(2,1)S(1)}, bf16[576,128]{1,0:T(8,128)(2,1)S(1)}) custom-call(s32[6]{0:T(128)S(1)} %copy-done.9, bf16[320,128]{1,0:T(8,128)(2,1)S(1)} %bitcast.28, bf16[320,128]{1,0:T(8,128)(2,1)S(1)} %bitcast.27, bf16[9,384,128]{2,1,0:T(8,128)(2,1)S(1)} %bitcast.25, ...), custom_call_target="tpu_custom_call" | custom-call | tf_op jit(solution)/shard_map/conv_rows/pallas_call | solution.py:84
  53.0 1.4 %collective-permute-start.1 = (bf16[576,128]{1,0:T(8,128)(2,1)S(1)}, bf16[576,128]{1,0:T(8,128)(2,1)S(1)}, u32[]{:S(2)}, u32[]{:S(2)}) collective-permute-start(bf16[576,128]{1,0:T(8,128)(2,1)S(1)} %get-tuple-element.21), channel_id=1, source_target_pairs={{0,2},{2,4},{4,6},{6,0},{1,3},{3,5},{5,7},{7,1},{8,10},{10,12},{12... | collective-permute-start | bytes 442376 | tf_op jit(solution)/shard_map/ppermute | solution.py:492
  54.4 2.4 %collective-permute-start.2 = (bf16[576,128]{1,0:T(8,128)(2,1)S(1)}, bf16[576,128]{1,0:T(8,128)(2,1)S(1)}, u32[]{:S(2)}, u32[]{:S(2)}) collective-permute-start(bf16[576,128]{1,0:T(8,128)(2,1)S(1)} %get-tuple-element.22), channel_id=1, source_target_pairs={{0,4},{2,6},{4,0},{6,2},{1,5},{3,7},{5,1},{7,3},{8,12},{10,14},{12... | collective-permute-start | bytes 442376 | tf_op jit(solution)/shard_map/ppermute | solution.py:492
  56.9 1.2 collective-permute-start.3
  58.0 1.2 %collective-permute-start.4 = (bf16[576,128]{1,0:T(8,128)(2,1)S(1)}, bf16[576,128]{1,0:T(8,128)(2,1)S(1)}, u32[]{:S(2)}, u32[]{:S(2)}) collective-permute-start(bf16[576,128]{1,0:T(8,128)(2,1)S(1)} %get-tuple-element.20.refs_0_.f_ref), channel_id=1, source_target_pairs={{0,1},{1,0},{2,3},{3,2},{4,5},{5,4},{6,7},{7,6},{8,9},{9,8},{10,11... | collective-permute-start | bytes 442376 | tf_op jit(solution)/shard_map/ppermute | solution.py:492
  59.3 1.2 %collective-permute-start.5 = (bf16[576,128]{1,0:T(8,128)(2,1)S(1)}, bf16[576,128]{1,0:T(8,128)(2,1)S(1)}, u32[]{:S(2)}, u32[]{:S(2)}) collective-permute-start(bf16[576,128]{1,0:T(8,128)(2,1)S(1)} %collective-permute-done.1.refs_1_), channel_id=1, source_target_pairs={{0,1},{1,0},{2,3},{3,2},{4,5},{5,4},{6,7},{7,6},{8,9},{9,8},{10,11... | collective-permute-start | bytes 442376 | tf_op jit(solution)/shard_map/ppermute | solution.py:492
  60.6 3.0 %collective-permute-done.2.refs_2_ = bf16[576,128]{1,0:T(8,128)(2,1)S(1)} collective-permute-done((bf16[576,128]{1,0:T(8,128)(2,1)S(1)}, bf16[576,128]{1,0:T(8,128)(2,1)S(1)}, u32[]{:S(2)}, u32[]{:S(2)}) %collective-permute-start.2) | collective-permute-done | bytes 147488 | tf_op jit(solution)/shard_map/ppermute | solution.py:492
  63.6 1.3 %collective-permute-start.6 = (bf16[576,128]{1,0:T(8,128)(2,1)S(1)}, bf16[576,128]{1,0:T(8,128)(2,1)S(1)}, u32[]{:S(2)}, u32[]{:S(2)}) collective-permute-start(bf16[576,128]{1,0:T(8,128)(2,1)S(1)} %collective-permute-done.2.refs_2_), channel_id=1, source_target_pairs={{0,1},{1,0},{2,3},{3,2},{4,5},{5,4},{6,7},{7,6},{8,9},{9,8},{10,11... | collective-permute-start | bytes 442376 | tf_op jit(solution)/shard_map/ppermute | solution.py:492
  65.1 0.7 collective-permute-done.6.refs_6_
  66.9 3.2 %norm_rows.1 = (bf16[2560,128]{1,0:T(8,128)(2,1)}, bf16[2560,128]{1,0:T(8,128)(2,1)}, bf16[2,4,2,64,128]{4,3,2,1,0:T(8,128)(2,1)}) custom-call(s32[6]{0:T(128)} %stack.23.at_ref, bf16[576,128]{1,0:T(8,128)(2,1)} %copy-done.4, bf16[576,128]{1,0:T(8,128)(2,1)} %copy-done.12, bf16[576,128]{1,0:T(8,128)(2,1)} %copy-done.13, bf16[576,128]{1,0:T(8,128)(2,1)} %copy-done.14, ...), custom_call_target="tpu_custom_call" | custom-call | tf_op jit(solution)/shard_map/norm_rows/pallas_call | solution.py:322
  70.0 0.7 copy-done.11
  70.8 7.8 %attend_all.1 = (bf16[512,128]{1,0:T(8,128)(2,1)}, bf16[2,64,256]{2,1,0:T(8,128)(2,1)}, bf16[2,64,256]{2,1,0:T(8,128)(2,1)}, bf16[2,64,256]{2,1,0:T(8,128)(2,1)}, bf16[2,64,256]{2,1,0:T(8,128)(2,1)}) custom-call(s32[6]{0:T(128)} %stack.23.at_ref, bf16[2560,128]{1,0:T(8,128)(2,1)} %get-tuple-element.25.flat_ref, ...), custom_call_target="tpu_custom_call" | custom-call | tf_op jit(solution)/shard_map/attend_all/pallas_call | solution.py:470
  78.6 14.3 %all_to_all.31 = bf16[32,16,128]{2,1,0:T(8,128)(2,1)S(1)} all-to-all(bf16[32,16,128]{2,1,0:T(8,128)(2,1)} %bitcast.33), channel_id=1, replica_groups=mesh['x'=4,'zh'=2,'zl'=4,'y'=4,'c'=2] {'x','y','c'}, dimensions={0} | all-to-all | bytes 262144 | tf_op jit(solution)/shard_map/all_to_all | solution.py:36
  93.6 3.3 %all-to-all-start.4 = ((bf16[8,16,128]{2,1,0:T(8,128)(2,1)}), bf16[8,16,128]{2,1,0:T(8,128)(2,1)S(1)}, u32[]{:S(2)}, u32[]{:S(2)}) async-start(bf16[8,16,128]{2,1,0:T(8,128)(2,1)} %broadcast_in_dim.14), calls=%async_computation.4 | async-start | bytes 65536 | tf_op jit(solution)/shard_map/all_to_all | solution.py:36
  96.9 1.0 collective-permute-start.8
  97.9 1.1 collective-permute-start.9
  99.0 4.7 %all-to-all-done.4 = bf16[8,16,128]{2,1,0:T(8,128)(2,1)S(1)} async-done(((bf16[8,16,128]{2,1,0:T(8,128)(2,1)}), bf16[8,16,128]{2,1,0:T(8,128)(2,1)S(1)}, u32[]{:S(2)}, u32[]{:S(2)}) %all-to-all-start.4) | async-done | bytes 32800 | tf_op jit(solution)/shard_map/all_to_all | solution.py:36
  103.7 0.7 broadcast_in_dim.15
  104.4 5.2 %all-to-all-start.5 = ((bf16[32,16,128]{2,1,0:T(8,128)(2,1)}), bf16[32,16,128]{2,1,0:T(8,128)(2,1)S(1)}, u32[]{:S(2)}, u32[]{:S(2)}) async-start(bf16[32,16,128]{2,1,0:T(8,128)(2,1)} %broadcast_in_dim.15), calls=%async_computation.5 | async-start | bytes 262144 | tf_op jit(solution)/shard_map/all_to_all | solution.py:36
  111.8 1.3 %copy-done.2 = bf16[128,5120]{1,0:T(8,128)(2,1)S(1)} copy-done((bf16[128,5120]{1,0:T(8,128)(2,1)S(1)}, bf16[128,5120]{1,0:T(8,128)(2,1)}, u32[]{:S(2)}) %copy-start.2) | copy-done | bytes 1310744
  113.1 0.8 copy-done.8
  114.0 5.8 %output_rows.1 = bf16[320,5120]{1,0:T(8,128)(2,1)} custom-call(s32[6]{0:T(128)S(1)} %copy-done.10, bf16[576,128]{1,0:T(8,128)(2,1)S(1)} %copy-done.5, bf16[2,64,256]{2,1,0:T(8,128)(2,1)S(1)} %copy-done.8, bf16[2,64,256]{2,1,0:T(8,128)(2,1)S(1)} %collective-permute-done.8.refs_1_, bf16[2,64,256]{2,1,0:T(8,128)(2,1)S(1)} %collective-permute-done.9.refs_2_, ...), custom_call_target="tpu_custom_call" | custom-call | tf_op jit(solution)/shard_map/output_rows/pallas_call | solution.py:209
  (70 shorter events, 6.1 us)
Async XLA Ops:
  1.3 31.0 %copy-start.7 = (bf16[2,4,40,128]{3,2,1,0:T(8,128)(2,1)S(1)}, bf16[2,4,40,128]{3,2,1,0:T(8,128)(2,1)}, u32[]{:S(2)}) copy-start(bf16[2,4,40,128]{3,2,1,0:T(8,128)(2,1)} %param.10) | copy-start | bytes 245764
  24.1 15.5 %all-to-all-start.1 = ((bf16[8,40,128]{2,1,0:T(8,128)(2,1)}), bf16[8,40,128]{2,1,0:T(8,128)(2,1)S(1)}, u32[]{:S(2)}, u32[]{:S(2)}) async-start(bf16[8,40,128]{2,1,0:T(8,128)(2,1)} %broadcast_in_dim.12), calls=%async_computation.1 | async-start | bytes 163840 | tf_op jit(solution)/shard_map/all_to_all | solution.py:36
  32.3 18.3 %collective-permute-start = (bf16[2,4,40,128]{3,2,1,0:T(8,128)(2,1)S(1)}, bf16[2,4,40,128]{3,2,1,0:T(8,128)(2,1)S(1)}, u32[]{:S(2)}, u32[]{:S(2)}) collective-permute-start(bf16[2,4,40,128]{3,2,1,0:T(8,128)(2,1)S(1)} %copy-done.7), channel_id=1, source_target_pairs={{0,1},{1,2},{2,3},{3,4},{4,5},{5,6},{6,7},{7,8},{8,9},{9,10},{10,1... | collective-permute-start | bytes 245768 | tf_op jit(solution)/shard_map/ppermute | solution.py:515
  40.4 29.6 %all-to-all-start.2 = ((bf16[32,40,128]{2,1,0:T(8,128)(2,1)}), bf16[32,40,128]{2,1,0:T(8,128)(2,1)S(1)}, u32[]{:S(2)}, u32[]{:S(2)}) async-start(bf16[32,40,128]{2,1,0:T(8,128)(2,1)} %broadcast_in_dim.13), calls=%async_computation.2 | async-start | bytes 655360 | tf_op jit(solution)/shard_map/all_to_all | solution.py:36
  45.7 4.9 %copy-start.3 = (bf16[3,3,3,128,128]{4,3,2,1,0:T(8,128)(2,1)S(1)}, bf16[3,3,3,128,128]{4,3,2,1,0:T(8,128)(2,1)}, u32[]{:S(2)}) copy-start(bf16[3,3,3,128,128]{4,3,2,1,0:T(8,128)(2,1)} %param.11) | copy-start | bytes 2654212
  45.7 4.9 %copy-start.9 = (s32[6]{0:T(128)S(1)}, s32[6]{0:T(128)}, u32[]{:S(2)}) copy-start(s32[6]{0:T(128)} %stack.23.at_ref) | copy-start | bytes 76
  53.0 13.2 %copy-start.4 = (bf16[576,128]{1,0:T(8,128)(2,1)}, bf16[576,128]{1,0:T(8,128)(2,1)S(1)}, u32[]{:S(2)}) copy-start(bf16[576,128]{1,0:T(8,128)(2,1)S(1)} %get-tuple-element.20.refs_0_.f_ref) | copy-start | bytes 442372
  53.0 6.3 %collective-permute-start.1 = (bf16[576,128]{1,0:T(8,128)(2,1)S(1)}, bf16[576,128]{1,0:T(8,128)(2,1)S(1)}, u32[]{:S(2)}, u32[]{:S(2)}) collective-permute-start(bf16[576,128]{1,0:T(8,128)(2,1)S(1)} %get-tuple-element.21), channel_id=1, source_target_pairs={{0,2},{2,4},{4,6},{6,0},{1,3},{3,5},{5,7},{7,1},{8,10},{10,12},{12... | collective-permute-start | bytes 442376 | tf_op jit(solution)/shard_map/ppermute | solution.py:492
  54.4 9.1 %collective-permute-start.2 = (bf16[576,128]{1,0:T(8,128)(2,1)S(1)}, bf16[576,128]{1,0:T(8,128)(2,1)S(1)}, u32[]{:S(2)}, u32[]{:S(2)}) collective-permute-start(bf16[576,128]{1,0:T(8,128)(2,1)S(1)} %get-tuple-element.22), channel_id=1, source_target_pairs={{0,4},{2,6},{4,0},{6,2},{1,5},{3,7},{5,1},{7,3},{8,12},{10,14},{12... | collective-permute-start | bytes 442376 | tf_op jit(solution)/shard_map/ppermute | solution.py:492
  56.9 8.0 %collective-permute-start.3 = (bf16[576,128]{1,0:T(8,128)(2,1)S(1)}, bf16[576,128]{1,0:T(8,128)(2,1)S(1)}, u32[]{:S(2)}, u32[]{:S(2)}) collective-permute-start(bf16[576,128]{1,0:T(8,128)(2,1)S(1)} %get-tuple-element.23), channel_id=1, source_target_pairs={{0,6},{2,0},{4,2},{6,4},{1,7},{3,1},{5,3},{7,5},{8,14},{10,8},{12,... | collective-permute-start | bytes 442376 | tf_op jit(solution)/shard_map/ppermute | solution.py:492
  58.0 7.1 %collective-permute-start.4 = (bf16[576,128]{1,0:T(8,128)(2,1)S(1)}, bf16[576,128]{1,0:T(8,128)(2,1)S(1)}, u32[]{:S(2)}, u32[]{:S(2)}) collective-permute-start(bf16[576,128]{1,0:T(8,128)(2,1)S(1)} %get-tuple-element.20.refs_0_.f_ref), channel_id=1, source_target_pairs={{0,1},{1,0},{2,3},{3,2},{4,5},{5,4},{6,7},{7,6},{8,9},{9,8},{10,11... | collective-permute-start | bytes 442376 | tf_op jit(solution)/shard_map/ppermute | solution.py:492
  59.3 6.9 %copy-start.12 = (bf16[576,128]{1,0:T(8,128)(2,1)}, bf16[576,128]{1,0:T(8,128)(2,1)S(1)}, u32[]{:S(2)}) copy-start(bf16[576,128]{1,0:T(8,128)(2,1)S(1)} %collective-permute-done.1.refs_1_) | copy-start | bytes 442372
  59.3 5.8 %collective-permute-start.5 = (bf16[576,128]{1,0:T(8,128)(2,1)S(1)}, bf16[576,128]{1,0:T(8,128)(2,1)S(1)}, u32[]{:S(2)}, u32[]{:S(2)}) collective-permute-start(bf16[576,128]{1,0:T(8,128)(2,1)S(1)} %collective-permute-done.1.refs_1_), channel_id=1, source_target_pairs={{0,1},{1,0},{2,3},{3,2},{4,5},{5,4},{6,7},{7,6},{8,9},{9,8},{10,11... | collective-permute-start | bytes 442376 | tf_op jit(solution)/shard_map/ppermute | solution.py:492
  63.6 2.6 %copy-start.13 = (bf16[576,128]{1,0:T(8,128)(2,1)}, bf16[576,128]{1,0:T(8,128)(2,1)S(1)}, u32[]{:S(2)}) copy-start(bf16[576,128]{1,0:T(8,128)(2,1)S(1)} %collective-permute-done.2.refs_2_) | copy-start | bytes 442372
  63.6 2.3 %collective-permute-start.6 = (bf16[576,128]{1,0:T(8,128)(2,1)S(1)}, bf16[576,128]{1,0:T(8,128)(2,1)S(1)}, u32[]{:S(2)}, u32[]{:S(2)}) collective-permute-start(bf16[576,128]{1,0:T(8,128)(2,1)S(1)} %collective-permute-done.2.refs_2_), channel_id=1, source_target_pairs={{0,1},{1,0},{2,3},{3,2},{4,5},{5,4},{6,7},{7,6},{8,9},{9,8},{10,11... | collective-permute-start | bytes 442376 | tf_op jit(solution)/shard_map/ppermute | solution.py:492
  64.8 1.4 %copy-start.14 = (bf16[576,128]{1,0:T(8,128)(2,1)}, bf16[576,128]{1,0:T(8,128)(2,1)S(1)}, u32[]{:S(2)}) copy-start(bf16[576,128]{1,0:T(8,128)(2,1)S(1)} %collective-permute-done.3.refs_3_) | copy-start | bytes 442372
  64.8 1.4 %collective-permute-start.7 = (bf16[576,128]{1,0:T(8,128)(2,1)S(1)}, bf16[576,128]{1,0:T(8,128)(2,1)S(1)}, u32[]{:S(2)}, u32[]{:S(2)}) collective-permute-start(bf16[576,128]{1,0:T(8,128)(2,1)S(1)} %collective-permute-done.3.refs_3_), channel_id=1, source_target_pairs={{0,1},{1,0},{2,3},{3,2},{4,5},{5,4},{6,7},{7,6},{8,9},{9,8},{10,11... | collective-permute-start | bytes 442376 | tf_op jit(solution)/shard_map/ppermute | solution.py:492
  70.8 41.0 %copy-start = (bf16[128,5120]{1,0:T(8,128)(2,1)S(1)}, bf16[128,5120]{1,0:T(8,128)(2,1)}, u32[]{:S(2)}) copy-start(bf16[128,5120]{1,0:T(8,128)(2,1)} %refs_8_.1) | copy-start | bytes 3932164
  70.8 41.0 %copy-start.1 = (bf16[128,5120]{1,0:T(8,128)(2,1)S(1)}, bf16[128,5120]{1,0:T(8,128)(2,1)}, u32[]{:S(2)}) copy-start(bf16[128,5120]{1,0:T(8,128)(2,1)} %refs_9_.1) | copy-start | bytes 3932164
  70.8 41.0 %copy-start.5 = (bf16[576,128]{1,0:T(8,128)(2,1)S(1)}, bf16[576,128]{1,0:T(8,128)(2,1)}, u32[]{:S(2)}) copy-start(bf16[576,128]{1,0:T(8,128)(2,1)} %copy-done.4) | copy-start | bytes 442372
  70.8 41.0 %copy-start.10 = (s32[6]{0:T(128)S(1)}, s32[6]{0:T(128)}, u32[]{:S(2)}) copy-start(s32[6]{0:T(128)} %stack.23.at_ref) | copy-start | bytes 76
  93.6 10.1 %all-to-all-start.4 = ((bf16[8,16,128]{2,1,0:T(8,128)(2,1)}), bf16[8,16,128]{2,1,0:T(8,128)(2,1)S(1)}, u32[]{:S(2)}, u32[]{:S(2)}) async-start(bf16[8,16,128]{2,1,0:T(8,128)(2,1)} %broadcast_in_dim.14), calls=%async_computation.4 | async-start | bytes 65536 | tf_op jit(solution)/shard_map/all_to_all | solution.py:36
  96.9 13.1 %collective-permute-start.8 = (bf16[2,64,256]{2,1,0:T(8,128)(2,1)}, bf16[2,64,256]{2,1,0:T(8,128)(2,1)S(1)}, u32[]{:S(2)}, u32[]{:S(2)}) collective-permute-start(bf16[2,64,256]{2,1,0:T(8,128)(2,1)} %get-tuple-element.30), channel_id=1, source_target_pairs={{0,6},{2,0},{4,2},{6,4},{1,7},{3,1},{5,3},{7,5},{8,14},{10,8},{12,... | collective-permute-start | bytes 196616 | tf_op jit(solution)/shard_map/ppermute | solution.py:492
  97.9 12.3 %collective-permute-start.9 = (bf16[2,64,256]{2,1,0:T(8,128)(2,1)}, bf16[2,64,256]{2,1,0:T(8,128)(2,1)S(1)}, u32[]{:S(2)}, u32[]{:S(2)}) collective-permute-start(bf16[2,64,256]{2,1,0:T(8,128)(2,1)} %get-tuple-element.31), channel_id=1, source_target_pairs={{0,4},{2,6},{4,0},{6,2},{1,5},{3,7},{5,1},{7,3},{8,12},{10,14},{12... | collective-permute-start | bytes 196616 | tf_op jit(solution)/shard_map/ppermute | solution.py:492
  99.0 11.5 %collective-permute-start.10 = (bf16[2,64,256]{2,1,0:T(8,128)(2,1)}, bf16[2,64,256]{2,1,0:T(8,128)(2,1)S(1)}, u32[]{:S(2)}, u32[]{:S(2)}) collective-permute-start(bf16[2,64,256]{2,1,0:T(8,128)(2,1)} %get-tuple-element.32), channel_id=1, source_target_pairs={{0,2},{2,4},{4,6},{6,0},{1,3},{3,5},{5,7},{7,1},{8,10},{10,12},{12... | collective-permute-start | bytes 196616 | tf_op jit(solution)/shard_map/ppermute | solution.py:492
  104.4 15.4 %copy-start.19 = (bf16[20,128]{1,0:T(8,128)(2,1)S(1)}, bf16[20,128]{1,0:T(8,128)(2,1)}, u32[]{:S(2)}) copy-start(bf16[20,128]{1,0:T(8,128)(2,1)} %get-tuple-element.33) | copy-start | bytes 15364
  104.4 15.8 %copy-start.20 = (f32[20,384]{1,0:T(8,128)S(1)}, f32[20,384]{1,0:T(8,128)}, u32[]{:S(2)}) copy-start(f32[20,384]{1,0:T(8,128)} %get-tuple-element.35) | copy-start | bytes 92164
  104.4 15.4 %all-to-all-start.5 = ((bf16[32,16,128]{2,1,0:T(8,128)(2,1)}), bf16[32,16,128]{2,1,0:T(8,128)(2,1)S(1)}, u32[]{:S(2)}, u32[]{:S(2)}) async-start(bf16[32,16,128]{2,1,0:T(8,128)(2,1)} %broadcast_in_dim.15), calls=%async_computation.5 | async-start | bytes 262144 | tf_op jit(solution)/shard_map/all_to_all | solution.py:36
  109.6 1.6 %collective-permute-start.11 = (bf16[2,64,256]{2,1,0:T(8,128)(2,1)}, bf16[2,64,256]{2,1,0:T(8,128)(2,1)S(1)}, u32[]{:S(2)}, u32[]{:S(2)}) collective-permute-start(bf16[2,64,256]{2,1,0:T(8,128)(2,1)} %get-tuple-element.29.refs_0_), channel_id=1, source_target_pairs={{0,1},{1,0},{2,3},{3,2},{4,5},{5,4},{6,7},{7,6},{8,9},{9,8},{10,11... | collective-permute-start | bytes 196616 | tf_op jit(solution)/shard_map/ppermute | solution.py:492
  110.0 1.3 %collective-permute-start.12 = (bf16[2,64,256]{2,1,0:T(8,128)(2,1)S(1)}, bf16[2,64,256]{2,1,0:T(8,128)(2,1)S(1)}, u32[]{:S(2)}, u32[]{:S(2)}) collective-permute-start(bf16[2,64,256]{2,1,0:T(8,128)(2,1)S(1)} %collective-permute-done.8.refs_1_), channel_id=1, source_target_pairs={{0,1},{1,0},{2,3},{3,2},{4,5},{5,4},{6,7},{7,6},{8,9},{9,8},{10,11... | collective-permute-start | bytes 196616 | tf_op jit(solution)/shard_map/ppermute | solution.py:492
  110.2 1.3 %collective-permute-start.13 = (bf16[2,64,256]{2,1,0:T(8,128)(2,1)S(1)}, bf16[2,64,256]{2,1,0:T(8,128)(2,1)S(1)}, u32[]{:S(2)}, u32[]{:S(2)}) collective-permute-start(bf16[2,64,256]{2,1,0:T(8,128)(2,1)S(1)} %collective-permute-done.9.refs_2_), channel_id=1, source_target_pairs={{0,1},{1,0},{2,3},{3,2},{4,5},{5,4},{6,7},{7,6},{8,9},{9,8},{10,11... | collective-permute-start | bytes 196616 | tf_op jit(solution)/shard_map/ppermute | solution.py:492
  110.5 1.3 %collective-permute-start.14 = (bf16[2,64,256]{2,1,0:T(8,128)(2,1)S(1)}, bf16[2,64,256]{2,1,0:T(8,128)(2,1)S(1)}, u32[]{:S(2)}, u32[]{:S(2)}) collective-permute-start(bf16[2,64,256]{2,1,0:T(8,128)(2,1)S(1)} %collective-permute-done.10.refs_3_), channel_id=1, source_target_pairs={{0,1},{1,0},{2,3},{3,2},{4,5},{5,4},{6,7},{7,6},{8,9},{9,8},{10,11... | collective-permute-start | bytes 196616 | tf_op jit(solution)/shard_map/ppermute | solution.py:492
  (8 other events, 7.4 us)
